TPU v7x, 256 devices: a whole 4x4x8 slice. The times are simulated.
256 devices in a mesh: cache: 32 (over x, z), owner: 8 (over y, core).
Axes of the slice: x: 4, y: 4, z: 8, core: 2. Of those that a mesh axis runs over, the one named last changes fastest.
Arguments:
- cache: bfloat16 [32, 4, 128, 256], P('cache'), may hold values from -2.5 to 2.5
- backing: bfloat16 [32, 64, 128, 256], P('cache', 'owner'), may hold values from -2.5 to 2.5
- resident: int32 [32, 4], P('cache'), may hold values from 0 to 63, as said below
- promote: int32 [32, 2], P('cache'), may hold values from 0 to 63, as said below
- victim: int32 [32, 2], P('cache'), may hold values from 0 to 3, as said below
- lookups: int32 [2, 32768, 32, 8], P(None, 'owner', 'cache'), may hold values from 0 to 511
- route: int32 [2, 8, 4096], P(None, 'owner'), may hold values from 0 to 4095, each once within a row
- dcn_down: bfloat16 [8192, 128], P('cache'), may hold values from -0.0625 to 0.0625
- dcn_up: bfloat16 [128, 8192], P(None, 'cache'), may hold values from -0.5 to 0.5
- dcn_bias: float32 [8192], replicated, may hold values from -5 to 5
- mlp_in: bfloat16 [8192, 1024], P('cache'), may hold values from -0.0625 to 0.0625
- mlp_bias: float32 [1024], replicated, may hold values from -3 to 3
- mlp_out: float32 [1024], replicated, may hold values from -0.1875 to 0.1875
- out_bias: float32 [1], replicated, may hold values from -4 to 4
Outputs:
- scores: float32 [2, 8, 4096], P(None, 'owner', 'cache')
- new_cache: bfloat16 [32, 4, 128, 256], P('cache')
- new_backing: bfloat16 [32, 64, 128, 256], P('cache', 'owner')
Inputs may be any that keep to these rules, and one draw needn't show every extreme that they name: `resident`: for each feature, 4 distinct backing blocks. `promote`: for each feature, 2 distinct backing blocks, none of them in that feature's resident; block k belongs to owner k // 8. `victim`: for each feature, 2 distinct slots. `route`: each batch and owner group holds every request index once.
All inputs are finite; a program needn't handle non-finite values.
Results may differ from a plain program's by a relative error of at most 0.004.
Values may be sent and summed in bfloat16 or wider, within the bound.
No kernel may reach another device: no remote copies, remote signals or barrier semaphores. Data moves between devices by JAX's collectives and lax.ppermute only.
A program may use at most 128 MiB of HBM per device.

v0:
```python
import jax
import jax.numpy as jnp
from jax import lax
from jax.sharding import PartitionSpec as P


def copy_for_each(x, axis):
    size = lax.axis_size(axis)
    return lax.all_to_all(jnp.broadcast_to(x[None], (size, *x.shape)), axis, 0, 0, tiled=True)


def in_order(blocks, dim):
    lengths = list(blocks.shape[1:])
    lengths[dim] *= blocks.shape[0]
    return jnp.moveaxis(blocks, 0, dim).reshape(lengths)


def gathered_copies(x, axis, dim):
    blocks = copy_for_each(x, axis)
    return in_order(blocks, dim)


def take_rows(table, wanted):
    return jax.vmap(lambda rows, chosen: rows[chosen])(table, wanted)


def pool_batch(requests, order, table):
    requests = requests[order]
    count = requests.shape[0]
    step = min(512, count)
    codes = jnp.arange(table.shape[1], dtype=jnp.int32)

    def one_block(lookup_block):
        counts = jnp.sum((lookup_block[..., None] == codes).astype(jnp.bfloat16), axis=2)
        return jnp.einsum("rfk,fke->rfe", counts, table, preferred_element_type=jnp.float32).astype(
            jnp.bfloat16
        )

    blocks = requests.reshape((count // step, step) + requests.shape[1:])
    pooled = lax.map(one_block, blocks)
    return pooled.reshape((count,) + pooled.shape[2:])


def on_device(
    cache,
    backing,
    resident,
    promote,
    victim,
    lookups,
    route,
    dcn_down,
    dcn_up,
    dcn_bias,
    mlp_in,
    mlp_bias,
    mlp_out,
    out_bias,
):
    held = cache.shape[0]
    slots = cache.shape[1]
    block = cache.shape[2]
    width = cache.shape[3]
    own_blocks = backing.shape[1]
    promoted_count = promote.shape[1]
    owner_here = lax.axis_index("owner")
    local_index = promote - owner_here * own_blocks
    owned_here = (local_index >= 0) & (local_index < own_blocks)
    clamped = jnp.clip(local_index, 0, own_blocks - 1)
    fetched = take_rows(backing, clamped)
    outgoing = jnp.where(owned_here[:, :, None, None], fetched, jnp.zeros_like(fetched))
    arrived = gathered_copies(outgoing, "owner", 0)
    owners = arrived.shape[0] // held
    arrived = arrived.reshape(owners, held, promoted_count, block, width)
    source = promote // own_blocks
    picked = source[None] == jnp.arange(owners, dtype=jnp.int32)[:, None, None]
    promoted = jnp.sum(jnp.where(picked[..., None, None], arrived, jnp.zeros_like(arrived)), axis=0)
    evicted = take_rows(cache, victim)
    leaving = take_rows(resident, victim) - owner_here * own_blocks
    slot_numbers = jnp.arange(slots, dtype=jnp.int32)
    block_numbers = jnp.arange(own_blocks, dtype=jnp.int32)
    new_cache = cache
    new_backing = backing
    for column in range(promoted_count):
        slot_hit = victim[:, column][:, None] == slot_numbers[None, :]
        new_cache = jnp.where(slot_hit[:, :, None, None], promoted[:, column][:, None], new_cache)
        block_hit = leaving[:, column][:, None] == block_numbers[None, :]
        new_backing = jnp.where(
            block_hit[:, :, None, None], evicted[:, column][:, None], new_backing
        )
    table = new_cache.reshape(held, slots * block, width)
    batches = lookups.shape[0]
    received = []
    for batch_turn in range(batches):
        pooled = pool_batch(lookups[batch_turn], route[batch_turn, 0], table)
        received.append(lax.all_to_all(pooled, "cache", split_axis=0, concat_axis=1, tiled=True))
    arrived_rows = jnp.stack(received)
    per_batch = arrived_rows.shape[1]
    features = arrived_rows.reshape(batches * per_batch, -1)
    columns = features
    low = jnp.dot(
        columns,
        lax.all_gather(dcn_down, "cache", axis=0, tiled=True),
        preferred_element_type=jnp.float32,
    ).astype(jnp.bfloat16)
    gate = (
        jnp.dot(
            low,
            lax.all_gather(dcn_up, "cache", axis=1, tiled=True),
            preferred_element_type=jnp.float32,
        )
        + dcn_bias
    )
    crossed = (features * gate + features).astype(jnp.bfloat16)
    columns = crossed
    before = jnp.dot(
        columns,
        lax.all_gather(mlp_in, "cache", axis=0, tiled=True),
        preferred_element_type=jnp.float32,
    )
    hidden = jnp.maximum(before + mlp_bias, 0.0)
    scores = jnp.sum(hidden * mlp_out, axis=-1) + out_bias[0]
    return (scores.reshape(batches, 1, per_batch), new_cache, new_backing)


def solution(mesh):
    in_specs = (
        P("cache", None, None, None),
        P("cache", "owner", None, None),
        P("cache", None),
        P("cache", None),
        P("cache", None),
        P(None, "owner", "cache", None),
        P(None, "owner", None),
        P("cache", None),
        P(None, "cache"),
        P(),
        P("cache", None),
        P(),
        P(),
        P(),
    )
    out_specs = (
        P(None, "owner", "cache"),
        P("cache", None, None, None),
        P("cache", "owner", None, None),
    )
    return jax.shard_map(
        on_device, mesh=mesh, in_specs=in_specs, out_specs=out_specs, check_vma=False
    )
```

profile of v0, /device:TPU:1, one launch (start us, length us, event | category | flops | bytes accessed | tf_op | source)
XLA Modules:
  0.0 363.3 jit_solution(7484960167387886002)
XLA Ops:
  13.9 6.7 %all-to-all-start = ((bf16[8,1,2,128,256]{4,3,2,1,0:T(8,128)(2,1)}), bf16[8,1,2,128,256]{4,3,2,1,0:T(8,128)(2,1)S(1)}, u32[]{:S(2)}, u32[]{:S(2)}) async-start(bf16[8,1,2,128,256]{4,3,2,1,0:T(8,128)(2,1)} %broadcast_in_dim.137), calls=%async_computation | async-start | bytes 2097152 | tf_op jit(solution)/shard_map/all_to_all | solution.py:9
  21.2 14.1 %gather_fusion = s32[4096,8]{1,0:T(8,128)} fusion(s32[4096,8]{1,0:T(8,128)S(1)} %bitcast.111, s32[4096]{0:T(1024)S(1)} %broadcast_clamp_fusion.1), kind=kCustom, calls=%fused_computation | custom fusion | bytes 278528 | tf_op jit(solution)/shard_map/gather | solution.py:28
  38.8 14.1 %gather_fusion.1 = s32[4096,8]{1,0:T(8,128)} fusion(s32[4096,8]{1,0:T(8,128)S(1)} %bitcast.110, s32[4096]{0:T(1024)S(1)} %broadcast_clamp_fusion), kind=kCustom, calls=%fused_computation.1 | custom fusion | bytes 278528 | tf_op jit(solution)/shard_map/gather | solution.py:28
  57.6 35.3 %while.26 = (s32[]{:T(128)}, bf16[8,512,1,256]{3,1,2,0:T(8,128)(2,1)S(1)}, s32[8,512,1,8]{1,3,2,0:T(8,128)}, bf16[1,512,256]{2,1,0:T(8,128)(2,1)S(1)}, s32[]{:T(128)}) while((s32[]{:T(128)}, bf16[8,512,1,256]{3,1,2,0:T(8,128)(2,1)S(1)}, s32[8,512,1,8]{1,3,2,0:T(8,128)}, bf16[1,512,256]{2,1,0:T(8,128)(2,1)S(1)}, s32[]{:T(128)}) %tuple.90), condition=%wide.region_3.4_spmd.clone, body=%wide.region_1.3_spmd.clone.sunk | while | flops 140378112 | bytes 1654853 | solution.py:40
  58.4 3.2 fusion.41
  62.8 3.2 fusion.41
  67.2 3.2 fusion.41
  76.1 3.2 fusion.41
  80.5 3.2 fusion.41
  84.9 3.2 fusion.41
  89.3 3.2 fusion.41
  96.3 4.0 %reshape.321 = bf16[32,2,16384]{2,1,0:T(2,128)(2,1)} reshape(bf16[4096,256]{1,0:T(8,128)(2,1)} %reduce.17) | data formatting | bytes 4194304
  100.3 10.3 %all-to-all-start.1 = ((bf16[32,2,16384]{2,1,0:T(2,128)(2,1)}), bf16[32,2,16384]{2,1,0:T(2,128)(2,1)S(1)}, u32[]{:S(2)}, u32[]{:S(2)}) async-start(bf16[32,2,16384]{2,1,0:T(2,128)(2,1)} %reshape.321), calls=%async_computation.1 | async-start | bytes 4194304 | tf_op jit(solution)/shard_map/all_to_all | solution.py:96
  112.1 35.1 %while.27 = (s32[]{:T(128)}, bf16[8,512,1,256]{3,1,2,0:T(8,128)(2,1)}, s32[8,512,1,8]{1,3,2,0:T(8,128)S(1)}, bf16[1,512,256]{2,1,0:T(8,128)(2,1)S(1)}, s32[]{:T(128)}) while((s32[]{:T(128)}, bf16[8,512,1,256]{3,1,2,0:T(8,128)(2,1)}, s32[8,512,1,8]{1,3,2,0:T(8,128)S(1)}, bf16[1,512,256]{2,1,0:T(8,128)(2,1)S(1)}, s32[]{:T(128)}) %tuple.91), condition=%wide.region_6.7_spmd.clone, body=%wide.region_4.6_spmd.clone.sunk | while | flops 140378112 | bytes 1655361 | solution.py:40
  112.2 3.2 fusion.45
  116.6 3.2 fusion.45
  121.0 3.2 fusion.45
  125.4 3.2 fusion.45
  129.8 3.2 fusion.45
  134.2 3.2 fusion.45
  138.6 3.2 fusion.45
  147.2 4.5 %reduce.16 = bf16[4096,256]{1,0:T(8,128)(2,1)} reduce(bf16[4096,1,256]{2,0,1:T(8,128)(2,1)} %bitcast.116, bf16[]{:T(256)} %broadcast.259), dimensions={1}, to_apply=%copy.68.reduce_sub_computation | reduce | bytes 4194306 | tf_op jit(solution)/shard_map/reshape | solution.py:41
  151.7 4.0 %reshape.319 = bf16[32,2,16384]{2,1,0:T(2,128)(2,1)} reshape(bf16[4096,256]{1,0:T(8,128)(2,1)} %reduce.16) | data formatting | bytes 4194304
  155.7 6.3 %all-to-all-done.1 = bf16[32,2,16384]{2,1,0:T(2,128)(2,1)S(1)} async-done(((bf16[32,2,16384]{2,1,0:T(2,128)(2,1)}), bf16[32,2,16384]{2,1,0:T(2,128)(2,1)S(1)}, u32[]{:S(2)}, u32[]{:S(2)}) %all-to-all-start.1) | async-done | bytes 2097184 | tf_op jit(solution)/shard_map/all_to_all | solution.py:96
  162.0 10.4 %all-to-all-start.2 = ((bf16[32,2,16384]{2,1,0:T(2,128)(2,1)}), bf16[32,2,16384]{2,1,0:T(2,128)(2,1)}, u32[]{:S(2)}, u32[]{:S(2)}) async-start(bf16[32,2,16384]{2,1,0:T(2,128)(2,1)} %reshape.319), calls=%async_computation.2 | async-start | bytes 4194304 | tf_op jit(solution)/shard_map/all_to_all | solution.py:96
  177.5 6.7 %reshape.322 = bf16[4096,1,256]{2,1,0:T(2,128)(2,1)} reshape(bf16[32,2,16384]{2,1,0:T(2,128)(2,1)S(1)} %all-to-all-done.1) | data formatting | bytes 4194304
  186.8 41.1 %all-to-all-done.2 = bf16[32,2,16384]{2,1,0:T(2,128)(2,1)} async-done(((bf16[32,2,16384]{2,1,0:T(2,128)(2,1)}), bf16[32,2,16384]{2,1,0:T(2,128)(2,1)}, u32[]{:S(2)}, u32[]{:S(2)}) %all-to-all-start.2) | async-done | bytes 2097184 | tf_op jit(solution)/shard_map/all_to_all | solution.py:96
  227.9 10.4 %reshape.320 = bf16[4096,1,256]{2,1,0:T(2,128)(2,1)} reshape(bf16[32,2,16384]{2,1,0:T(2,128)(2,1)} %all-to-all-done.2) | data formatting | bytes 4194304
  243.7 6.2 %copy.77 = bf16[32,8,32,256]{3,1,2,0:T(8,128)(2,1)} copy(bf16[32,8,32,256]{3,2,1,0:T(8,128)(2,1)S(1)} %bitcast.114) | data formatting | bytes 8388608
  249.9 4.1 %convolution_convert_fusion.2 = bf16[256,128]{1,0:T(8,128)(2,1)S(1)} fusion(bf16[256,8192]{1,0:T(8,128)(2,1)} %bitcast.112, bf16[8192,128]{1,0:T(8,128)(2,1)} %all-gather.4.cloned.1.call-done), kind=kOutput, calls=%fused_computation.31 | convolution fusion | flops 536903680 | bytes 6356992 | tf_op jit(solution)/shard_map/dot_general | solution.py:101
  254.1 89.4 %all-gather.8.cloned.1.call-done = bf16[8192,1024]{1,0:T(8,128)(2,1)} async-done(((bf16[256,1024]{1,0:T(8,128)(2,1)}), bf16[8192,1024]{1,0:T(8,128)(2,1)}) %all-gather.8.cloned.1.call-update) | async-done | bytes 16777232 | tf_op jit(solution)/shard_map/all_gather | solution.py:118
  343.5 12.7 %fusion.17 = f32[256]{0:T(256)S(1)} fusion(bf16[8192,1024]{1,0:T(8,128)(2,1)} %all-gather.8.cloned.1.call-done, bf16[256,128]{1,0:T(8,128)(2,1)S(1)} %convolution_convert_fusion.2, bf16[128,8192]{1,0:T(8,128)(2,1)} %all-gather.6.cloned.1.call-done, bf16[256,8192]{1,0:T(8,128)(2,1)} %bitcast.113, f32[8192]{0:T(1024)S(1)} %copy-done.8, ...), kind=kOutput, calls=%fused_computation.30 | convolution fusion | flops 4843372544 | bytes 23176192 | tf_op jit(solution)/shard_map/dot_general | solution.py:116
  (123 shorter events, 58.0 us)
Async XLA Ops:
  7.2 166.8 %copy-start = (s32[1,4]{1,0:T(1,128)S(1)}, s32[1,4]{1,0:T(1,128)}, u32[]{:S(2)}) copy-start(s32[1,4]{1,0:T(1,128)} %param.20) | copy-start | bytes 52
  7.2 242.7 %all-gather.4.cloned.1.call-start = ((), (), s32[]{:S(2)}) async-start(), calls=%async_computation.3 | async-start | bytes 2162688 | tf_op jit(solution)/shard_map/all_gather | solution.py:103
  7.9 246.2 %all-gather.6.cloned.1.call-start = ((), (), s32[]{:S(2)}) async-start(), calls=%async_computation.4 | async-start | bytes 2162688 | tf_op jit(solution)/shard_map/all_gather | solution.py:109
  8.7 11.9 %copy-start.5 = (s32[2,4096,1,8]{1,3,2,0:T(8,128)S(1)}, s32[2,4096,1,8]{1,3,2,0:T(8,128)}, u32[]{:S(2)}) copy-start(s32[2,4096,1,8]{1,3,2,0:T(8,128)} %param.23) | copy-start | bytes 786436
  8.7 334.8 %all-gather.8.cloned.1.call-start = ((), (), s32[]{:S(2)}) async-start(), calls=%async_computation.5 | async-start | bytes 17301504 | tf_op jit(solution)/shard_map/all_gather | solution.py:118
  12.0 8.5 %copy-start.6 = (s32[2,1,4096]{2,1,0:T(1,128)S(1)}, s32[2,1,4096]{2,1,0:T(1,128)}, u32[]{:S(2)}) copy-start(s32[2,1,4096]{2,1,0:T(1,128)} %param.24) | copy-start | bytes 98308
  13.9 43.2 %all-to-all-start = ((bf16[8,1,2,128,256]{4,3,2,1,0:T(8,128)(2,1)}), bf16[8,1,2,128,256]{4,3,2,1,0:T(8,128)(2,1)S(1)}, u32[]{:S(2)}, u32[]{:S(2)}) async-start(bf16[8,1,2,128,256]{4,3,2,1,0:T(8,128)(2,1)} %broadcast_in_dim.137), calls=%async_computation | async-start | bytes 2097152 | tf_op jit(solution)/shard_map/all_to_all | solution.py:9
  52.9 2.2 copy-start.7
  52.9 4.4 %copy-start.3 = (bf16[1,4,128,256]{3,2,1,0:T(8,128)(2,1)S(1)}, bf16[1,4,128,256]{3,2,1,0:T(8,128)(2,1)}, u32[]{:S(2)}) copy-start(bf16[1,4,128,256]{3,2,1,0:T(8,128)(2,1)} %param.18) | copy-start | bytes 786436
  100.3 61.7 %all-to-all-start.1 = ((bf16[32,2,16384]{2,1,0:T(2,128)(2,1)}), bf16[32,2,16384]{2,1,0:T(2,128)(2,1)S(1)}, u32[]{:S(2)}, u32[]{:S(2)}) async-start(bf16[32,2,16384]{2,1,0:T(2,128)(2,1)} %reshape.321), calls=%async_computation.1 | async-start | bytes 4194304 | tf_op jit(solution)/shard_map/all_to_all | solution.py:96
  147.2 4.5 %copy-start.4 = (bf16[1,512,256]{2,1,0:T(8,128)(2,1)}, bf16[1,512,256]{2,1,0:T(8,128)(2,1)S(1)}, u32[]{:S(2)}) copy-start(bf16[1,512,256]{2,1,0:T(8,128)(2,1)S(1)} %get-tuple-element.330) | copy-start | bytes 786436
  155.7 20.8 %copy-start.2 = (bf16[1,8,128,256]{3,2,1,0:T(8,128)(2,1)S(1)}, bf16[1,8,128,256]{3,2,1,0:T(8,128)(2,1)}, u32[]{:S(2)}) copy-start(bf16[1,8,128,256]{3,2,1,0:T(8,128)(2,1)} %param.19) | copy-start | bytes 1572868
  162.0 65.9 %all-to-all-start.2 = ((bf16[32,2,16384]{2,1,0:T(2,128)(2,1)}), bf16[32,2,16384]{2,1,0:T(2,128)(2,1)}, u32[]{:S(2)}, u32[]{:S(2)}) async-start(bf16[32,2,16384]{2,1,0:T(2,128)(2,1)} %reshape.319), calls=%async_computation.2 | async-start | bytes 4194304 | tf_op jit(solution)/shard_map/all_to_all | solution.py:96
  249.9 93.6 %copy-start.8 = (f32[8192]{0:T(1024)S(1)}, f32[8192]{0:T(1024)}, u32[]{:S(2)}) copy-start(f32[8192]{0:T(1024)} %param.27) | copy-start | bytes 98308
  249.9 93.6 %copy-start.9 = (f32[1024]{0:T(1024)S(1)}, f32[1024]{0:T(1024)}, u32[]{:S(2)}) copy-start(f32[1024]{0:T(1024)} %param.30) | copy-start | bytes 12292
  249.9 93.6 %copy-start.10 = (f32[1024]{0:T(1024)S(1)}, f32[1024]{0:T(1024)}, u32[]{:S(2)}) copy-start(f32[1024]{0:T(1024)} %param.29) | copy-start | bytes 12292
  343.5 13.2 %copy-start.1 = (s32[1,4]{1,0:T(1,128)S(1)}, s32[1,4]{1,0:T(1,128)}, u32[]{:S(2)}) copy-start(s32[1,4]{1,0:T(1,128)} %param.20) | copy-start | bytes 52
Sparse Core Ops, SparseCore 0:
  10.6 77.0 all-gather.3
  90.1 95.1 all-gather.5
  187.9 155.6 all-gather.7
where the time goes:
time: 365 us; the launch traced here: 363 us
  waiting for transfers between devices  139 us (38%)
  local copies, waits for them, and re-layouts  88.8 us (24%)
  other arithmetic  65.7 us (18%)
  starting transfers between devices  27.5 us (8%)
  matrix products  27.3 us (7%)
  between operations  14.7 us (4%)
    all_gather x1, waiting for transfers between devices, on_device(): lax.all_gather(mlp_in, 'cache', axis=0, tiled=True)  89.4 us
    reduce_sum x16, other arithmetic, one_block(): jnp.sum((lookup_block[..., None] == codes).astype(jnp.bfloat16), axis=2)  51.7 us
    all_to_all x2, waiting for transfers between devices, on_device(): lax.all_to_all(pooled, 'cache', split_axis=0, concat_axis=1, tiled=True)  47.4 us
    unnamed x35, local copies, waits for them, and re-layouts  42.9 us
    gather x2, local copies, waits for them, and re-layouts, pool_batch(): requests = requests[order]  28.2 us
    all_to_all x2, starting transfers between devices, on_device(): lax.all_to_all(pooled, 'cache', split_axis=0, concat_axis=1, tiled=True)  20.7 us
    dot_general x1, matrix products, on_device(): jnp.dot(columns, lax.all_gather(mlp_in, 'cache', axis=0, tiled=True), pre...  12.7 us
    dot_general x16, matrix products, one_block(): jnp.einsum('rfk,fke->rfe', counts, table, preferred_element_type=jnp.floa...  10.5 us
  transfers between devices with their start and end apart: 6, of which 3 were waited for; matrix products, arithmetic and copies ran while one was open for 46% of the time, Pallas kernels for 0%

commit v1 on v0

v1 whole, which is shorter than its diff:
```python
import jax
import jax.numpy as jnp
from jax import lax
from jax.experimental import pallas as pl
from jax.experimental.pallas import tpu as pltpu
from jax.sharding import Mesh, PartitionSpec as P

BF = jnp.bfloat16
F32 = jnp.float32
NX, NZ, NY, NC = 4, 8, 4, 2
SLOTS, BLOCK, E = 4, 128, 256
HID, RANK = 1024, 128
LANE = 128


SMEM = pl.BlockSpec(memory_space=pltpu.SMEM)
VMEM = pl.BlockSpec(memory_space=pltpu.VMEM)
ANY = pl.BlockSpec(memory_space=pl.ANY)


def near(*vs):
    return [pltpu.with_memory_space_constraint(v, pltpu.VMEM) for v in vs]


def kernel(body, out_shape, in_specs, out_specs, scratch=(), flops=0, limit=16):
    return pl.pallas_call(
        body,
        out_shape=out_shape,
        in_specs=in_specs,
        out_specs=out_specs,
        scratch_shapes=list(scratch),
        compiler_params=pltpu.CompilerParams(vmem_limit_bytes=limit * 1024 * 1024),
        cost_estimate=pl.CostEstimate(flops=flops, bytes_accessed=0, transcendentals=0),
    )


def bf(*shape):
    return jax.ShapeDtypeStruct(shape, BF)


def fetch_body(promote, victim, backing, out, blocks, sems):
    count = backing.shape[0]
    base = (lax.axis_index("y") * NC + lax.axis_index("c")) * count
    copies = []
    for k in range(2):
        at = jnp.clip(promote[0, k] - base, 0, count - 1)
        copies.append(pltpu.make_async_copy(backing.at[at], blocks.at[k], sems.at[k]))
    for copy in copies:
        copy.start()
    out[...] = jnp.zeros(out.shape, BF)
    for copy in copies:
        copy.wait()
    for k in range(2):
        local = promote[0, k] - base

        @pl.when((local >= 0) & (local < count))
        def _():
            s = victim[0, k]
            out[2 * s] = blocks[k, :, :LANE]
            out[2 * s + 1] = blocks[k, :, LANE:]


def fetch(promote, victim, backing):
    return kernel(
        fetch_body, bf(NY * NC, BLOCK, LANE), [SMEM, SMEM, ANY], VMEM,
        [pltpu.VMEM((2, BLOCK, E), BF), pltpu.SemaphoreType.DMA((2,))],
    )(promote, victim, pltpu.with_memory_space_constraint(backing, pltpu.HBM))


def piece_body(victim, arrived, cache, factors, sent, out):
    s = lax.axis_index("y")
    c = lax.axis_index("c")
    total = arrived[0]
    for i in range(1, NY * NC):
        total = total + arrived[i]
    block = cache[s]
    kept = jnp.where(c == 0, block[:, :LANE], block[:, LANE:])
    evicted = (victim[0, 0] == s) | (victim[0, 1] == s)
    piece = jnp.where(evicted, total, kept).T
    for i in range(NZ):
        out[i, :LANE, :] = piece
        out[i, LANE:192, :] = factors[...]
        out[i, 192:, :] = sent[i]


def make_piece(victim, arrived, cache, factors, sent):
    return kernel(
        piece_body, bf(NZ, 256, BLOCK), [SMEM] + [VMEM] * 4, VMEM
    )(victim, *near(arrived, cache, factors, sent))


def back_body(resident, victim, cache, backing, out):
    base = (lax.axis_index("y") * NC + lax.axis_index("c")) * backing.shape[0]
    out[...] = backing[...]
    for k in range(2):
        v = victim[0, k]
        local = resident[0, v] - base

        @pl.when((local >= 0) & (local < backing.shape[0]))
        def _():
            out[local] = cache[v]


def write_back(resident, victim, cache, backing):
    return kernel(
        back_body, jax.ShapeDtypeStruct(backing.shape, BF), [SMEM, SMEM, VMEM, VMEM], VMEM
    )(resident, victim, cache, backing)


def route_body(lookups, route, out):
    batches, bag, count = lookups.shape
    tiles = count // LANE

    def one(t, _):
        q = t // NZ
        z = t % NZ
        parts = []
        for b in range(batches):
            row = jnp.broadcast_to(route[b, pl.ds(t, 1), :], (bag, LANE))
            lane = row & (LANE - 1)
            tile = row >> 7
            got = jnp.zeros((bag, LANE), jnp.int32)
            for v in range(tiles):
                cand = jnp.take_along_axis(
                    lookups[b, :, v * LANE : (v + 1) * LANE], lane, axis=1, mode="promise_in_bounds"
                )
                got = jnp.where(tile == v, cand, got)
            parts.append(got)
        both = (jnp.concatenate(parts, axis=0) - 256).astype(F32).astype(BF)
        out[z, pl.ds(pl.multiple_of(q * 16, 16), 16), :] = both
        return 0

    lax.fori_loop(0, NX * NZ, one, 0)


def route_lookups(lookups, route):
    return kernel(route_body, bf(NZ, 64, LANE), [VMEM, VMEM], VMEM, flops=1 << 22)(lookups, route)


def weights_body(down, up, mlp, factors, top, scratch):
    o = lax.axis_index("y") * NC + lax.axis_index("c")
    rows = RANK // (NY * NC)
    at = pl.multiple_of(o * rows, rows)
    scratch[...] = down[...].T
    piece = jnp.concatenate([scratch[pl.ds(at, rows), :], up[pl.ds(at, rows), :]], axis=0)
    factors[0:32, :] = piece[:, :LANE]
    factors[32:64, :] = piece[:, LANE:]
    top[...] = mlp[:, pl.ds(pl.multiple_of(o * LANE, LANE), LANE)].T


def own_weights(down, up, mlp):
    return kernel(
        weights_body, [bf(64, LANE), bf(LANE, E)], [VMEM] * 3, [VMEM] * 2, [pltpu.VMEM((RANK, E), BF)]
    )(down, up, mlp)


def factor(tables, i, start):
    rows = [
        jnp.concatenate([t[i, start : start + 16, :], t[i, start + 32 : start + 48, :]], axis=1)
        for t in tables
    ]
    return jnp.concatenate(rows, axis=0)


def far(*vs):
    return [pltpu.with_memory_space_constraint(v, pltpu.HBM) for v in vs]


def load(sources, holds, sems):
    waits = []
    for i in range(NZ):
        step = []
        for n, (source, hold) in enumerate(zip(sources, holds)):
            copy = pltpu.make_async_copy(source.at[i], hold.at[i], sems.at[n, i])
            copy.start()
            step.append(copy)
        waits.append(step)
    return waits


def pool_step(batch, i, table, down, lookups, codes, hold):
    for q in range(NX):
        wanted = lookups[i, q * 16 + batch * 8 : q * 16 + batch * 8 + 8, :]
        rows = [jnp.broadcast_to(wanted[l : l + 1, :], (BLOCK, LANE)) for l in range(8)]
        for r in range(NY):
            total = jnp.where(rows[0] == codes[r], jnp.ones((), BF), jnp.zeros((), BF))
            for l in range(1, 8):
                total = total + jnp.where(rows[l] == codes[r], jnp.ones((), BF), jnp.zeros((), BF))
            hold[r * BLOCK : (r + 1) * BLOCK, q * LANE : (q + 1) * LANE] = total
    pooled = jnp.dot(table, hold[...], preferred_element_type=F32).astype(BF)
    return pooled, jnp.dot(down, pooled, preferred_element_type=F32)


def slot_codes():
    y = lax.axis_index("y")
    line = lax.broadcasted_iota(jnp.int32, (BLOCK, LANE), 0)
    return [(line + (((y + r) % NY) * BLOCK - 256)).astype(F32).astype(BF) for r in range(NY)]


def pool0_body(lookups, *refs):
    tables = refs[0:8]
    x0_out, low_out, table_out, factor_out, new_cache = refs[8:13]
    counts, x0, whole_table, factors, sems = refs[13:]
    y = lax.axis_index("y")
    c = lax.axis_index("c")
    codes = slot_codes()
    low = None
    copies = []
    for i in range(NZ):
        mine = jnp.concatenate([t[i, :LANE, :] for t in tables[:4]], axis=1)
        theirs = jnp.concatenate([t[i, :LANE, :] for t in tables[4:]], axis=1)
        table = jnp.concatenate([jnp.where(c == 0, mine, theirs), jnp.where(c == 0, theirs, mine)], axis=0)
        whole_table[i] = table
        down = factor(tables, i, LANE)
        factors[i, :RANK, :] = down
        factors[i, RANK:, :] = factor(tables, i, LANE + 16)

        @pl.when(lax.axis_index("z") == i)
        def _():
            for r in range(NY):
                new_cache[(y + r) % NY] = table[:, r * BLOCK : (r + 1) * BLOCK].T

        pooled, part = pool_step(0, i, table, down, lookups, codes, counts.at[i % 2])
        x0[i] = pooled
        low = part if low is None else low + part
        for n, (source, out) in enumerate(((x0, x0_out), (whole_table, table_out), (factors, factor_out))):
            copy = pltpu.make_async_copy(source.at[i], out.at[i], sems.at[n, i])
            copy.start()
            copies.append(copy)
    low_out[...] = low
    for copy in copies:
        copy.wait()


MANY = NX * LANE


def pool0(lookups, tables):
    return kernel(
        pool0_body,
        [pltpu.HBM((NZ, E, MANY), BF), jax.ShapeDtypeStruct((RANK, MANY), F32), pltpu.HBM((NZ, E, SLOTS * BLOCK), BF),
         pltpu.HBM((NZ, 2 * RANK, E), BF), bf(SLOTS, BLOCK, E)],
        [VMEM] * 9, [ANY, VMEM, ANY, ANY, VMEM],
        [pltpu.VMEM((2, SLOTS * BLOCK, MANY), BF), pltpu.VMEM((NZ, E, MANY), BF), pltpu.VMEM((NZ, E, SLOTS * BLOCK), BF),
         pltpu.VMEM((NZ, 2 * RANK, E), BF), pltpu.SemaphoreType.DMA((3, NZ))],
        flops=1 << 32, limit=24,
    )(*near(lookups, *tables))


def pool1_body(lookups, table_in, factor_in, x0_out, low_out, counts, x0, tables, factors, sems, out_sems):
    codes = slot_codes()
    low = None
    copies = []
    waits = load((table_in, factor_in), (tables, factors), sems)
    for i in range(NZ):
        for copy in waits[i]:
            copy.wait()
        pooled, part = pool_step(1, i, tables[i], factors[i, :RANK, :], lookups, codes, counts.at[i % 2])
        x0[i] = pooled
        low = part if low is None else low + part
        copy = pltpu.make_async_copy(x0.at[i], x0_out.at[i], out_sems.at[i])
        copy.start()
        copies.append(copy)
    low_out[...] = low
    for copy in copies:
        copy.wait()


def pool1(lookups, table, factors):
    return kernel(
        pool1_body, [pltpu.HBM((NZ, E, MANY), BF), jax.ShapeDtypeStruct((RANK, MANY), F32)],
        [VMEM, ANY, ANY], [ANY, VMEM],
        [pltpu.VMEM((2, SLOTS * BLOCK, MANY), BF), pltpu.VMEM((NZ, E, MANY), BF), pltpu.VMEM((NZ, E, SLOTS * BLOCK), BF),
         pltpu.VMEM((NZ, 2 * RANK, E), BF), pltpu.SemaphoreType.DMA((2, NZ)), pltpu.SemaphoreType.DMA((NZ,))],
        flops=1 << 32, limit=24,
    )(*near(lookups), *far(table, factors))


def gate_body(l0, l1, l2, l3, bias, x0_in, factor_in, x1_out, x0, factors, sems, out_sems):
    x = lax.axis_index("x")
    waits = load((x0_in, factor_in), (x0, factors), sems)
    low = (l0[...] + l1[...] + l2[...] + l3[...]).astype(BF)
    columns = bias[pl.ds(pl.multiple_of(x * NZ, NZ), NZ), :].T
    copies = []
    for i in range(NZ):
        for copy in waits[i]:
            copy.wait()
        gate = lax.dot_general(factors[i, RANK:, :], low, (((0,), (0,)), ((), ())), preferred_element_type=F32)
        gate = gate + columns[:, i : i + 1]
        features = x0[i].astype(F32)
        x0[i] = (features * gate + features).astype(BF)
        copy = pltpu.make_async_copy(x0.at[i], x1_out.at[i], out_sems.at[i])
        copy.start()
        copies.append(copy)
    for copy in copies:
        copy.wait()


def gate(lows, bias, x0, factors):
    return kernel(
        gate_body, pltpu.HBM((NZ, E, MANY), BF), [VMEM] * 5 + [ANY] * 2, ANY,
        [pltpu.VMEM((NZ, E, MANY), BF), pltpu.VMEM((NZ, 2 * RANK, E), BF),
         pltpu.SemaphoreType.DMA((2, NZ)), pltpu.SemaphoreType.DMA((NZ,))],
        flops=1 << 31,
    )(*near(*lows, bias), *far(x0, factors))


def top_body(x1_0, x1_1, t0, t1, t2, t3, *refs):
    outs = refs[0:4]
    weights, crossed, hold, sems = refs[4:]
    x = lax.axis_index("x")
    copies = []
    for b, source in enumerate((x1_0, x1_1)):
        step = []
        for i in range(NZ):
            copy = pltpu.make_async_copy(source.at[i], crossed.at[b, pl.ds(i * E, E), :], sems.at[b, i])
            copy.start()
            step.append(copy)
        copies.append(step)
    for i in range(NZ):
        for j, t in enumerate((t0, t1, t2, t3)):
            weights[j * LANE : (j + 1) * LANE, i * E : (i + 1) * E] = t[i]
    for b in range(2):
        for copy in copies[b]:
            copy.wait()
        part = jnp.dot(weights[...], crossed[b], preferred_element_type=F32).astype(BF)
        for q in range(NX):
            hold[q, :, b * LANE : (b + 1) * LANE] = part[:, q * LANE : (q + 1) * LANE]
    for r in range(NX):
        outs[r][...] = hold[(x + r) % NX]


def top_half(x1, tops):
    return kernel(
        top_body, [bf(HID // 2, 2 * LANE)] * NX, [ANY] * 2 + [VMEM] * 4, [VMEM] * NX,
        [pltpu.VMEM((HID // 2, NZ * E), BF), pltpu.VMEM((2, NZ * E, MANY), BF),
         pltpu.VMEM((NX, HID // 2, 2 * LANE), BF), pltpu.SemaphoreType.DMA((2, NZ))],
        flops=1 << 32, limit=24,
    )(*far(*x1), *near(*tops))


def score_body(mlp_bias, mlp_out, out_bias, *refs):
    hs = refs[0:8]
    out, rows = refs[8:]
    y = lax.axis_index("y")
    c = lax.axis_index("c")
    for j in range(8):
        o = ((y + j % 4) % NY) * NC + (c + j // 4) % NC
        rows[j : j + 1, :] = mlp_bias[pl.ds(o, 1), :]
        rows[8 + j : 9 + j, :] = mlp_out[pl.ds(o, 1), :]
    columns = rows[...].T
    total = jnp.zeros((LANE, 2 * LANE), F32)
    for j in range(8):
        before = columns[:, j : j + 1]
        for h in hs[4 * (j // 4) : 4 * (j // 4) + 4]:
            before = before + h[(j % 4) * LANE : (j % 4 + 1) * LANE, :].astype(F32)
        total = total + jnp.maximum(before, 0.0) * columns[:, 8 + j : 9 + j]
    total = jnp.sum(total, axis=0, keepdims=True) + out_bias[0]
    for b in range(2):
        out[b : b + 1, :] = total[:, b * LANE : (b + 1) * LANE]


def score(mlp_bias, mlp_out, out_bias, ha, hb):
    return kernel(
        score_body, jax.ShapeDtypeStruct((2, LANE), F32), [VMEM, VMEM, SMEM] + [VMEM] * 8, VMEM,
        [pltpu.VMEM((16, LANE), F32)],
    )(mlp_bias, mlp_out, out_bias, *near(*ha, *hb))


def shift(v, axis, size, k):
    return lax.ppermute(v, axis, [(i, (i + k) % size) for i in range(size)])


def spread(v, axis, size):
    out = [v]
    for k in range(1, size):
        out.append(shift(v, axis, size, size - k))
    return out


def deal(parts):
    out = [parts[0]]
    for k in range(1, NX):
        out.append(shift(parts[k], "x", NX, k))
    return out


def exchange(v, axis):
    return lax.all_to_all(v, axis, 0, 0, tiled=True)


def swaps(vs):
    return [shift(v, "c", NC, 1) for v in vs]


def tie(v, *others):
    return lax.optimization_barrier((v, *others))[0]


def on_device(
    cache, backing, resident, promote, victim, lookups, route,
    dcn_down, dcn_up, dcn_bias, mlp_in, mlp_bias, mlp_out, out_bias,
):
    cache = cache[0]
    backing = backing[0]
    bias = dcn_bias.reshape(-1, E)
    outgoing = fetch(promote, victim, backing)
    arrived = exchange(outgoing, ("y", "c"))
    wanted = jnp.transpose(lookups[:, :, 0, :], (0, 2, 1))
    factors, top = own_weights(dcn_down, dcn_up, mlp_in)
    sent = route_lookups(wanted, route[:, 0].reshape(2, -1, LANE))
    piece = make_piece(victim, arrived, cache, factors, sent)
    mixed = exchange(piece, "z")
    own = spread(mixed[:, :192, :], "y", NY)
    mixed = mixed[:, 192:, :]
    tops = jnp.broadcast_to(tie(top, mixed)[None], (NZ, *top.shape))
    tops = exchange(tops, "z")
    tables = own + swaps(own)
    own = spread(tops, "y", NY)
    other = swaps(own)
    x00, low0, table, factors, new_cache = pool0(mixed, tables)
    lows0 = spread(low0, "x", NX)
    x01, low1 = pool1(tie(mixed, low0), table, factors)
    lows1 = spread(low1, "x", NX)
    x10 = gate(lows0, bias, tie(x00, low1), factors)
    x11 = gate(lows1, bias, x01, factors)
    ha = top_half((x10, x11), own)
    ra = deal(ha)
    hb = top_half((x10, tie(x11, ha[0])), other)
    rb = deal(hb)
    new_backing = write_back(resident, victim, cache, backing)
    scores = score(mlp_bias.reshape(8, LANE), mlp_out.reshape(8, LANE), out_bias, ra, rb)
    return scores[:, None, :], new_cache[None], new_backing[None]


def solution(mesh):
    fine = Mesh(mesh.devices.reshape(NX, NZ, NY, NC), ("x", "z", "y", "c"))
    ca, ow = ("x", "z"), ("y", "c")
    in_specs = (
        P(ca, None, None, None),
        P(ca, ow, None, None),
        P(ca, None),
        P(ca, None),
        P(ca, None),
        P(None, ow, ca, None),
        P(None, ow, None),
        P(ca, None),
        P(None, ca),
        P(),
        P(ca, None),
        P(),
        P(),
        P(),
    )
    out_specs = (
        P(None, ow, ca),
        P(ca, None, None, None),
        P(ca, ow, None, None),
    )
    return jax.shard_map(
        on_device, mesh=fine, in_specs=in_specs, out_specs=out_specs, check_vma=False
    )
```

time: 365 us -> 169 us (0.46)
  waiting for transfers between devices: 139 us -> 41.9 us
  local copies, waits for them, and re-layouts: 88.8 us -> 9.8 us
  other arithmetic: 65.7 us -> 0 us
  Pallas kernels: 0 us -> 46.8 us
  matrix products: 27.3 us -> 0 us
  blocking collectives: 0 us -> 25.4 us
  starting transfers between devices: 27.5 us -> 42.8 us
  between operations: 14.7 us -> 1.59 us
    all_gather x3 -> x0, waiting for transfers between devices: 89.4 us -> none  [the longest x1 89.4 us: on_device(): lax.all_gather(mlp_in, 'cache', axis=0, tiled=True)]
    reduce_sum x17 -> x0, other arithmetic: 51.9 us -> none  [the longest x16 51.7 us: one_block(): jnp.sum((lookup_block[..., None] == codes).astype(jnp.bfloat16), axis=2)]
    all_to_all x3 -> x2, waiting for transfers between devices: 47.4 us -> 0.01 us  [exchange(): return lax.all_to_all(v, axis, 0, 0, tiled=True)]
    pallas_call x0 -> x12, Pallas kernels: none -> 46.8 us  [the longest x2 10 us: gate(): kernel(gate_body, pltpu.HBM((NZ, E, MANY), BF), [VMEM] * 5 + [ANY] * 2, A...]
    ppermute x0 -> x26, waiting for transfers between devices: none -> 41.9 us  [shift(): return lax.ppermute(v, axis, [(i, (i + k) % size) for i in range(size)])]
    unnamed x35 -> x40, local copies, waits for them, and re-layouts: 42.9 us -> 8.92 us
    ppermute x0 -> x26, starting transfers between devices: none -> 32.7 us  [shift(): return lax.ppermute(v, axis, [(i, (i + k) % size) for i in range(size)])]
    gather x7 -> x0, local copies, waits for them, and re-layouts: 31.2 us -> none  [the longest x2 28.2 us: pool_batch(): requests = requests[order]]
  transfers between devices with their start and end apart: 6 -> 28, of which waited for: 3 -> 7; matrix products, arithmetic and copies ran while one was open for 46% -> 1% of each run, Pallas kernels for 0% -> 25%
where the time goes in v1:
time: 169 us; the launch traced here: 168 us
  Pallas kernels  46.8 us (28%)
  starting transfers between devices  42.8 us (25%)
  waiting for transfers between devices  41.9 us (25%)
  blocking collectives  25.4 us (15%)
  local copies, waits for them, and re-layouts  9.8 us (6%)
    ppermute x26, waiting for transfers between devices, shift(): return lax.ppermute(v, axis, [(i, (i + k) % size) for i in range(size)])  41.9 us
    ppermute x26, starting transfers between devices, shift(): return lax.ppermute(v, axis, [(i, (i + k) % size) for i in range(size)])  32.7 us
    all_to_all x1, blocking collectives, exchange(): return lax.all_to_all(v, axis, 0, 0, tiled=True)  25.4 us
    pallas_call x2, Pallas kernels, gate(): kernel(gate_body, pltpu.HBM((NZ, E, MANY), BF), [VMEM] * 5 + [ANY] * 2, A...  10 us
    all_to_all x2, starting transfers between devices, exchange(): return lax.all_to_all(v, axis, 0, 0, tiled=True)  10 us
    pallas_call x1, Pallas kernels, pool0(): kernel(pool0_body, [pltpu.HBM((NZ, E, MANY), BF), jax.ShapeDtypeStruct((R...  9.81 us
    unnamed x40, local copies, waits for them, and re-layouts  8.92 us
    pallas_call x2, Pallas kernels, top_half(): kernel(top_body, [bf(HID // 2, 2 * LANE)] * NX, [ANY] * 2 + [VMEM] * 4, [...  8.44 us
  transfers between devices with their start and end apart: 28, of which 7 were waited for; matrix products, arithmetic and copies ran while one was open for 1% of the time, Pallas kernels for 25%

profile of v1, /device:TPU:1, one launch (start us, length us, event | category | flops | bytes accessed | tf_op | source)
XLA Modules:
  0.0 168.3 jit_solution(10478601208055783431)
XLA Ops:
  2.0 2.2 %shard_map.157 = bf16[8,128,128]{2,1,0:T(8,128)(2,1)} custom-call(s32[1,2]{1,0:T(1,128)S(1)} %copy-done.11, s32[1,2]{1,0:T(1,128)S(1)} %copy-done.7, bf16[8,128,256]{2,1,0:T(8,128)(2,1)} %bitcast.13), custom_call_target="tpu_custom_call" | custom-call | tf_op jit(solution)/shard_map/pallas_call | solution.py:64
  4.2 6.5 %all-to-all-start = ((bf16[8,128,128]{2,1,0:T(8,128)(2,1)}), bf16[8,128,128]{2,1,0:T(8,128)(2,1)S(1)}, u32[]{:S(2)}, u32[]{:S(2)}) async-start(bf16[8,128,128]{2,1,0:T(8,128)(2,1)} %shard_map.157), calls=%async_computation | async-start | bytes 524288 | tf_op jit(solution)/shard_map/all_to_all | solution.py:389
  10.7 1.0 copy-done.2
  14.3 4.7 %shard_map.159.sent = bf16[8,64,128]{2,1,0:T(8,128)(2,1)S(1)} custom-call(s32[2,8,4096]{2,1,0:T(8,128)S(1)} %bitcast.17, s32[2,32,128]{2,1,0:T(8,128)S(1)} %bitcast.18), custom_call_target="tpu_custom_call" | custom-call | flops 4194304 | tf_op jit(solution)/shard_map/pallas_call | solution.py:137
  19.7 25.4 %all_to_all.15 = bf16[8,256,128]{2,1,0:T(8,128)(2,1)S(1)} all-to-all(bf16[8,256,128]{2,1,0:T(8,128)(2,1)S(1)} %shard_map.160), channel_id=1, replica_groups=mesh['x'=4,'z'=8,'y'=4,'c'=2] {'z'}, dimensions={0} | all-to-all | bytes 1048576 | tf_op jit(solution)/shard_map/all_to_all | solution.py:389
  45.1 1.3 collective-permute-start
  47.6 2.6 %collective-permute-start.3 = (bf16[8,192,128]{2,1,0:T(8,128)(2,1)S(1)}, bf16[8,192,128]{2,1,0:T(8,128)(2,1)S(1)}, u32[]{:S(2)}, u32[]{:S(2)}) collective-permute-start(bf16[8,192,128]{2,1,0:T(8,128)(2,1)S(1)} %slice.9.refs_0_), channel_id=1, source_target_pairs={{0,1},{1,0},{2,3},{3,2},{4,5},{5,4},{6,7},{7,6},{8,9},{9,8},{10,11... | collective-permute-start | bytes 1179656 | tf_op jit(solution)/shard_map/ppermute | solution.py:371
  50.2 5.2 %collective-permute-done.refs_1_ = bf16[8,192,128]{2,1,0:T(8,128)(2,1)S(1)} collective-permute-done((bf16[8,192,128]{2,1,0:T(8,128)(2,1)S(1)}, bf16[8,192,128]{2,1,0:T(8,128)(2,1)S(1)}, u32[]{:S(2)}, u32[]{:S(2)}) %collective-permute-start) | collective-permute-done | bytes 393248 | tf_op jit(solution)/shard_map/ppermute | solution.py:371
  55.4 2.2 %collective-permute-start.4 = (bf16[8,192,128]{2,1,0:T(8,128)(2,1)S(1)}, bf16[8,192,128]{2,1,0:T(8,128)(2,1)S(1)}, u32[]{:S(2)}, u32[]{:S(2)}) collective-permute-start(bf16[8,192,128]{2,1,0:T(8,128)(2,1)S(1)} %collective-permute-done.refs_1_), channel_id=1, source_target_pairs={{0,1},{1,0},{2,3},{3,2},{4,5},{5,4},{6,7},{7,6},{8,9},{9,8},{10,11... | collective-permute-start | bytes 1179656 | tf_op jit(solution)/shard_map/ppermute | solution.py:371
  57.7 4.3 %collective-permute-start.5 = (bf16[8,192,128]{2,1,0:T(8,128)(2,1)S(1)}, bf16[8,192,128]{2,1,0:T(8,128)(2,1)}, u32[]{:S(2)}, u32[]{:S(2)}) collective-permute-start(bf16[8,192,128]{2,1,0:T(8,128)(2,1)S(1)} %collective-permute-done.1.refs_2_), channel_id=1, source_target_pairs={{0,1},{1,0},{2,3},{3,2},{4,5},{5,4},{6,7},{7,6},{8,9},{9,8},{10,11... | collective-permute-start | bytes 1179656 | tf_op jit(solution)/shard_map/ppermute | solution.py:371
  62.0 5.4 %collective-permute-done.2.refs_3_ = bf16[8,192,128]{2,1,0:T(8,128)(2,1)S(1)} collective-permute-done((bf16[8,192,128]{2,1,0:T(8,128)(2,1)S(1)}, bf16[8,192,128]{2,1,0:T(8,128)(2,1)S(1)}, u32[]{:S(2)}, u32[]{:S(2)}) %collective-permute-start.2) | collective-permute-done | bytes 393248 | tf_op jit(solution)/shard_map/ppermute | solution.py:371
  68.7 3.5 %all-to-all-start.2 = ((bf16[8,128,256]{2,1,0:T(8,128)(2,1)}), bf16[8,128,256]{2,1,0:T(8,128)(2,1)S(1)}, u32[]{:S(2)}, u32[]{:S(2)}) async-start(bf16[8,128,256]{2,1,0:T(8,128)(2,1)} %broadcast_in_dim.15), calls=%async_computation.2 | async-start | bytes 1048576 | tf_op jit(solution)/shard_map/all_to_all | solution.py:389
  72.3 9.8 %shard_map.161 = (bf16[8,256,512]{2,1,0:T(8,128)(2,1)}, f32[128,512]{1,0:T(8,128)S(1)}, bf16[8,256,512]{2,1,0:T(8,128)(2,1)}, bf16[8,256,256]{2,1,0:T(8,128)(2,1)}, bf16[4,128,256]{2,1,0:T(8,128)(2,1)}) custom-call(bf16[8,64,128]{2,1,0:T(8,128)(2,1)S(1)} %slice.8.lookups, bf16[8,192,128]{2,1,0:T(8,128)(2,1)S(1)} %slice.9.refs_0_, ...), custom_call_target="tpu_custom_call" | custom-call | flops 4294967296 | tf_op jit(solution)/shard_map/pallas_call | solution.py:239
  82.9 8.3 %shard_map.162 = (bf16[8,256,512]{2,1,0:T(8,128)(2,1)}, f32[128,512]{1,0:T(8,128)S(1)}) custom-call(bf16[8,64,128]{2,1,0:T(8,128)(2,1)S(1)} %slice.8.lookups, bf16[8,256,512]{2,1,0:T(8,128)(2,1)} %get-tuple-element.28.table_in, bf16[8,256,256]{2,1,0:T(8,128)(2,1)} %get-tuple-element.29.factor_in), custom_call_target="tpu_custom_call" | custom-call | flops 4294967296 | tf_op jit(solution)/shard_map/pallas_call | solution.py:270
  91.2 2.6 %collective-permute-start.10 = (f32[128,512]{1,0:T(8,128)S(1)}, f32[128,512]{1,0:T(8,128)S(1)}, u32[]{:S(2)}, u32[]{:S(2)}) collective-permute-start(f32[128,512]{1,0:T(8,128)S(1)} %get-tuple-element.30.l0), channel_id=1, source_target_pairs={{0,192},{64,0},{128,64},{192,128},{1,193},{65,1},{129,65},{193,129... | collective-permute-start | bytes 786440 | tf_op jit(solution)/shard_map/ppermute | solution.py:371
  95.8 9.1 %collective-permute-done.10.l1 = f32[128,512]{1,0:T(8,128)S(1)} collective-permute-done((f32[128,512]{1,0:T(8,128)S(1)}, f32[128,512]{1,0:T(8,128)S(1)}, u32[]{:S(2)}, u32[]{:S(2)}) %collective-permute-start.10) | collective-permute-done | bytes 262176 | tf_op jit(solution)/shard_map/ppermute | solution.py:371
  106.3 3.6 %collective-permute-start.7 = (f32[128,512]{1,0:T(8,128)S(1)}, f32[128,512]{1,0:T(8,128)S(1)}, u32[]{:S(2)}, u32[]{:S(2)}) collective-permute-start(f32[128,512]{1,0:T(8,128)S(1)} %copy-done.14), channel_id=1, source_target_pairs={{0,192},{64,0},{128,64},{192,128},{1,193},{65,1},{129,65},{193,129... | collective-permute-start | bytes 786440 | tf_op jit(solution)/shard_map/ppermute | solution.py:371
  109.9 10.3 %collective-permute-done.7.l1 = f32[128,512]{1,0:T(8,128)S(1)} collective-permute-done((f32[128,512]{1,0:T(8,128)S(1)}, f32[128,512]{1,0:T(8,128)S(1)}, u32[]{:S(2)}, u32[]{:S(2)}) %collective-permute-start.7) | collective-permute-done | bytes 262176 | tf_op jit(solution)/shard_map/ppermute | solution.py:371
  121.1 0.9 copy-done.18
  122.1 5.0 %shard_map.164.x1_1 = bf16[8,256,512]{2,1,0:T(8,128)(2,1)} custom-call(f32[128,512]{1,0:T(8,128)S(1)} %get-tuple-element.30.l0, f32[128,512]{1,0:T(8,128)S(1)} %copy-done.16, f32[128,512]{1,0:T(8,128)S(1)} %copy-done.18, f32[128,512]{1,0:T(8,128)} %collective-permute-done.12.l3, f32[32,256]{1,0:T(8,128)S(1)} %reshape.18.bias, ...), custom_call_target="tpu_custom_call" | custom-call | flops 2147483648 | tf_op jit(solution)/shard_map/pallas_call | solution.py:300
  127.1 2.0 %collective-permute-start.19 = (bf16[8,128,256]{2,1,0:T(8,128)(2,1)S(1)}, bf16[8,128,256]{2,1,0:T(8,128)(2,1)S(1)}, u32[]{:S(2)}, u32[]{:S(2)}) collective-permute-start(bf16[8,128,256]{2,1,0:T(8,128)(2,1)S(1)} %all-to-all-done.2.t0), channel_id=1, source_target_pairs={{0,1},{1,0},{2,3},{3,2},{4,5},{5,4},{6,7},{7,6},{8,9},{9,8},{10,11... | collective-permute-start | bytes 1572872 | tf_op jit(solution)/shard_map/ppermute | solution.py:371
  129.6 5.1 %shard_map.163.x1_0 = bf16[8,256,512]{2,1,0:T(8,128)(2,1)} custom-call(f32[128,512]{1,0:T(8,128)S(1)} %copy-done.14, f32[128,512]{1,0:T(8,128)S(1)} %collective-permute-done.7.l1, f32[128,512]{1,0:T(8,128)} %collective-permute-done.8.l2, f32[128,512]{1,0:T(8,128)} %collective-permute-done.9.l3, f32[32,256]{1,0:T(8,128)S(1)} %reshape.18.bias, ...), custom_call_target="tpu_custom_call" | custom-call | flops 2147483648 | tf_op jit(solution)/shard_map/pallas_call | solution.py:300
  134.7 4.2 %shard_map.165 = (bf16[512,256]{1,0:T(8,128)(2,1)S(1)}, bf16[512,256]{1,0:T(8,128)(2,1)S(1)}, bf16[512,256]{1,0:T(8,128)(2,1)S(1)}, bf16[512,256]{1,0:T(8,128)(2,1)S(1)}) custom-call(bf16[8,256,512]{2,1,0:T(8,128)(2,1)} %shard_map.163.x1_0, bf16[8,256,512]{2,1,0:T(8,128)(2,1)} %shard_map.164.x1_1, bf16[8,128,256]{2,1,0:T(8,128)(2,1)S(1)} %all-to-all-done.2.t0, ...), custom_call_target="tpu_custom_call" | custom-call | flops 4294967296 | tf_op jit(solution)/shard_map/pallas_call | solution.py:334
  139.1 5.0 %collective-permute-start.17 = (bf16[512,256]{1,0:T(8,128)(2,1)S(1)}, bf16[512,256]{1,0:T(8,128)(2,1)S(1)}, u32[]{:S(2)}, u32[]{:S(2)}) collective-permute-start(bf16[512,256]{1,0:T(8,128)(2,1)S(1)} %get-tuple-element.37), channel_id=1, source_target_pairs={{0,128},{64,192},{128,0},{192,64},{1,129},{65,193},{129,1},{193,65... | collective-permute-start | bytes 786440 | tf_op jit(solution)/shard_map/ppermute | solution.py:371
  144.0 2.0 %collective-permute-start.18 = (bf16[512,256]{1,0:T(8,128)(2,1)S(1)}, bf16[512,256]{1,0:T(8,128)(2,1)S(1)}, u32[]{:S(2)}, u32[]{:S(2)}) collective-permute-start(bf16[512,256]{1,0:T(8,128)(2,1)S(1)} %get-tuple-element.38), channel_id=1, source_target_pairs={{0,192},{64,0},{128,64},{192,128},{1,193},{65,1},{129,65},{193,129... | collective-permute-start | bytes 786440 | tf_op jit(solution)/shard_map/ppermute | solution.py:371
  146.1 4.2 %shard_map.166 = (bf16[512,256]{1,0:T(8,128)(2,1)S(1)}, bf16[512,256]{1,0:T(8,128)(2,1)S(1)}, bf16[512,256]{1,0:T(8,128)(2,1)S(1)}, bf16[512,256]{1,0:T(8,128)(2,1)S(1)}) custom-call(bf16[8,256,512]{2,1,0:T(8,128)(2,1)} %shard_map.163.x1_0, bf16[8,256,512]{2,1,0:T(8,128)(2,1)} %shard_map.164.x1_1, bf16[8,128,256]{2,1,0:T(8,128)(2,1)S(1)} %collective-permute-done.19.t0, ...), custom_call_target="tpu_custom_call" | custom-call | flops 4294967296 | tf_op jit(solution)/shard_map/pallas_call | solution.py:334
  150.4 1.3 collective-permute-start.24
  151.7 1.4 collective-permute-start.25
  153.7 1.4 shard_map.168
  155.8 6.6 %collective-permute-done.23.refs_5_ = bf16[512,256]{1,0:T(8,128)(2,1)S(1)} collective-permute-done((bf16[512,256]{1,0:T(8,128)(2,1)S(1)}, bf16[512,256]{1,0:T(8,128)(2,1)S(1)}, u32[]{:S(2)}, u32[]{:S(2)}) %collective-permute-start.23) | collective-permute-done | bytes 262176 | tf_op jit(solution)/shard_map/ppermute | solution.py:371
  162.4 4.7 %collective-permute-done.24.refs_6_ = bf16[512,256]{1,0:T(8,128)(2,1)S(1)} collective-permute-done((bf16[512,256]{1,0:T(8,128)(2,1)S(1)}, bf16[512,256]{1,0:T(8,128)(2,1)S(1)}, u32[]{:S(2)}, u32[]{:S(2)}) %collective-permute-start.24) | collective-permute-done | bytes 262176 | tf_op jit(solution)/shard_map/ppermute | solution.py:371
  167.0 1.2 shard_map.167
  (81 shorter events, 13.7 us)
Async XLA Ops:
  4.2 14.8 %all-to-all-start = ((bf16[8,128,128]{2,1,0:T(8,128)(2,1)}), bf16[8,128,128]{2,1,0:T(8,128)(2,1)S(1)}, u32[]{:S(2)}, u32[]{:S(2)}) async-start(bf16[8,128,128]{2,1,0:T(8,128)(2,1)} %shard_map.157), calls=%async_computation | async-start | bytes 524288 | tf_op jit(solution)/shard_map/all_to_all | solution.py:389
  45.1 10.3 %collective-permute-start = (bf16[8,192,128]{2,1,0:T(8,128)(2,1)S(1)}, bf16[8,192,128]{2,1,0:T(8,128)(2,1)S(1)}, u32[]{:S(2)}, u32[]{:S(2)}) collective-permute-start(bf16[8,192,128]{2,1,0:T(8,128)(2,1)S(1)} %slice.9.refs_0_), channel_id=1, source_target_pairs={{0,6},{2,0},{4,2},{6,4},{1,7},{3,1},{5,3},{7,5},{8,14},{10,8},{12,... | collective-permute-start | bytes 1179656 | tf_op jit(solution)/shard_map/ppermute | solution.py:371
  46.4 11.2 %collective-permute-start.1 = (bf16[8,192,128]{2,1,0:T(8,128)(2,1)S(1)}, bf16[8,192,128]{2,1,0:T(8,128)(2,1)S(1)}, u32[]{:S(2)}, u32[]{:S(2)}) collective-permute-start(bf16[8,192,128]{2,1,0:T(8,128)(2,1)S(1)} %slice.9.refs_0_), channel_id=1, source_target_pairs={{0,4},{2,6},{4,0},{6,2},{1,5},{3,7},{5,1},{7,3},{8,12},{10,14},{12... | collective-permute-start | bytes 1179656 | tf_op jit(solution)/shard_map/ppermute | solution.py:371
  47.0 20.4 %collective-permute-start.2 = (bf16[8,192,128]{2,1,0:T(8,128)(2,1)S(1)}, bf16[8,192,128]{2,1,0:T(8,128)(2,1)S(1)}, u32[]{:S(2)}, u32[]{:S(2)}) collective-permute-start(bf16[8,192,128]{2,1,0:T(8,128)(2,1)S(1)} %slice.9.refs_0_), channel_id=1, source_target_pairs={{0,2},{2,4},{4,6},{6,0},{1,3},{3,5},{5,7},{7,1},{8,10},{10,12},{12... | collective-permute-start | bytes 1179656 | tf_op jit(solution)/shard_map/ppermute | solution.py:371
  47.6 24.7 %collective-permute-start.3 = (bf16[8,192,128]{2,1,0:T(8,128)(2,1)S(1)}, bf16[8,192,128]{2,1,0:T(8,128)(2,1)S(1)}, u32[]{:S(2)}, u32[]{:S(2)}) collective-permute-start(bf16[8,192,128]{2,1,0:T(8,128)(2,1)S(1)} %slice.9.refs_0_), channel_id=1, source_target_pairs={{0,1},{1,0},{2,3},{3,2},{4,5},{5,4},{6,7},{7,6},{8,9},{9,8},{10,11... | collective-permute-start | bytes 1179656 | tf_op jit(solution)/shard_map/ppermute | solution.py:371
  55.4 16.9 %collective-permute-start.4 = (bf16[8,192,128]{2,1,0:T(8,128)(2,1)S(1)}, bf16[8,192,128]{2,1,0:T(8,128)(2,1)S(1)}, u32[]{:S(2)}, u32[]{:S(2)}) collective-permute-start(bf16[8,192,128]{2,1,0:T(8,128)(2,1)S(1)} %collective-permute-done.refs_1_), channel_id=1, source_target_pairs={{0,1},{1,0},{2,3},{3,2},{4,5},{5,4},{6,7},{7,6},{8,9},{9,8},{10,11... | collective-permute-start | bytes 1179656 | tf_op jit(solution)/shard_map/ppermute | solution.py:371
  57.7 14.6 %collective-permute-start.5 = (bf16[8,192,128]{2,1,0:T(8,128)(2,1)S(1)}, bf16[8,192,128]{2,1,0:T(8,128)(2,1)}, u32[]{:S(2)}, u32[]{:S(2)}) collective-permute-start(bf16[8,192,128]{2,1,0:T(8,128)(2,1)S(1)} %collective-permute-done.1.refs_2_), channel_id=1, source_target_pairs={{0,1},{1,0},{2,3},{3,2},{4,5},{5,4},{6,7},{7,6},{8,9},{9,8},{10,11... | collective-permute-start | bytes 1179656 | tf_op jit(solution)/shard_map/ppermute | solution.py:371
  67.4 4.9 %collective-permute-start.6 = (bf16[8,192,128]{2,1,0:T(8,128)(2,1)S(1)}, bf16[8,192,128]{2,1,0:T(8,128)(2,1)}, u32[]{:S(2)}, u32[]{:S(2)}) collective-permute-start(bf16[8,192,128]{2,1,0:T(8,128)(2,1)S(1)} %collective-permute-done.2.refs_3_), channel_id=1, source_target_pairs={{0,1},{1,0},{2,3},{3,2},{4,5},{5,4},{6,7},{7,6},{8,9},{9,8},{10,11... | collective-permute-start | bytes 1179656 | tf_op jit(solution)/shard_map/ppermute | solution.py:371
  68.7 26.1 %all-to-all-start.2 = ((bf16[8,128,256]{2,1,0:T(8,128)(2,1)}), bf16[8,128,256]{2,1,0:T(8,128)(2,1)S(1)}, u32[]{:S(2)}, u32[]{:S(2)}) async-start(bf16[8,128,256]{2,1,0:T(8,128)(2,1)} %broadcast_in_dim.15), calls=%async_computation.2 | async-start | bytes 1048576 | tf_op jit(solution)/shard_map/all_to_all | solution.py:389
  82.9 23.4 %copy-start.14 = (f32[128,512]{1,0:T(8,128)S(1)}, f32[128,512]{1,0:T(8,128)}, u32[]{:S(2)}) copy-start(f32[128,512]{1,0:T(8,128)} %copy-done.13) | copy-start | bytes 786436
  82.9 37.3 %copy-start.19 = (f32[8192]{0:T(1024)S(1)}, f32[8192]{0:T(1024)}, u32[]{:S(2)}) copy-start(f32[8192]{0:T(1024)} %param.23) | copy-start | bytes 98308
  91.2 13.7 %collective-permute-start.10 = (f32[128,512]{1,0:T(8,128)S(1)}, f32[128,512]{1,0:T(8,128)S(1)}, u32[]{:S(2)}, u32[]{:S(2)}) collective-permute-start(f32[128,512]{1,0:T(8,128)S(1)} %get-tuple-element.30.l0), channel_id=1, source_target_pairs={{0,192},{64,0},{128,64},{192,128},{1,193},{65,1},{129,65},{193,129... | collective-permute-start | bytes 786440 | tf_op jit(solution)/shard_map/ppermute | solution.py:371
  93.7 11.8 %collective-permute-start.11 = (f32[128,512]{1,0:T(8,128)S(1)}, f32[128,512]{1,0:T(8,128)S(1)}, u32[]{:S(2)}, u32[]{:S(2)}) collective-permute-start(f32[128,512]{1,0:T(8,128)S(1)} %get-tuple-element.30.l0), channel_id=1, source_target_pairs={{0,128},{64,192},{128,0},{192,64},{1,129},{65,193},{129,1},{193,65... | collective-permute-start | bytes 786440 | tf_op jit(solution)/shard_map/ppermute | solution.py:371
  94.3 15.6 %collective-permute-start.12 = (f32[128,512]{1,0:T(8,128)S(1)}, f32[128,512]{1,0:T(8,128)}, u32[]{:S(2)}, u32[]{:S(2)}) collective-permute-start(f32[128,512]{1,0:T(8,128)S(1)} %get-tuple-element.30.l0), channel_id=1, source_target_pairs={{0,64},{64,128},{128,192},{192,0},{1,65},{65,129},{129,193},{193,1... | collective-permute-start | bytes 786440 | tf_op jit(solution)/shard_map/ppermute | solution.py:371
  94.9 34.1 %collective-permute-start.13 = (bf16[8,128,256]{2,1,0:T(8,128)(2,1)S(1)}, bf16[8,128,256]{2,1,0:T(8,128)(2,1)S(1)}, u32[]{:S(2)}, u32[]{:S(2)}) collective-permute-start(bf16[8,128,256]{2,1,0:T(8,128)(2,1)S(1)} %all-to-all-done.2.t0), channel_id=1, source_target_pairs={{0,6},{2,0},{4,2},{6,4},{1,7},{3,1},{5,3},{7,5},{8,14},{10,8},{12,... | collective-permute-start | bytes 1572872 | tf_op jit(solution)/shard_map/ppermute | solution.py:371
  95.2 33.9 %collective-permute-start.14 = (bf16[8,128,256]{2,1,0:T(8,128)(2,1)S(1)}, bf16[8,128,256]{2,1,0:T(8,128)(2,1)S(1)}, u32[]{:S(2)}, u32[]{:S(2)}) collective-permute-start(bf16[8,128,256]{2,1,0:T(8,128)(2,1)S(1)} %all-to-all-done.2.t0), channel_id=1, source_target_pairs={{0,4},{2,6},{4,0},{6,2},{1,5},{3,7},{5,1},{7,3},{8,12},{10,14},{12... | collective-permute-start | bytes 1572872 | tf_op jit(solution)/shard_map/ppermute | solution.py:371
  105.6 24.0 %collective-permute-start.15 = (bf16[8,128,256]{2,1,0:T(8,128)(2,1)S(1)}, bf16[8,128,256]{2,1,0:T(8,128)(2,1)S(1)}, u32[]{:S(2)}, u32[]{:S(2)}) collective-permute-start(bf16[8,128,256]{2,1,0:T(8,128)(2,1)S(1)} %all-to-all-done.2.t0), channel_id=1, source_target_pairs={{0,2},{2,4},{4,6},{6,0},{1,3},{3,5},{5,7},{7,1},{8,10},{10,12},{12... | collective-permute-start | bytes 1572872 | tf_op jit(solution)/shard_map/ppermute | solution.py:371
  106.3 13.8 %collective-permute-start.7 = (f32[128,512]{1,0:T(8,128)S(1)}, f32[128,512]{1,0:T(8,128)S(1)}, u32[]{:S(2)}, u32[]{:S(2)}) collective-permute-start(f32[128,512]{1,0:T(8,128)S(1)} %copy-done.14), channel_id=1, source_target_pairs={{0,192},{64,0},{128,64},{192,128},{1,193},{65,1},{129,65},{193,129... | collective-permute-start | bytes 786440 | tf_op jit(solution)/shard_map/ppermute | solution.py:371
  109.9 17.2 %collective-permute-start.8 = (f32[128,512]{1,0:T(8,128)S(1)}, f32[128,512]{1,0:T(8,128)}, u32[]{:S(2)}, u32[]{:S(2)}) collective-permute-start(f32[128,512]{1,0:T(8,128)S(1)} %copy-done.14), channel_id=1, source_target_pairs={{0,128},{64,192},{128,0},{192,64},{1,129},{65,193},{129,1},{193,65... | collective-permute-start | bytes 786440 | tf_op jit(solution)/shard_map/ppermute | solution.py:371
  120.1 9.5 %collective-permute-start.9 = (f32[128,512]{1,0:T(8,128)S(1)}, f32[128,512]{1,0:T(8,128)}, u32[]{:S(2)}, u32[]{:S(2)}) collective-permute-start(f32[128,512]{1,0:T(8,128)S(1)} %copy-done.14), channel_id=1, source_target_pairs={{0,64},{64,128},{128,192},{192,0},{1,65},{65,129},{129,193},{193,1... | collective-permute-start | bytes 786440 | tf_op jit(solution)/shard_map/ppermute | solution.py:371
  127.1 12.0 %collective-permute-start.19 = (bf16[8,128,256]{2,1,0:T(8,128)(2,1)S(1)}, bf16[8,128,256]{2,1,0:T(8,128)(2,1)S(1)}, u32[]{:S(2)}, u32[]{:S(2)}) collective-permute-start(bf16[8,128,256]{2,1,0:T(8,128)(2,1)S(1)} %all-to-all-done.2.t0), channel_id=1, source_target_pairs={{0,1},{1,0},{2,3},{3,2},{4,5},{5,4},{6,7},{7,6},{8,9},{9,8},{10,11... | collective-permute-start | bytes 1572872 | tf_op jit(solution)/shard_map/ppermute | solution.py:371
  129.0 15.0 %collective-permute-start.20 = (bf16[8,128,256]{2,1,0:T(8,128)(2,1)S(1)}, bf16[8,128,256]{2,1,0:T(8,128)(2,1)S(1)}, u32[]{:S(2)}, u32[]{:S(2)}) collective-permute-start(bf16[8,128,256]{2,1,0:T(8,128)(2,1)S(1)} %collective-permute-done.13.t1), channel_id=1, source_target_pairs={{0,1},{1,0},{2,3},{3,2},{4,5},{5,4},{6,7},{7,6},{8,9},{9,8},{10,11... | collective-permute-start | bytes 1572872 | tf_op jit(solution)/shard_map/ppermute | solution.py:371
  129.1 17.0 %collective-permute-start.21 = (bf16[8,128,256]{2,1,0:T(8,128)(2,1)S(1)}, bf16[8,128,256]{2,1,0:T(8,128)(2,1)S(1)}, u32[]{:S(2)}, u32[]{:S(2)}) collective-permute-start(bf16[8,128,256]{2,1,0:T(8,128)(2,1)S(1)} %collective-permute-done.14.t2), channel_id=1, source_target_pairs={{0,1},{1,0},{2,3},{3,2},{4,5},{5,4},{6,7},{7,6},{8,9},{9,8},{10,11... | collective-permute-start | bytes 1572872 | tf_op jit(solution)/shard_map/ppermute | solution.py:371
  129.5 16.6 %collective-permute-start.22 = (bf16[8,128,256]{2,1,0:T(8,128)(2,1)S(1)}, bf16[8,128,256]{2,1,0:T(8,128)(2,1)S(1)}, u32[]{:S(2)}, u32[]{:S(2)}) collective-permute-start(bf16[8,128,256]{2,1,0:T(8,128)(2,1)S(1)} %collective-permute-done.15.t3), channel_id=1, source_target_pairs={{0,1},{1,0},{2,3},{3,2},{4,5},{5,4},{6,7},{7,6},{8,9},{9,8},{10,11... | collective-permute-start | bytes 1572872 | tf_op jit(solution)/shard_map/ppermute | solution.py:371
  138.9 12.7 %collective-permute-start.16 = (bf16[512,256]{1,0:T(8,128)(2,1)S(1)}, bf16[512,256]{1,0:T(8,128)(2,1)S(1)}, u32[]{:S(2)}, u32[]{:S(2)}) collective-permute-start(bf16[512,256]{1,0:T(8,128)(2,1)S(1)} %get-tuple-element.36), channel_id=1, source_target_pairs={{0,64},{64,128},{128,192},{192,0},{1,65},{65,129},{129,193},{193,1... | collective-permute-start | bytes 786440 | tf_op jit(solution)/shard_map/ppermute | solution.py:371
  139.1 16.7 %collective-permute-start.17 = (bf16[512,256]{1,0:T(8,128)(2,1)S(1)}, bf16[512,256]{1,0:T(8,128)(2,1)S(1)}, u32[]{:S(2)}, u32[]{:S(2)}) collective-permute-start(bf16[512,256]{1,0:T(8,128)(2,1)S(1)} %get-tuple-element.37), channel_id=1, source_target_pairs={{0,128},{64,192},{128,0},{192,64},{1,129},{65,193},{129,1},{193,65... | collective-permute-start | bytes 786440 | tf_op jit(solution)/shard_map/ppermute | solution.py:371
  144.0 23.0 %copy-start.9 = (f32[1024]{0:T(1024)S(1)}, f32[1024]{0:T(1024)}, u32[]{:S(2)}) copy-start(f32[1024]{0:T(1024)} %param.25) | copy-start | bytes 12292
  144.0 23.0 %copy-start.10 = (f32[1024]{0:T(1024)S(1)}, f32[1024]{0:T(1024)}, u32[]{:S(2)}) copy-start(f32[1024]{0:T(1024)} %param.26) | copy-start | bytes 12292
  144.0 11.8 %collective-permute-start.18 = (bf16[512,256]{1,0:T(8,128)(2,1)S(1)}, bf16[512,256]{1,0:T(8,128)(2,1)S(1)}, u32[]{:S(2)}, u32[]{:S(2)}) collective-permute-start(bf16[512,256]{1,0:T(8,128)(2,1)S(1)} %get-tuple-element.38), channel_id=1, source_target_pairs={{0,192},{64,0},{128,64},{192,128},{1,193},{65,1},{129,65},{193,129... | collective-permute-start | bytes 786440 | tf_op jit(solution)/shard_map/ppermute | solution.py:371
  150.3 12.1 %collective-permute-start.23 = (bf16[512,256]{1,0:T(8,128)(2,1)S(1)}, bf16[512,256]{1,0:T(8,128)(2,1)S(1)}, u32[]{:S(2)}, u32[]{:S(2)}) collective-permute-start(bf16[512,256]{1,0:T(8,128)(2,1)S(1)} %get-tuple-element.41), channel_id=1, source_target_pairs={{0,64},{64,128},{128,192},{192,0},{1,65},{65,129},{129,193},{193,1... | collective-permute-start | bytes 786440 | tf_op jit(solution)/shard_map/ppermute | solution.py:371
  150.4 16.6 %collective-permute-start.24 = (bf16[512,256]{1,0:T(8,128)(2,1)S(1)}, bf16[512,256]{1,0:T(8,128)(2,1)S(1)}, u32[]{:S(2)}, u32[]{:S(2)}) collective-permute-start(bf16[512,256]{1,0:T(8,128)(2,1)S(1)} %get-tuple-element.42), channel_id=1, source_target_pairs={{0,128},{64,192},{128,0},{192,64},{1,129},{65,193},{129,1},{193,65... | collective-permute-start | bytes 786440 | tf_op jit(solution)/shard_map/ppermute | solution.py:371
  151.7 15.4 %collective-permute-start.25 = (bf16[512,256]{1,0:T(8,128)(2,1)S(1)}, bf16[512,256]{1,0:T(8,128)(2,1)S(1)}, u32[]{:S(2)}, u32[]{:S(2)}) collective-permute-start(bf16[512,256]{1,0:T(8,128)(2,1)S(1)} %get-tuple-element.43), channel_id=1, source_target_pairs={{0,192},{64,0},{128,64},{192,128},{1,193},{65,1},{129,65},{193,129... | collective-permute-start | bytes 786440 | tf_op jit(solution)/shard_map/ppermute | solution.py:371
  (16 other events, 76.6 us)

commit v2 on v1

v2 whole, which is shorter than its diff:
```python
import jax
import jax.numpy as jnp
from jax import lax
from jax.experimental import pallas as pl
from jax.experimental.pallas import tpu as pltpu
from jax.sharding import Mesh, PartitionSpec as P

BF = jnp.bfloat16
F32 = jnp.float32
NX, NZ, NY, NC = 4, 8, 4, 2
SLOTS, BLOCK, E = 4, 128, 256
HID, RANK = 1024, 128
LANE = 128


SMEM = pl.BlockSpec(memory_space=pltpu.SMEM)
VMEM = pl.BlockSpec(memory_space=pltpu.VMEM)
ANY = pl.BlockSpec(memory_space=pl.ANY)


def near(*vs):
    return [pltpu.with_memory_space_constraint(v, pltpu.VMEM) for v in vs]


def far(*vs):
    return [pltpu.with_memory_space_constraint(v, pltpu.HBM) for v in vs]


def kernel(body, out_shape, in_specs, out_specs, scratch=(), flops=0, limit=16):
    return pl.pallas_call(
        body,
        out_shape=out_shape,
        in_specs=in_specs,
        out_specs=out_specs,
        scratch_shapes=list(scratch),
        compiler_params=pltpu.CompilerParams(vmem_limit_bytes=limit * 1024 * 1024),
        cost_estimate=pl.CostEstimate(flops=flops, bytes_accessed=0, transcendentals=0),
    )


def bf(*shape):
    return jax.ShapeDtypeStruct(shape, BF)


def fetch_body(promote_in, victim_in, backing, out, promote, victim, blocks, sems):
    count = backing.shape[0]
    base = (lax.axis_index("y") * NC + lax.axis_index("c")) * count
    small = [
        pltpu.make_async_copy(promote_in, promote, sems.at[2]),
        pltpu.make_async_copy(victim_in, victim, sems.at[3]),
    ]
    for copy in small:
        copy.start()
    out[...] = jnp.zeros(out.shape, BF)
    for copy in small:
        copy.wait()
    copies = []
    for k in range(2):
        at = jnp.clip(promote[0, k] - base, 0, count - 1)
        copies.append(pltpu.make_async_copy(backing.at[at], blocks.at[k], sems.at[k]))
    for copy in copies:
        copy.start()
    for copy in copies:
        copy.wait()
    for k in range(2):
        local = promote[0, k] - base

        @pl.when((local >= 0) & (local < count))
        def _():
            s = victim[0, k]
            out[2 * s] = blocks[k, :, :LANE]
            out[2 * s + 1] = blocks[k, :, LANE:]


def fetch(promote, victim, backing):
    return kernel(
        fetch_body, bf(NY * NC, BLOCK, LANE), [ANY] * 3, VMEM,
        [pltpu.SMEM((1, 2), jnp.int32), pltpu.SMEM((1, 2), jnp.int32),
         pltpu.VMEM((2, BLOCK, E), BF), pltpu.SemaphoreType.DMA((4,))],
    )(*far(promote, victim, backing))


def piece_body(victim, arrived, cache, factors, sent, out):
    s = lax.axis_index("y")
    c = lax.axis_index("c")
    total = arrived[0]
    for i in range(1, NY * NC):
        total = total + arrived[i]
    block = cache[s]
    kept = jnp.where(c == 0, block[:, :LANE], block[:, LANE:])
    evicted = (victim[0, 0] == s) | (victim[0, 1] == s)
    piece = jnp.where(evicted, total, kept).T
    for i in range(NZ):
        out[i, :LANE, :] = piece
        out[i, LANE:160, :] = factors[...]
        out[i, 160:, :] = sent[i]


def make_piece(victim, arrived, cache, factors, sent):
    return kernel(
        piece_body, bf(NZ, 224, BLOCK), [SMEM] + [VMEM] * 4, VMEM
    )(victim, *near(arrived, cache, factors, sent))


def back_body(resident, victim, cache, backing, out):
    base = (lax.axis_index("y") * NC + lax.axis_index("c")) * backing.shape[0]
    out[...] = backing[...]
    for k in range(2):
        v = victim[0, k]
        local = resident[0, v] - base

        @pl.when((local >= 0) & (local < backing.shape[0]))
        def _():
            out[local] = cache[v]


def write_back(resident, victim, cache, backing):
    return kernel(
        back_body, jax.ShapeDtypeStruct(backing.shape, BF), [SMEM, SMEM, VMEM, VMEM], VMEM
    )(resident, victim, cache, backing)


def route_body(lookups_in, route_in, down_in, out, factors, lookups, route, down, scratch, sems):
    copies = [
        pltpu.make_async_copy(source, hold, sems.at[n])
        for n, (source, hold) in enumerate(((down_in, down), (route_in, route), (lookups_in, lookups)))
    ]
    for copy in copies:
        copy.start()
    copies[0].wait()
    o = lax.axis_index("y") * NC + lax.axis_index("c")
    rows = RANK // (NY * NC)
    scratch[...] = down[...].T
    piece = scratch[pl.ds(pl.multiple_of(o * rows, rows), rows), :]
    factors[0:16, :] = piece[:, :LANE]
    factors[16:32, :] = piece[:, LANE:]
    copies[1].wait()
    copies[2].wait()
    batches, bag, count = lookups.shape
    tiles = count // LANE

    def one(z, _):
        for q in range(NX):
            parts = []
            for b in range(batches):
                row = jnp.broadcast_to(route[b, pl.ds(q * NZ + z, 1), :], (bag, LANE))
                lane = row & (LANE - 1)
                tile = row >> 7
                got = jnp.zeros((bag, LANE), jnp.int32)
                for v in range(tiles):
                    cand = jnp.take_along_axis(
                        lookups[b, :, v * LANE : (v + 1) * LANE], lane, axis=1, mode="promise_in_bounds"
                    )
                    got = jnp.where(tile == v, cand, got)
                parts.append(got)
            both = (jnp.concatenate(parts, axis=0) - 256).astype(F32).astype(BF)
            out[z, q * 16 : q * 16 + 16, :] = both
        return 0

    lax.fori_loop(0, NZ, one, 0)


def route_lookups(lookups, route, down):
    return kernel(
        route_body, [bf(NZ, 64, LANE), bf(32, LANE)], [ANY] * 3, [VMEM] * 2,
        [pltpu.VMEM(lookups.shape, jnp.int32), pltpu.VMEM(route.shape, jnp.int32), pltpu.VMEM(down.shape, BF),
         pltpu.VMEM((RANK, E), BF), pltpu.SemaphoreType.DMA((3,))],
        flops=1 << 22,
    )(*far(lookups, route, down))


def own_body(up, mlp, out):
    o = lax.axis_index("y") * NC + lax.axis_index("c")
    rows = RANK // (NY * NC)
    out[:LANE, :] = mlp[:, pl.ds(pl.multiple_of(o * LANE, LANE), LANE)].T
    out[LANE:, :] = up[pl.ds(pl.multiple_of(o * rows, rows), rows), :]


def own_weights(up, mlp):
    return kernel(own_body, bf(LANE + 16, E), [VMEM] * 2, VMEM)(up, mlp)


def stack_body(*refs):
    out = refs[-1]
    z = lax.axis_index("z")
    for k in range(NZ):
        out[(z + k) % NZ] = refs[k][...]


def stacked(parts):
    return kernel(stack_body, bf(NZ, LANE + 16, E), [VMEM] * NZ, VMEM)(*near(*parts))


def factor(tables, i):
    rows = [jnp.concatenate([t[i, LANE : LANE + 16, :], t[i, LANE + 16 :, :]], axis=1) for t in tables]
    return jnp.concatenate(rows, axis=0)


def load(sources, holds, sems):
    waits = []
    for i in range(NZ):
        step = []
        for n, (source, hold) in enumerate(zip(sources, holds)):
            copy = pltpu.make_async_copy(source.at[i], hold.at[i], sems.at[n, i])
            copy.start()
            step.append(copy)
        waits.append(step)
    return waits


def pool_step(batch, i, table, down, lookups, hold):
    y = lax.axis_index("y")
    line = lax.broadcasted_iota(jnp.int32, (BLOCK, LANE), 0).astype(F32).astype(BF)
    none = jnp.zeros((), BF)
    for q in range(NX):
        wanted = lookups[i, q * 16 + batch * 8 : q * 16 + batch * 8 + 8, :]
        wanted = wanted.astype(F32).astype(jnp.int32) + 256
        slot = ((wanted >> 7) + (NY - y)) & 3
        weight = jnp.where((slot & 1) == 1, 16.0, 1.0)
        row = (wanted & (BLOCK - 1)).astype(F32).astype(BF)
        lower = jnp.where(slot < 2, weight, 0.0).astype(BF)
        upper = jnp.where(slot < 2, 0.0, weight).astype(BF)
        sums = [None, None]
        for l in range(8):
            hit = jnp.broadcast_to(row[l : l + 1, :], (BLOCK, LANE)) == line
            for n, w in enumerate((lower, upper)):
                term = jnp.where(hit, jnp.broadcast_to(w[l : l + 1, :], (BLOCK, LANE)), none)
                sums[n] = term if sums[n] is None else sums[n] + term
        for n in range(2):
            second = (sums[n] * jnp.asarray(0.0625, BF) + jnp.asarray(128.0, BF)) - jnp.asarray(128.0, BF)
            first = sums[n] - second * jnp.asarray(16.0, BF)
            at = 2 * n * BLOCK
            hold[at : at + BLOCK, q * LANE : (q + 1) * LANE] = first
            hold[at + BLOCK : at + 2 * BLOCK, q * LANE : (q + 1) * LANE] = second
    pooled = jnp.dot(table, hold[...], preferred_element_type=F32).astype(BF)
    return pooled, jnp.dot(down, pooled, preferred_element_type=F32)


def pool0_body(lookups, *refs):
    tables = refs[0:8]
    x0_out, low_out, table_out, factor_out, new_cache = refs[8:13]
    counts, x0, whole_table, factors, sems = refs[13:]
    y = lax.axis_index("y")
    c = lax.axis_index("c")
    low_out[...] = jnp.zeros(low_out.shape, F32)

    def writes(i):
        return [
            pltpu.make_async_copy(source.at[i], out.at[i], sems.at[n, i])
            for n, (source, out) in enumerate(((x0, x0_out), (whole_table, table_out), (factors, factor_out)))
        ]

    def pair(j, _):
        low = None
        for m in range(2):
            i = 2 * j + m
            mine = jnp.concatenate([t[i, :LANE, :] for t in tables[:4]], axis=1)
            theirs = jnp.concatenate([t[i, :LANE, :] for t in tables[4:]], axis=1)
            table = jnp.concatenate([jnp.where(c == 0, mine, theirs), jnp.where(c == 0, theirs, mine)], axis=0)
            whole_table[i] = table
            down = factor(tables, i)
            factors[i] = down
            pooled, part = pool_step(0, i, table, down, lookups, counts.at[m])
            x0[i] = pooled
            low = part if low is None else low + part
            for copy in writes(i):
                copy.start()
        low_out[...] = low_out[...] + low
        return 0

    lax.fori_loop(0, NZ // 2, pair, 0)
    own = whole_table[lax.axis_index("z")]
    for r in range(NY):
        new_cache[(y + r) % NY] = own[:, r * BLOCK : (r + 1) * BLOCK].T
    for i in range(NZ):
        for copy in writes(i):
            copy.wait()


MANY = NX * LANE


def pool0(lookups, tables):
    return kernel(
        pool0_body,
        [pltpu.HBM((NZ, E, MANY), BF), jax.ShapeDtypeStruct((RANK, MANY), F32), pltpu.HBM((NZ, E, SLOTS * BLOCK), BF),
         pltpu.HBM((NZ, RANK, E), BF), bf(SLOTS, BLOCK, E)],
        [VMEM] * 9, [ANY, VMEM, ANY, ANY, VMEM],
        [pltpu.VMEM((2, SLOTS * BLOCK, MANY), BF), pltpu.VMEM((NZ, E, MANY), BF), pltpu.VMEM((NZ, E, SLOTS * BLOCK), BF),
         pltpu.VMEM((NZ, RANK, E), BF), pltpu.SemaphoreType.DMA((3, NZ))],
        flops=1 << 32, limit=24,
    )(*near(lookups, *tables))


def pool1_body(lookups, table_in, factor_in, x0_out, low_out, counts, x0, tables, factors, sems, out_sems):
    low_out[...] = jnp.zeros(low_out.shape, F32)

    def reads(i):
        return [
            pltpu.make_async_copy(source.at[i], hold.at[i], sems.at[n, i])
            for n, (source, hold) in enumerate(((table_in, tables), (factor_in, factors)))
        ]

    def write(i):
        return pltpu.make_async_copy(x0.at[i], x0_out.at[i], out_sems.at[i])

    for i in range(NZ):
        for copy in reads(i):
            copy.start()

    def pair(j, _):
        low = None
        for m in range(2):
            i = 2 * j + m
            for copy in reads(i):
                copy.wait()
            pooled, part = pool_step(1, i, tables[i], factors[i], lookups, counts.at[m])
            x0[i] = pooled
            low = part if low is None else low + part
            write(i).start()
        low_out[...] = low_out[...] + low
        return 0

    lax.fori_loop(0, NZ // 2, pair, 0)
    for i in range(NZ):
        write(i).wait()


def pool1(lookups, table, factors):
    return kernel(
        pool1_body, [pltpu.HBM((NZ, E, MANY), BF), jax.ShapeDtypeStruct((RANK, MANY), F32)],
        [VMEM, ANY, ANY], [ANY, VMEM],
        [pltpu.VMEM((2, SLOTS * BLOCK, MANY), BF), pltpu.VMEM((NZ, E, MANY), BF), pltpu.VMEM((NZ, E, SLOTS * BLOCK), BF),
         pltpu.VMEM((NZ, RANK, E), BF), pltpu.SemaphoreType.DMA((2, NZ)), pltpu.SemaphoreType.DMA((NZ,))],
        flops=1 << 32, limit=24,
    )(*near(lookups), *far(table, factors))


def cross_body(*refs):
    lows = refs[0:4]
    bias = refs[4]
    tops = refs[5:13]
    x0_in = refs[13]
    outs = refs[14:18]
    x0, weights, crossed, hold, sems = refs[18:]
    x = lax.axis_index("x")
    waits = load((x0_in,), (x0,), sems)
    low = (lows[0][...] + lows[1][...] + lows[2][...] + lows[3][...]).astype(BF)
    columns = bias[pl.ds(pl.multiple_of(x * NZ, NZ), NZ), :].T
    for i in range(NZ):
        for copy in waits[i]:
            copy.wait()
        up = jnp.concatenate([t[i, LANE:, :] for t in tops], axis=0)
        gate = lax.dot_general(up, low, (((0,), (0,)), ((), ())), preferred_element_type=F32)
        gate = gate + columns[:, i : i + 1]
        features = x0[i].astype(F32)
        crossed[i * E : (i + 1) * E, :] = (features * gate + features).astype(BF)
        for j in range(8):
            weights[j * LANE : (j + 1) * LANE, i * E : (i + 1) * E] = tops[j][i, :LANE, :]
    part = jnp.dot(weights[...], crossed[...], preferred_element_type=F32).astype(BF)
    for q in range(NX):
        hold[q] = part[:, q * LANE : (q + 1) * LANE]
    for r in range(NX):
        outs[r][...] = hold[(x + r) % NX]


def cross(lows, bias, tops, x0):
    return kernel(
        cross_body, [bf(HID, LANE)] * NX, [VMEM] * 13 + [ANY], [VMEM] * NX,
        [pltpu.VMEM((NZ, E, MANY), BF), pltpu.VMEM((HID, NZ * E), BF), pltpu.VMEM((NZ * E, MANY), BF),
         pltpu.VMEM((NX, HID, LANE), BF), pltpu.SemaphoreType.DMA((1, NZ))],
        flops=1 << 32, limit=32,
    )(*near(*lows, bias, *tops), *far(x0))


def score_body(mlp_bias, mlp_out, out_bias, *refs):
    hs = refs[0:8]
    out, rows = refs[8:]
    y = lax.axis_index("y")
    c = lax.axis_index("c")
    for j in range(8):
        o = ((y + j % 4) % NY) * NC + (c + j // 4) % NC
        rows[j : j + 1, :] = mlp_bias[pl.ds(o, 1), :]
        rows[8 + j : 9 + j, :] = mlp_out[pl.ds(o, 1), :]
    columns = rows[...].T
    for b in range(2):
        total = jnp.zeros((LANE, LANE), F32)
        for j in range(8):
            before = columns[:, j : j + 1]
            for h in hs[4 * b : 4 * b + 4]:
                before = before + h[j * LANE : (j + 1) * LANE, :].astype(F32)
            total = total + jnp.maximum(before, 0.0) * columns[:, 8 + j : 9 + j]
        out[b : b + 1, :] = jnp.sum(total, axis=0, keepdims=True) + out_bias[0]


def score(mlp_bias, mlp_out, out_bias, ha, hb):
    return kernel(
        score_body, jax.ShapeDtypeStruct((2, LANE), F32), [VMEM, VMEM, SMEM] + [VMEM] * 8, VMEM,
        [pltpu.VMEM((16, LANE), F32)],
    )(mlp_bias, mlp_out, out_bias, *near(*ha, *hb))


def shift(v, axis, size, k):
    return lax.ppermute(v, axis, [(i, (i + k) % size) for i in range(size)])


def spread(v, axis, size):
    out = [v]
    for k in range(1, size):
        out.append(shift(v, axis, size, size - k))
    return out


def deal(parts):
    out = [parts[0]]
    for k in range(1, NX):
        out.append(shift(parts[k], "x", NX, k))
    return out


def exchange(v, axis):
    return lax.all_to_all(v, axis, 0, 0, tiled=True)


def swaps(vs):
    return [shift(v, "c", NC, 1) for v in vs]


def tie(v, *others):
    return lax.optimization_barrier((v, *others))[0]


def on_device(
    cache, backing, resident, promote, victim, lookups, route,
    dcn_down, dcn_up, dcn_bias, mlp_in, mlp_bias, mlp_out, out_bias,
):
    cache = cache[0]
    backing = backing[0]
    bias = dcn_bias.reshape(-1, E)
    outgoing = fetch(promote, victim, backing)
    arrived = exchange(outgoing, ("y", "c"))
    wanted = jnp.transpose(lookups[:, :, 0, :], (0, 2, 1))
    sent, factors = route_lookups(wanted, route[:, 0].reshape(2, -1, LANE), dcn_down)
    piece = make_piece(victim, arrived, cache, factors, sent)
    mixed = exchange(piece, "z")
    top = own_weights(dcn_up, mlp_in)
    new_backing = write_back(resident, victim, cache, backing)
    own = spread(mixed[:, :160, :], "y", NY)
    mixed = mixed[:, 160:, :]
    tops = stacked(spread(tie(top, piece), "z", NZ))
    tables = own + swaps(own)
    own = spread(tops, "y", NY)
    tops = own + swaps(own)
    x00, low0, table, factors, new_cache = pool0(mixed, tables)
    lows0 = spread(low0, "x", NX)
    x01, low1 = pool1(tie(mixed, low0), table, factors)
    lows1 = spread(low1, "x", NX)
    h0 = cross(lows0, bias, tops, tie(x00, low1))
    ra = deal(h0)
    h1 = cross(lows1, bias, tops, tie(x01, h0[0]))
    rb = deal(h1)
    scores = score(mlp_bias.reshape(8, LANE), mlp_out.reshape(8, LANE), out_bias, ra, rb)
    return scores[:, None, :], new_cache[None], new_backing[None]


def solution(mesh):
    fine = Mesh(mesh.devices.reshape(NX, NZ, NY, NC), ("x", "z", "y", "c"))
    ca, ow = ("x", "z"), ("y", "c")
    in_specs = (
        P(ca, None, None, None),
        P(ca, ow, None, None),
        P(ca, None),
        P(ca, None),
        P(ca, None),
        P(None, ow, ca, None),
        P(None, ow, None),
        P(ca, None),
        P(None, ca),
        P(),
        P(ca, None),
        P(),
        P(),
        P(),
    )
    out_specs = (
        P(None, ow, ca),
        P(ca, None, None, None),
        P(ca, ow, None, None),
    )
    return jax.shard_map(
        on_device, mesh=fine, in_specs=in_specs, out_specs=out_specs, check_vma=False
    )
```

time: 169 us -> 173 us (1.024)
  starting transfers between devices: 42.8 us -> 71.6 us
  blocking collectives: 25.4 us -> 0 us
  waiting for transfers between devices: 41.9 us -> 55.7 us
  Pallas kernels: 46.8 us -> 39 us
  local copies, waits for them, and re-layouts: 9.8 us -> 4.31 us
    all_to_all x1 -> x0, blocking collectives: 25.4 us -> none  [exchange(): return lax.all_to_all(v, axis, 0, 0, tiled=True)]
    ppermute x26 -> x33, starting transfers between devices: 32.7 us -> 57.5 us  [shift(): return lax.ppermute(v, axis, [(i, (i + k) % size) for i in range(size)])]
    ppermute x26 -> x33, waiting for transfers between devices: 41.9 us -> 53.1 us  [shift(): return lax.ppermute(v, axis, [(i, (i + k) % size) for i in range(size)])]
    unnamed x40 -> x28, local copies, waits for them, and re-layouts: 8.92 us -> 3.35 us
    pallas_call x8 -> x7, Pallas kernels: 26.1 us -> 21.3 us  [the longest x2 13.3 us: cross(): kernel(cross_body, [bf(HID, LANE)] * NX, [VMEM] * 13 + [ANY], [VMEM] * NX...]
    all_to_all x2, starting transfers between devices: 10 us -> 14.1 us  [exchange(): return lax.all_to_all(v, axis, 0, 0, tiled=True)]
    all_to_all x2, waiting for transfers between devices: 0.01 us -> 2.53 us  [exchange(): return lax.all_to_all(v, axis, 0, 0, tiled=True)]
    pallas_call x1, Pallas kernels: 9.81 us -> 7.94 us  [pool0(): kernel(pool0_body, [pltpu.HBM((NZ, E, MANY), BF), jax.ShapeDtypeStruct((R...]
  transfers between devices with their start and end apart: 28 -> 35, of which waited for: 7 -> 16; matrix products, arithmetic and copies ran while one was open for 1% -> 1% of each run, Pallas kernels for 25% -> 16%
where the time goes in v2:
time: 173 us; the launch traced here: 172 us
  starting transfers between devices  71.6 us (41%)
  waiting for transfers between devices  55.7 us (32%)
  Pallas kernels  39 us (23%)
  local copies, waits for them, and re-layouts  4.31 us (2%)
    ppermute x33, starting transfers between devices, shift(): return lax.ppermute(v, axis, [(i, (i + k) % size) for i in range(size)])  57.5 us
    ppermute x33, waiting for transfers between devices, shift(): return lax.ppermute(v, axis, [(i, (i + k) % size) for i in range(size)])  53.1 us
    all_to_all x2, starting transfers between devices, exchange(): return lax.all_to_all(v, axis, 0, 0, tiled=True)  14.1 us
    pallas_call x2, Pallas kernels, cross(): kernel(cross_body, [bf(HID, LANE)] * NX, [VMEM] * 13 + [ANY], [VMEM] * NX...  13.3 us
    pallas_call x1, Pallas kernels, pool0(): kernel(pool0_body, [pltpu.HBM((NZ, E, MANY), BF), jax.ShapeDtypeStruct((R...  7.94 us
    pallas_call x1, Pallas kernels, pool1(): kernel(pool1_body, [pltpu.HBM((NZ, E, MANY), BF), jax.ShapeDtypeStruct((R...  7.18 us
    pallas_call x1, Pallas kernels, route_lookups(): kernel(route_body, [bf(NZ, 64, LANE), bf(32, LANE)], [ANY] * 3, [VMEM] *...  3.96 us
  transfers between devices with their start and end apart: 35, of which 16 were waited for; matrix products, arithmetic and copies ran while one was open for 1% of the time, Pallas kernels for 16%

profile of v2, /device:TPU:1, one launch (start us, length us, event | category | flops | bytes accessed | tf_op | source)
XLA Modules:
  0.0 172.1 jit_solution(9094572648813156945)
XLA Ops:
  0.7 2.5 %shard_map.157 = bf16[8,128,128]{2,1,0:T(8,128)(2,1)} custom-call(s32[1,2]{1,0:T(1,128)} %promote_in.1, s32[1,2]{1,0:T(1,128)} %victim.3, bf16[8,128,256]{2,1,0:T(8,128)(2,1)} %bitcast.13), custom_call_target="tpu_custom_call" | custom-call | tf_op jit(solution)/shard_map/pallas_call | solution.py:76
  3.1 6.5 %all-to-all-start = ((bf16[8,128,128]{2,1,0:T(8,128)(2,1)}), bf16[8,128,128]{2,1,0:T(8,128)(2,1)S(1)}, u32[]{:S(2)}, u32[]{:S(2)}) async-start(bf16[8,128,128]{2,1,0:T(8,128)(2,1)} %shard_map.157), calls=%async_computation | async-start | bytes 524288 | tf_op jit(solution)/shard_map/all_to_all | solution.py:422
  9.6 4.0 %shard_map.158 = (bf16[8,64,128]{2,1,0:T(8,128)(2,1)S(1)}, bf16[32,128]{1,0:T(8,128)(2,1)S(1)}) custom-call(s32[2,8,4096]{2,1,0:T(8,128)} %bitcast.20, s32[2,32,128]{2,1,0:T(8,128)} %bitcast.21, bf16[256,128]{1,0:T(8,128)(2,1)} %down_in.1), custom_call_target="tpu_custom_call" | custom-call | flops 4194304 | tf_op jit(solution)/shard_map/pallas_call | solution.py:164
  13.6 2.5 %all-to-all-done.arrived = bf16[8,128,128]{2,1,0:T(8,128)(2,1)S(1)} async-done(((bf16[8,128,128]{2,1,0:T(8,128)(2,1)}), bf16[8,128,128]{2,1,0:T(8,128)(2,1)S(1)}, u32[]{:S(2)}, u32[]{:S(2)}) %all-to-all-start) | async-done | bytes 262176 | tf_op jit(solution)/shard_map/all_to_all | solution.py:422
  19.2 7.6 %all-to-all-start.1 = ((bf16[8,224,128]{2,1,0:T(8,128)(2,1)}), bf16[8,224,128]{2,1,0:T(8,128)(2,1)S(1)}, u32[]{:S(2)}, u32[]{:S(2)}) async-start(bf16[8,224,128]{2,1,0:T(8,128)(2,1)} %shard_map.159), calls=%async_computation.1 | async-start | bytes 917504 | tf_op jit(solution)/shard_map/all_to_all | solution.py:422
  26.9 2.7 %collective-permute-start.10 = (bf16[144,256]{1,0:T(8,128)(2,1)S(1)}, bf16[144,256]{1,0:T(8,128)(2,1)S(1)}, u32[]{:S(2)}, u32[]{:S(2)}) collective-permute-start(bf16[144,256]{1,0:T(8,128)(2,1)S(1)} %shard_map.161.refs_0_), channel_id=1, source_target_pairs={{0,56},{8,0},{16,8},{24,16},{32,24},{40,32},{48,40},{56,48},{1,57}... | collective-permute-start | bytes 221192 | tf_op jit(solution)/shard_map/ppermute | solution.py:404
  29.6 2.1 %collective-permute-start.11 = (bf16[144,256]{1,0:T(8,128)(2,1)S(1)}, bf16[144,256]{1,0:T(8,128)(2,1)S(1)}, u32[]{:S(2)}, u32[]{:S(2)}) collective-permute-start(bf16[144,256]{1,0:T(8,128)(2,1)S(1)} %shard_map.161.refs_0_), channel_id=1, source_target_pairs={{0,48},{8,56},{16,0},{24,8},{32,16},{40,24},{48,32},{56,40},{1,49}... | collective-permute-start | bytes 221192 | tf_op jit(solution)/shard_map/ppermute | solution.py:404
  32.9 3.3 %collective-permute-start.13 = (bf16[144,256]{1,0:T(8,128)(2,1)S(1)}, bf16[144,256]{1,0:T(8,128)(2,1)S(1)}, u32[]{:S(2)}, u32[]{:S(2)}) collective-permute-start(bf16[144,256]{1,0:T(8,128)(2,1)S(1)} %shard_map.161.refs_0_), channel_id=1, source_target_pairs={{0,32},{8,40},{16,48},{24,56},{32,0},{40,8},{48,16},{56,24},{1,33}... | collective-permute-start | bytes 221192 | tf_op jit(solution)/shard_map/ppermute | solution.py:404
  36.2 2.0 %collective-permute-done.10.refs_1_ = bf16[144,256]{1,0:T(8,128)(2,1)S(1)} collective-permute-done((bf16[144,256]{1,0:T(8,128)(2,1)S(1)}, bf16[144,256]{1,0:T(8,128)(2,1)S(1)}, u32[]{:S(2)}, u32[]{:S(2)}) %collective-permute-start.10) | collective-permute-done | bytes 73760 | tf_op jit(solution)/shard_map/ppermute | solution.py:404
  39.4 1.8 %collective-permute-done.11.refs_2_ = bf16[144,256]{1,0:T(8,128)(2,1)S(1)} collective-permute-done((bf16[144,256]{1,0:T(8,128)(2,1)S(1)}, bf16[144,256]{1,0:T(8,128)(2,1)S(1)}, u32[]{:S(2)}, u32[]{:S(2)}) %collective-permute-start.11) | collective-permute-done | bytes 73760 | tf_op jit(solution)/shard_map/ppermute | solution.py:404
  42.1 2.6 %collective-permute-done.12.refs_3_ = bf16[144,256]{1,0:T(8,128)(2,1)S(1)} collective-permute-done((bf16[144,256]{1,0:T(8,128)(2,1)S(1)}, bf16[144,256]{1,0:T(8,128)(2,1)S(1)}, u32[]{:S(2)}, u32[]{:S(2)}) %collective-permute-start.12) | collective-permute-done | bytes 73760 | tf_op jit(solution)/shard_map/ppermute | solution.py:404
  44.7 2.0 %collective-permute-done.13.refs_4_ = bf16[144,256]{1,0:T(8,128)(2,1)S(1)} collective-permute-done((bf16[144,256]{1,0:T(8,128)(2,1)S(1)}, bf16[144,256]{1,0:T(8,128)(2,1)S(1)}, u32[]{:S(2)}, u32[]{:S(2)}) %collective-permute-start.13) | collective-permute-done | bytes 73760 | tf_op jit(solution)/shard_map/ppermute | solution.py:404
  46.7 4.9 %collective-permute-done.14.refs_5_ = bf16[144,256]{1,0:T(8,128)(2,1)S(1)} collective-permute-done((bf16[144,256]{1,0:T(8,128)(2,1)S(1)}, bf16[144,256]{1,0:T(8,128)(2,1)S(1)}, u32[]{:S(2)}, u32[]{:S(2)}) %collective-permute-start.14) | collective-permute-done | bytes 73760 | tf_op jit(solution)/shard_map/ppermute | solution.py:404
  54.7 2.7 %collective-permute-start = (bf16[8,160,128]{2,1,0:T(8,128)(2,1)S(1)}, bf16[8,160,128]{2,1,0:T(8,128)(2,1)}, u32[]{:S(2)}, u32[]{:S(2)}) collective-permute-start(bf16[8,160,128]{2,1,0:T(8,128)(2,1)S(1)} %slice.9.refs_0_), channel_id=1, source_target_pairs={{0,6},{2,0},{4,2},{6,4},{1,7},{3,1},{5,3},{7,5},{8,14},{10,8},{12,... | collective-permute-start | bytes 983048 | tf_op jit(solution)/shard_map/ppermute | solution.py:404
  58.0 7.0 %collective-permute-done.17.refs_6_ = bf16[8,144,256]{2,1,0:T(8,128)(2,1)S(1)} collective-permute-done((bf16[8,144,256]{2,1,0:T(8,128)(2,1)S(1)}, bf16[8,144,256]{2,1,0:T(8,128)(2,1)S(1)}, u32[]{:S(2)}, u32[]{:S(2)}) %collective-permute-start.17) | collective-permute-done | bytes 589856 | tf_op jit(solution)/shard_map/ppermute | solution.py:404
  65.8 1.4 collective-permute-done.18.refs_7_
  67.2 17.2 %collective-permute-start.3 = (bf16[8,160,128]{2,1,0:T(8,128)(2,1)S(1)}, bf16[8,160,128]{2,1,0:T(8,128)(2,1)S(1)}, u32[]{:S(2)}, u32[]{:S(2)}) collective-permute-start(bf16[8,160,128]{2,1,0:T(8,128)(2,1)S(1)} %slice.9.refs_0_), channel_id=1, source_target_pairs={{0,1},{1,0},{2,3},{3,2},{4,5},{5,4},{6,7},{7,6},{8,9},{9,8},{10,11... | collective-permute-start | bytes 983048 | tf_op jit(solution)/shard_map/ppermute | solution.py:404
  84.9 6.2 %collective-permute-start.4 = (bf16[8,160,128]{2,1,0:T(8,128)(2,1)}, bf16[8,160,128]{2,1,0:T(8,128)(2,1)}, u32[]{:S(2)}, u32[]{:S(2)}) collective-permute-start(bf16[8,160,128]{2,1,0:T(8,128)(2,1)} %collective-permute-done.refs_1_), channel_id=1, source_target_pairs={{0,1},{1,0},{2,3},{3,2},{4,5},{5,4},{6,7},{7,6},{8,9},{9,8},{10,11... | collective-permute-start | bytes 983048 | tf_op jit(solution)/shard_map/ppermute | solution.py:404
  91.1 2.6 %collective-permute-start.5 = (bf16[8,160,128]{2,1,0:T(8,128)(2,1)}, bf16[8,160,128]{2,1,0:T(8,128)(2,1)}, u32[]{:S(2)}, u32[]{:S(2)}) collective-permute-start(bf16[8,160,128]{2,1,0:T(8,128)(2,1)} %collective-permute-done.1.refs_2_), channel_id=1, source_target_pairs={{0,1},{1,0},{2,3},{3,2},{4,5},{5,4},{6,7},{7,6},{8,9},{9,8},{10,11... | collective-permute-start | bytes 983048 | tf_op jit(solution)/shard_map/ppermute | solution.py:404
  93.7 3.3 %collective-permute-done.2.refs_3_ = bf16[8,160,128]{2,1,0:T(8,128)(2,1)} collective-permute-done((bf16[8,160,128]{2,1,0:T(8,128)(2,1)S(1)}, bf16[8,160,128]{2,1,0:T(8,128)(2,1)}, u32[]{:S(2)}, u32[]{:S(2)}) %collective-permute-start.2) | collective-permute-done | bytes 327712 | tf_op jit(solution)/shard_map/ppermute | solution.py:404
  101.3 7.9 %shard_map.160 = (bf16[8,256,512]{2,1,0:T(8,128)(2,1)}, f32[128,512]{1,0:T(8,128)S(1)}, bf16[8,256,512]{2,1,0:T(8,128)(2,1)}, bf16[8,128,256]{2,1,0:T(8,128)(2,1)}, bf16[4,128,256]{2,1,0:T(8,128)(2,1)}) custom-call(bf16[8,64,128]{2,1,0:T(8,128)(2,1)S(1)} %slice.8.lookups, bf16[8,160,128]{2,1,0:T(8,128)(2,1)S(1)} %slice.9.refs_0_, ...), custom_call_target="tpu_custom_call" | custom-call | flops 4294967296 | tf_op jit(solution)/shard_map/pallas_call | solution.py:284
  109.3 2.6 %collective-permute-start.7 = (f32[128,512]{1,0:T(8,128)S(1)}, f32[128,512]{1,0:T(8,128)S(1)}, u32[]{:S(2)}, u32[]{:S(2)}) collective-permute-start(f32[128,512]{1,0:T(8,128)S(1)} %get-tuple-element.26.refs_0_), channel_id=1, source_target_pairs={{0,192},{64,0},{128,64},{192,128},{1,193},{65,1},{129,65},{193,129... | collective-permute-start | bytes 786440 | tf_op jit(solution)/shard_map/ppermute | solution.py:404
  112.9 7.2 %shard_map.163 = (bf16[8,256,512]{2,1,0:T(8,128)(2,1)}, f32[128,512]{1,0:T(8,128)S(1)}) custom-call(bf16[8,64,128]{2,1,0:T(8,128)(2,1)S(1)} %slice.8.lookups, bf16[8,256,512]{2,1,0:T(8,128)(2,1)} %get-tuple-element.30.table_in, bf16[8,128,256]{2,1,0:T(8,128)(2,1)} %get-tuple-element.31.factor_in), custom_call_target="tpu_custom_call" | custom-call | flops 4294967296 | tf_op jit(solution)/shard_map/pallas_call | solution.py:330
  120.1 2.2 %collective-permute-start.27 = (f32[128,512]{1,0:T(8,128)S(1)}, f32[128,512]{1,0:T(8,128)S(1)}, u32[]{:S(2)}, u32[]{:S(2)}) collective-permute-start(f32[128,512]{1,0:T(8,128)S(1)} %get-tuple-element.32.refs_0_), channel_id=1, source_target_pairs={{0,192},{64,0},{128,64},{192,128},{1,193},{65,1},{129,65},{193,129... | collective-permute-start | bytes 786440 | tf_op jit(solution)/shard_map/ppermute | solution.py:404
  123.5 4.3 %collective-permute-done.9.refs_3_ = f32[128,512]{1,0:T(8,128)S(1)} collective-permute-done((f32[128,512]{1,0:T(8,128)S(1)}, f32[128,512]{1,0:T(8,128)S(1)}, u32[]{:S(2)}, u32[]{:S(2)}) %collective-permute-start.9) | collective-permute-done | bytes 262176 | tf_op jit(solution)/shard_map/ppermute | solution.py:404
  127.8 6.6 %shard_map.164 = (bf16[1024,128]{1,0:T(8,128)(2,1)S(1)}, bf16[1024,128]{1,0:T(8,128)(2,1)S(1)}, bf16[1024,128]{1,0:T(8,128)(2,1)S(1)}, bf16[1024,128]{1,0:T(8,128)(2,1)S(1)}) custom-call(f32[128,512]{1,0:T(8,128)S(1)} %get-tuple-element.26.refs_0_, f32[128,512]{1,0:T(8,128)S(1)} %collective-permute-done.7.refs_1_, ...), custom_call_target="tpu_custom_call" | custom-call | flops 4294967296 | tf_op jit(solution)/shard_map/pallas_call | solution.py:368
  134.6 3.8 %collective-permute-done.29.refs_3_ = f32[128,512]{1,0:T(8,128)S(1)} collective-permute-done((f32[128,512]{1,0:T(8,128)S(1)}, f32[128,512]{1,0:T(8,128)S(1)}, u32[]{:S(2)}, u32[]{:S(2)}) %collective-permute-start.29) | collective-permute-done | bytes 262176 | tf_op jit(solution)/shard_map/ppermute | solution.py:404
  138.4 6.6 %shard_map.165 = (bf16[1024,128]{1,0:T(8,128)(2,1)S(1)}, bf16[1024,128]{1,0:T(8,128)(2,1)S(1)}, bf16[1024,128]{1,0:T(8,128)(2,1)S(1)}, bf16[1024,128]{1,0:T(8,128)(2,1)S(1)}) custom-call(f32[128,512]{1,0:T(8,128)S(1)} %get-tuple-element.32.refs_0_, f32[128,512]{1,0:T(8,128)S(1)} %collective-permute-done.27.refs_1_, ...), custom_call_target="tpu_custom_call" | custom-call | flops 4294967296 | tf_op jit(solution)/shard_map/pallas_call | solution.py:368
  145.9 1.9 %collective-permute-start.32 = (bf16[1024,128]{1,0:T(8,128)(2,1)S(1)}, bf16[1024,128]{1,0:T(8,128)(2,1)S(1)}, u32[]{:S(2)}, u32[]{:S(2)}) collective-permute-start(bf16[1024,128]{1,0:T(8,128)(2,1)S(1)} %get-tuple-element.43), channel_id=1, source_target_pairs={{0,192},{64,0},{128,64},{192,128},{1,193},{65,1},{129,65},{193,129... | collective-permute-start | bytes 786440 | tf_op jit(solution)/shard_map/ppermute | solution.py:404
  148.3 1.8 %collective-permute-start.25 = (bf16[1024,128]{1,0:T(8,128)(2,1)S(1)}, bf16[1024,128]{1,0:T(8,128)(2,1)S(1)}, u32[]{:S(2)}, u32[]{:S(2)}) collective-permute-start(bf16[1024,128]{1,0:T(8,128)(2,1)S(1)} %get-tuple-element.36), channel_id=1, source_target_pairs={{0,128},{64,192},{128,0},{192,64},{1,129},{65,193},{129,1},{193,65... | collective-permute-start | bytes 786440 | tf_op jit(solution)/shard_map/ppermute | solution.py:404
  150.1 8.2 %collective-permute-done.30.refs_5_ = bf16[1024,128]{1,0:T(8,128)(2,1)S(1)} collective-permute-done((bf16[1024,128]{1,0:T(8,128)(2,1)S(1)}, bf16[1024,128]{1,0:T(8,128)(2,1)S(1)}, u32[]{:S(2)}, u32[]{:S(2)}) %collective-permute-start.30) | collective-permute-done | bytes 262176 | tf_op jit(solution)/shard_map/ppermute | solution.py:404
  160.4 10.1 %collective-permute-done.24.refs_1_ = bf16[1024,128]{1,0:T(8,128)(2,1)S(1)} collective-permute-done((bf16[1024,128]{1,0:T(8,128)(2,1)S(1)}, bf16[1024,128]{1,0:T(8,128)(2,1)S(1)}, u32[]{:S(2)}, u32[]{:S(2)}) %collective-permute-start.24) | collective-permute-done | bytes 262176 | tf_op jit(solution)/shard_map/ppermute | solution.py:404
  (80 shorter events, 22.4 us)
Async XLA Ops:
  3.1 13.0 %all-to-all-start = ((bf16[8,128,128]{2,1,0:T(8,128)(2,1)}), bf16[8,128,128]{2,1,0:T(8,128)(2,1)S(1)}, u32[]{:S(2)}, u32[]{:S(2)}) async-start(bf16[8,128,128]{2,1,0:T(8,128)(2,1)} %shard_map.157), calls=%async_computation | async-start | bytes 524288 | tf_op jit(solution)/shard_map/all_to_all | solution.py:422
  19.2 35.5 %all-to-all-start.1 = ((bf16[8,224,128]{2,1,0:T(8,128)(2,1)}), bf16[8,224,128]{2,1,0:T(8,128)(2,1)S(1)}, u32[]{:S(2)}, u32[]{:S(2)}) async-start(bf16[8,224,128]{2,1,0:T(8,128)(2,1)} %shard_map.159), calls=%async_computation.1 | async-start | bytes 917504 | tf_op jit(solution)/shard_map/all_to_all | solution.py:422
  26.9 11.3 %collective-permute-start.10 = (bf16[144,256]{1,0:T(8,128)(2,1)S(1)}, bf16[144,256]{1,0:T(8,128)(2,1)S(1)}, u32[]{:S(2)}, u32[]{:S(2)}) collective-permute-start(bf16[144,256]{1,0:T(8,128)(2,1)S(1)} %shard_map.161.refs_0_), channel_id=1, source_target_pairs={{0,56},{8,0},{16,8},{24,16},{32,24},{40,32},{48,40},{56,48},{1,57}... | collective-permute-start | bytes 221192 | tf_op jit(solution)/shard_map/ppermute | solution.py:404
  29.6 11.6 %collective-permute-start.11 = (bf16[144,256]{1,0:T(8,128)(2,1)S(1)}, bf16[144,256]{1,0:T(8,128)(2,1)S(1)}, u32[]{:S(2)}, u32[]{:S(2)}) collective-permute-start(bf16[144,256]{1,0:T(8,128)(2,1)S(1)} %shard_map.161.refs_0_), channel_id=1, source_target_pairs={{0,48},{8,56},{16,0},{24,8},{32,16},{40,24},{48,32},{56,40},{1,49}... | collective-permute-start | bytes 221192 | tf_op jit(solution)/shard_map/ppermute | solution.py:404
  31.7 13.0 %collective-permute-start.12 = (bf16[144,256]{1,0:T(8,128)(2,1)S(1)}, bf16[144,256]{1,0:T(8,128)(2,1)S(1)}, u32[]{:S(2)}, u32[]{:S(2)}) collective-permute-start(bf16[144,256]{1,0:T(8,128)(2,1)S(1)} %shard_map.161.refs_0_), channel_id=1, source_target_pairs={{0,40},{8,48},{16,56},{24,0},{32,8},{40,16},{48,24},{56,32},{1,41}... | collective-permute-start | bytes 221192 | tf_op jit(solution)/shard_map/ppermute | solution.py:404
  32.9 13.8 %collective-permute-start.13 = (bf16[144,256]{1,0:T(8,128)(2,1)S(1)}, bf16[144,256]{1,0:T(8,128)(2,1)S(1)}, u32[]{:S(2)}, u32[]{:S(2)}) collective-permute-start(bf16[144,256]{1,0:T(8,128)(2,1)S(1)} %shard_map.161.refs_0_), channel_id=1, source_target_pairs={{0,32},{8,40},{16,48},{24,56},{32,0},{40,8},{48,16},{56,24},{1,33}... | collective-permute-start | bytes 221192 | tf_op jit(solution)/shard_map/ppermute | solution.py:404
  36.2 15.4 %collective-permute-start.14 = (bf16[144,256]{1,0:T(8,128)(2,1)S(1)}, bf16[144,256]{1,0:T(8,128)(2,1)S(1)}, u32[]{:S(2)}, u32[]{:S(2)}) collective-permute-start(bf16[144,256]{1,0:T(8,128)(2,1)S(1)} %shard_map.161.refs_0_), channel_id=1, source_target_pairs={{0,24},{8,32},{16,40},{24,48},{32,56},{40,0},{48,8},{56,16},{1,25}... | collective-permute-start | bytes 221192 | tf_op jit(solution)/shard_map/ppermute | solution.py:404
  38.2 13.4 %collective-permute-start.15 = (bf16[144,256]{1,0:T(8,128)(2,1)S(1)}, bf16[144,256]{1,0:T(8,128)(2,1)S(1)}, u32[]{:S(2)}, u32[]{:S(2)}) collective-permute-start(bf16[144,256]{1,0:T(8,128)(2,1)S(1)} %shard_map.161.refs_0_), channel_id=1, source_target_pairs={{0,16},{8,24},{16,32},{24,40},{32,48},{40,56},{48,0},{56,8},{1,17}... | collective-permute-start | bytes 221192 | tf_op jit(solution)/shard_map/ppermute | solution.py:404
  52.5 12.5 %collective-permute-start.17 = (bf16[8,144,256]{2,1,0:T(8,128)(2,1)S(1)}, bf16[8,144,256]{2,1,0:T(8,128)(2,1)S(1)}, u32[]{:S(2)}, u32[]{:S(2)}) collective-permute-start(bf16[8,144,256]{2,1,0:T(8,128)(2,1)S(1)} %shard_map.162.refs_5_), channel_id=1, source_target_pairs={{0,6},{2,0},{4,2},{6,4},{1,7},{3,1},{5,3},{7,5},{8,14},{10,8},{12,... | collective-permute-start | bytes 1769480 | tf_op jit(solution)/shard_map/ppermute | solution.py:404
  53.5 13.8 %collective-permute-start.18 = (bf16[8,144,256]{2,1,0:T(8,128)(2,1)S(1)}, bf16[8,144,256]{2,1,0:T(8,128)(2,1)S(1)}, u32[]{:S(2)}, u32[]{:S(2)}) collective-permute-start(bf16[8,144,256]{2,1,0:T(8,128)(2,1)S(1)} %shard_map.162.refs_5_), channel_id=1, source_target_pairs={{0,4},{2,6},{4,0},{6,2},{1,5},{3,7},{5,1},{7,3},{8,12},{10,14},{12... | collective-permute-start | bytes 1769480 | tf_op jit(solution)/shard_map/ppermute | solution.py:404
  54.7 42.9 %collective-permute-start.19 = (bf16[8,144,256]{2,1,0:T(8,128)(2,1)S(1)}, bf16[8,144,256]{2,1,0:T(8,128)(2,1)S(1)}, u32[]{:S(2)}, u32[]{:S(2)}) collective-permute-start(bf16[8,144,256]{2,1,0:T(8,128)(2,1)S(1)} %shard_map.162.refs_5_), channel_id=1, source_target_pairs={{0,2},{2,4},{4,6},{6,0},{1,3},{3,5},{5,7},{7,1},{8,10},{10,12},{12... | collective-permute-start | bytes 1769480 | tf_op jit(solution)/shard_map/ppermute | solution.py:404
  54.7 30.1 %collective-permute-start = (bf16[8,160,128]{2,1,0:T(8,128)(2,1)S(1)}, bf16[8,160,128]{2,1,0:T(8,128)(2,1)}, u32[]{:S(2)}, u32[]{:S(2)}) collective-permute-start(bf16[8,160,128]{2,1,0:T(8,128)(2,1)S(1)} %slice.9.refs_0_), channel_id=1, source_target_pairs={{0,6},{2,0},{4,2},{6,4},{1,7},{3,1},{5,3},{7,5},{8,14},{10,8},{12,... | collective-permute-start | bytes 983048 | tf_op jit(solution)/shard_map/ppermute | solution.py:404
  57.5 33.6 %collective-permute-start.1 = (bf16[8,160,128]{2,1,0:T(8,128)(2,1)S(1)}, bf16[8,160,128]{2,1,0:T(8,128)(2,1)}, u32[]{:S(2)}, u32[]{:S(2)}) collective-permute-start(bf16[8,160,128]{2,1,0:T(8,128)(2,1)S(1)} %slice.9.refs_0_), channel_id=1, source_target_pairs={{0,4},{2,6},{4,0},{6,2},{1,5},{3,7},{5,1},{7,3},{8,12},{10,14},{12... | collective-permute-start | bytes 983048 | tf_op jit(solution)/shard_map/ppermute | solution.py:404
  65.0 31.9 %collective-permute-start.2 = (bf16[8,160,128]{2,1,0:T(8,128)(2,1)S(1)}, bf16[8,160,128]{2,1,0:T(8,128)(2,1)}, u32[]{:S(2)}, u32[]{:S(2)}) collective-permute-start(bf16[8,160,128]{2,1,0:T(8,128)(2,1)S(1)} %slice.9.refs_0_), channel_id=1, source_target_pairs={{0,2},{2,4},{4,6},{6,0},{1,3},{3,5},{5,7},{7,1},{8,10},{10,12},{12... | collective-permute-start | bytes 983048 | tf_op jit(solution)/shard_map/ppermute | solution.py:404
  67.2 30.4 %collective-permute-start.3 = (bf16[8,160,128]{2,1,0:T(8,128)(2,1)S(1)}, bf16[8,160,128]{2,1,0:T(8,128)(2,1)S(1)}, u32[]{:S(2)}, u32[]{:S(2)}) collective-permute-start(bf16[8,160,128]{2,1,0:T(8,128)(2,1)S(1)} %slice.9.refs_0_), channel_id=1, source_target_pairs={{0,1},{1,0},{2,3},{3,2},{4,5},{5,4},{6,7},{7,6},{8,9},{9,8},{10,11... | collective-permute-start | bytes 983048 | tf_op jit(solution)/shard_map/ppermute | solution.py:404
  84.9 14.9 %collective-permute-start.4 = (bf16[8,160,128]{2,1,0:T(8,128)(2,1)}, bf16[8,160,128]{2,1,0:T(8,128)(2,1)}, u32[]{:S(2)}, u32[]{:S(2)}) collective-permute-start(bf16[8,160,128]{2,1,0:T(8,128)(2,1)} %collective-permute-done.refs_1_), channel_id=1, source_target_pairs={{0,1},{1,0},{2,3},{3,2},{4,5},{5,4},{6,7},{7,6},{8,9},{9,8},{10,11... | collective-permute-start | bytes 983048 | tf_op jit(solution)/shard_map/ppermute | solution.py:404
  97.5 14.3 %collective-permute-start.20 = (bf16[8,144,256]{2,1,0:T(8,128)(2,1)S(1)}, bf16[8,144,256]{2,1,0:T(8,128)(2,1)S(1)}, u32[]{:S(2)}, u32[]{:S(2)}) collective-permute-start(bf16[8,144,256]{2,1,0:T(8,128)(2,1)S(1)} %shard_map.162.refs_5_), channel_id=1, source_target_pairs={{0,1},{1,0},{2,3},{3,2},{4,5},{5,4},{6,7},{7,6},{8,9},{9,8},{10,11... | collective-permute-start | bytes 1769480 | tf_op jit(solution)/shard_map/ppermute | solution.py:404
  98.4 14.0 %collective-permute-start.21 = (bf16[8,144,256]{2,1,0:T(8,128)(2,1)S(1)}, bf16[8,144,256]{2,1,0:T(8,128)(2,1)}, u32[]{:S(2)}, u32[]{:S(2)}) collective-permute-start(bf16[8,144,256]{2,1,0:T(8,128)(2,1)S(1)} %collective-permute-done.17.refs_6_), channel_id=1, source_target_pairs={{0,1},{1,0},{2,3},{3,2},{4,5},{5,4},{6,7},{7,6},{8,9},{9,8},{10,11... | collective-permute-start | bytes 1769480 | tf_op jit(solution)/shard_map/ppermute | solution.py:404
  99.7 20.4 %collective-permute-start.22 = (bf16[8,144,256]{2,1,0:T(8,128)(2,1)S(1)}, bf16[8,144,256]{2,1,0:T(8,128)(2,1)S(1)}, u32[]{:S(2)}, u32[]{:S(2)}) collective-permute-start(bf16[8,144,256]{2,1,0:T(8,128)(2,1)S(1)} %collective-permute-done.18.refs_7_), channel_id=1, source_target_pairs={{0,1},{1,0},{2,3},{3,2},{4,5},{5,4},{6,7},{7,6},{8,9},{9,8},{10,11... | collective-permute-start | bytes 1769480 | tf_op jit(solution)/shard_map/ppermute | solution.py:404
  99.9 22.4 %collective-permute-start.23 = (bf16[8,144,256]{2,1,0:T(8,128)(2,1)S(1)}, bf16[8,144,256]{2,1,0:T(8,128)(2,1)S(1)}, u32[]{:S(2)}, u32[]{:S(2)}) collective-permute-start(bf16[8,144,256]{2,1,0:T(8,128)(2,1)S(1)} %collective-permute-done.19.refs_8_), channel_id=1, source_target_pairs={{0,1},{1,0},{2,3},{3,2},{4,5},{5,4},{6,7},{7,6},{8,9},{9,8},{10,11... | collective-permute-start | bytes 1769480 | tf_op jit(solution)/shard_map/ppermute | solution.py:404
  109.3 14.3 %collective-permute-start.7 = (f32[128,512]{1,0:T(8,128)S(1)}, f32[128,512]{1,0:T(8,128)S(1)}, u32[]{:S(2)}, u32[]{:S(2)}) collective-permute-start(f32[128,512]{1,0:T(8,128)S(1)} %get-tuple-element.26.refs_0_), channel_id=1, source_target_pairs={{0,192},{64,0},{128,64},{192,128},{1,193},{65,1},{129,65},{193,129... | collective-permute-start | bytes 786440 | tf_op jit(solution)/shard_map/ppermute | solution.py:404
  111.8 11.7 %collective-permute-start.8 = (f32[128,512]{1,0:T(8,128)S(1)}, f32[128,512]{1,0:T(8,128)S(1)}, u32[]{:S(2)}, u32[]{:S(2)}) collective-permute-start(f32[128,512]{1,0:T(8,128)S(1)} %get-tuple-element.26.refs_0_), channel_id=1, source_target_pairs={{0,128},{64,192},{128,0},{192,64},{1,129},{65,193},{129,1},{193,65... | collective-permute-start | bytes 786440 | tf_op jit(solution)/shard_map/ppermute | solution.py:404
  112.3 15.5 %collective-permute-start.9 = (f32[128,512]{1,0:T(8,128)S(1)}, f32[128,512]{1,0:T(8,128)S(1)}, u32[]{:S(2)}, u32[]{:S(2)}) collective-permute-start(f32[128,512]{1,0:T(8,128)S(1)} %get-tuple-element.26.refs_0_), channel_id=1, source_target_pairs={{0,64},{64,128},{128,192},{192,0},{1,65},{65,129},{129,193},{193,1... | collective-permute-start | bytes 786440 | tf_op jit(solution)/shard_map/ppermute | solution.py:404
  120.1 14.4 %collective-permute-start.27 = (f32[128,512]{1,0:T(8,128)S(1)}, f32[128,512]{1,0:T(8,128)S(1)}, u32[]{:S(2)}, u32[]{:S(2)}) collective-permute-start(f32[128,512]{1,0:T(8,128)S(1)} %get-tuple-element.32.refs_0_), channel_id=1, source_target_pairs={{0,192},{64,0},{128,64},{192,128},{1,193},{65,1},{129,65},{193,129... | collective-permute-start | bytes 786440 | tf_op jit(solution)/shard_map/ppermute | solution.py:404
  122.3 12.2 %collective-permute-start.28 = (f32[128,512]{1,0:T(8,128)S(1)}, f32[128,512]{1,0:T(8,128)S(1)}, u32[]{:S(2)}, u32[]{:S(2)}) collective-permute-start(f32[128,512]{1,0:T(8,128)S(1)} %get-tuple-element.32.refs_0_), channel_id=1, source_target_pairs={{0,128},{64,192},{128,0},{192,64},{1,129},{65,193},{129,1},{193,65... | collective-permute-start | bytes 786440 | tf_op jit(solution)/shard_map/ppermute | solution.py:404
  123.5 14.8 %collective-permute-start.29 = (f32[128,512]{1,0:T(8,128)S(1)}, f32[128,512]{1,0:T(8,128)S(1)}, u32[]{:S(2)}, u32[]{:S(2)}) collective-permute-start(f32[128,512]{1,0:T(8,128)S(1)} %get-tuple-element.32.refs_0_), channel_id=1, source_target_pairs={{0,64},{64,128},{128,192},{192,0},{1,65},{65,129},{129,193},{193,1... | collective-permute-start | bytes 786440 | tf_op jit(solution)/shard_map/ppermute | solution.py:404
  145.0 13.3 %collective-permute-start.30 = (bf16[1024,128]{1,0:T(8,128)(2,1)S(1)}, bf16[1024,128]{1,0:T(8,128)(2,1)S(1)}, u32[]{:S(2)}, u32[]{:S(2)}) collective-permute-start(bf16[1024,128]{1,0:T(8,128)(2,1)S(1)} %get-tuple-element.41), channel_id=1, source_target_pairs={{0,64},{64,128},{128,192},{192,0},{1,65},{65,129},{129,193},{193,1... | collective-permute-start | bytes 786440 | tf_op jit(solution)/shard_map/ppermute | solution.py:404
  145.1 15.3 %collective-permute-start.31 = (bf16[1024,128]{1,0:T(8,128)(2,1)S(1)}, bf16[1024,128]{1,0:T(8,128)(2,1)S(1)}, u32[]{:S(2)}, u32[]{:S(2)}) collective-permute-start(bf16[1024,128]{1,0:T(8,128)(2,1)S(1)} %get-tuple-element.42), channel_id=1, source_target_pairs={{0,128},{64,192},{128,0},{192,64},{1,129},{65,193},{129,1},{193,65... | collective-permute-start | bytes 786440 | tf_op jit(solution)/shard_map/ppermute | solution.py:404
  145.9 14.5 %collective-permute-start.32 = (bf16[1024,128]{1,0:T(8,128)(2,1)S(1)}, bf16[1024,128]{1,0:T(8,128)(2,1)S(1)}, u32[]{:S(2)}, u32[]{:S(2)}) collective-permute-start(bf16[1024,128]{1,0:T(8,128)(2,1)S(1)} %get-tuple-element.43), channel_id=1, source_target_pairs={{0,192},{64,0},{128,64},{192,128},{1,193},{65,1},{129,65},{193,129... | collective-permute-start | bytes 786440 | tf_op jit(solution)/shard_map/ppermute | solution.py:404
  147.8 22.7 %collective-permute-start.24 = (bf16[1024,128]{1,0:T(8,128)(2,1)S(1)}, bf16[1024,128]{1,0:T(8,128)(2,1)S(1)}, u32[]{:S(2)}, u32[]{:S(2)}) collective-permute-start(bf16[1024,128]{1,0:T(8,128)(2,1)S(1)} %get-tuple-element.35), channel_id=1, source_target_pairs={{0,64},{64,128},{128,192},{192,0},{1,65},{65,129},{129,193},{193,1... | collective-permute-start | bytes 786440 | tf_op jit(solution)/shard_map/ppermute | solution.py:404
  148.3 22.1 %collective-permute-start.25 = (bf16[1024,128]{1,0:T(8,128)(2,1)S(1)}, bf16[1024,128]{1,0:T(8,128)(2,1)S(1)}, u32[]{:S(2)}, u32[]{:S(2)}) collective-permute-start(bf16[1024,128]{1,0:T(8,128)(2,1)S(1)} %get-tuple-element.36), channel_id=1, source_target_pairs={{0,128},{64,192},{128,0},{192,64},{1,129},{65,193},{129,1},{193,65... | collective-permute-start | bytes 786440 | tf_op jit(solution)/shard_map/ppermute | solution.py:404
  158.3 12.6 %collective-permute-start.26 = (bf16[1024,128]{1,0:T(8,128)(2,1)S(1)}, bf16[1024,128]{1,0:T(8,128)(2,1)S(1)}, u32[]{:S(2)}, u32[]{:S(2)}) collective-permute-start(bf16[1024,128]{1,0:T(8,128)(2,1)S(1)} %get-tuple-element.37), channel_id=1, source_target_pairs={{0,192},{64,0},{128,64},{192,128},{1,193},{65,1},{129,65},{193,129... | collective-permute-start | bytes 786440 | tf_op jit(solution)/shard_map/ppermute | solution.py:404
  (17 other events, 373.5 us)

commit v3 on v2

--- a/solution.py
+++ b/solution.py
@@ -339,10 +339,10 @@
 def cross_body(*refs):
     lows = refs[0:4]
     bias = refs[4]
-    tops = refs[5:13]
-    x0_in = refs[13]
-    outs = refs[14:18]
-    x0, weights, crossed, hold, sems = refs[18:]
+    tops = refs[5:15]
+    x0_in = refs[15]
+    outs = refs[16:20]
+    x0, weights, crossed, hold, sems = refs[20:]
     x = lax.axis_index("x")
     waits = load((x0_in,), (x0,), sems)
     low = (lows[0][...] + lows[1][...] + lows[2][...] + lows[3][...]).astype(BF)
@@ -350,13 +350,18 @@
     for i in range(NZ):
         for copy in waits[i]:
             copy.wait()
-        up = jnp.concatenate([t[i, LANE:, :] for t in tops], axis=0)
+        at = i % (NZ // 2)
+        pieces = []
+        for side in (tops[:5], tops[5:]):
+            across = side[3][at] if i < NZ // 2 else side[4][at]
+            pieces += [side[0][i], side[1][i], across, side[2][i]]
+        up = jnp.concatenate([t[LANE:, :] for t in pieces], axis=0)
         gate = lax.dot_general(up, low, (((0,), (0,)), ((), ())), preferred_element_type=F32)
         gate = gate + columns[:, i : i + 1]
         features = x0[i].astype(F32)
         crossed[i * E : (i + 1) * E, :] = (features * gate + features).astype(BF)
         for j in range(8):
-            weights[j * LANE : (j + 1) * LANE, i * E : (i + 1) * E] = tops[j][i, :LANE, :]
+            weights[j * LANE : (j + 1) * LANE, i * E : (i + 1) * E] = pieces[j][:LANE, :]
     part = jnp.dot(weights[...], crossed[...], preferred_element_type=F32).astype(BF)
     for q in range(NX):
         hold[q] = part[:, q * LANE : (q + 1) * LANE]
@@ -366,7 +371,7 @@
 
 def cross(lows, bias, tops, x0):
     return kernel(
-        cross_body, [bf(HID, LANE)] * NX, [VMEM] * 13 + [ANY], [VMEM] * NX,
+        cross_body, [bf(HID, LANE)] * NX, [VMEM] * 15 + [ANY], [VMEM] * NX,
         [pltpu.VMEM((NZ, E, MANY), BF), pltpu.VMEM((HID, NZ * E), BF), pltpu.VMEM((NZ * E, MANY), BF),
          pltpu.VMEM((NX, HID, LANE), BF), pltpu.SemaphoreType.DMA((1, NZ))],
         flops=1 << 32, limit=32,
@@ -411,6 +416,15 @@
     return out
 
 
+def around(v):
+    half = NZ // 2
+    after = shift(v, "y", NY, NY - 1)
+    before = shift(v, "y", NY, 1)
+    first = shift(after[:half], "y", NY, NY - 1)
+    second = shift(before[half:], "y", NY, 1)
+    return [v, after, before, first, second]
+
+
 def deal(parts):
     out = [parts[0]]
     for k in range(1, NX):
@@ -444,21 +458,21 @@
     piece = make_piece(victim, arrived, cache, factors, sent)
     mixed = exchange(piece, "z")
     top = own_weights(dcn_up, mlp_in)
-    new_backing = write_back(resident, victim, cache, backing)
     own = spread(mixed[:, :160, :], "y", NY)
     mixed = mixed[:, 160:, :]
     tops = stacked(spread(tie(top, piece), "z", NZ))
     tables = own + swaps(own)
-    own = spread(tops, "y", NY)
+    own = around(tops)
     tops = own + swaps(own)
     x00, low0, table, factors, new_cache = pool0(mixed, tables)
     lows0 = spread(low0, "x", NX)
-    x01, low1 = pool1(tie(mixed, low0), table, factors)
+    x01, low1 = pool1(tie(mixed, low0, bias), table, factors)
     lows1 = spread(low1, "x", NX)
     h0 = cross(lows0, bias, tops, tie(x00, low1))
     ra = deal(h0)
     h1 = cross(lows1, bias, tops, tie(x01, h0[0]))
     rb = deal(h1)
+    new_backing = write_back(resident, victim, cache, tie(backing, h1[0]))
     scores = score(mlp_bias.reshape(8, LANE), mlp_out.reshape(8, LANE), out_bias, ra, rb)
     return scores[:, None, :], new_cache[None], new_backing[None]
 

time: 173 us -> 173 us (level)
  waiting for transfers between devices: 55.7 us -> 52.4 us
  local copies, waits for them, and re-layouts: 4.31 us -> 7.03 us
    ppermute x33 -> x35, waiting for transfers between devices: 53.1 us -> 49.8 us  [shift(): return lax.ppermute(v, axis, [(i, (i + k) % size) for i in range(size)])]
    unnamed x28 -> x40, local copies, waits for them, and re-layouts: 3.35 us -> 6.04 us
    ppermute x33 -> x35, starting transfers between devices: 57.5 us -> 56.5 us  [shift(): return lax.ppermute(v, axis, [(i, (i + k) % size) for i in range(size)])]
  transfers between devices with their start and end apart: 35 -> 37, of which waited for: 16 -> 14; matrix products, arithmetic and copies ran while one was open for 1% -> 1% of each run, Pallas kernels for 16% -> 16%
where the time goes in v3:
time: 173 us; the launch traced here: 171 us
  starting transfers between devices  70.8 us (41%)
  waiting for transfers between devices  52.4 us (30%)
  Pallas kernels  39.1 us (23%)
  local copies, waits for them, and re-layouts  7.03 us (4%)
    ppermute x35, starting transfers between devices, shift(): return lax.ppermute(v, axis, [(i, (i + k) % size) for i in range(size)])  56.5 us
    ppermute x35, waiting for transfers between devices, shift(): return lax.ppermute(v, axis, [(i, (i + k) % size) for i in range(size)])  49.8 us
    all_to_all x2, starting transfers between devices, exchange(): return lax.all_to_all(v, axis, 0, 0, tiled=True)  14.3 us
    pallas_call x2, Pallas kernels, cross(): kernel(cross_body, [bf(HID, LANE)] * NX, [VMEM] * 15 + [ANY], [VMEM] * NX...  13.5 us
    pallas_call x1, Pallas kernels, pool0(): kernel(pool0_body, [pltpu.HBM((NZ, E, MANY), BF), jax.ShapeDtypeStruct((R...  7.75 us
    pallas_call x1, Pallas kernels, pool1(): kernel(pool1_body, [pltpu.HBM((NZ, E, MANY), BF), jax.ShapeDtypeStruct((R...  7.24 us
    unnamed x40, local copies, waits for them, and re-layouts  6.04 us
    pallas_call x1, Pallas kernels, route_lookups(): kernel(route_body, [bf(NZ, 64, LANE), bf(32, LANE)], [ANY] * 3, [VMEM] *...  3.96 us
  transfers between devices with their start and end apart: 37, of which 14 were waited for; matrix products, arithmetic and copies ran while one was open for 1% of the time, Pallas kernels for 16%

profile of v3, /device:TPU:1, one launch (start us, length us, event | category | flops | bytes accessed | tf_op | source)
XLA Modules:
  0.0 170.8 jit_solution(8108252583455245018)
XLA Ops:
  0.7 2.5 %shard_map.157 = bf16[8,128,128]{2,1,0:T(8,128)(2,1)} custom-call(s32[1,2]{1,0:T(1,128)} %promote_in.1, s32[1,2]{1,0:T(1,128)} %victim.3, bf16[8,128,256]{2,1,0:T(8,128)(2,1)} %bitcast.13), custom_call_target="tpu_custom_call" | custom-call | tf_op jit(solution)/shard_map/pallas_call | solution.py:76
  3.1 6.5 %all-to-all-start = ((bf16[8,128,128]{2,1,0:T(8,128)(2,1)}), bf16[8,128,128]{2,1,0:T(8,128)(2,1)S(1)}, u32[]{:S(2)}, u32[]{:S(2)}) async-start(bf16[8,128,128]{2,1,0:T(8,128)(2,1)} %shard_map.157), calls=%async_computation | async-start | bytes 524288 | tf_op jit(solution)/shard_map/all_to_all | solution.py:436
  9.6 4.0 %shard_map.158 = (bf16[8,64,128]{2,1,0:T(8,128)(2,1)S(1)}, bf16[32,128]{1,0:T(8,128)(2,1)S(1)}) custom-call(s32[2,8,4096]{2,1,0:T(8,128)} %bitcast.20, s32[2,32,128]{2,1,0:T(8,128)} %bitcast.21, bf16[256,128]{1,0:T(8,128)(2,1)} %down_in.1), custom_call_target="tpu_custom_call" | custom-call | flops 4194304 | tf_op jit(solution)/shard_map/pallas_call | solution.py:164
  13.6 2.5 %all-to-all-done.arrived = bf16[8,128,128]{2,1,0:T(8,128)(2,1)S(1)} async-done(((bf16[8,128,128]{2,1,0:T(8,128)(2,1)}), bf16[8,128,128]{2,1,0:T(8,128)(2,1)S(1)}, u32[]{:S(2)}, u32[]{:S(2)}) %all-to-all-start) | async-done | bytes 262176 | tf_op jit(solution)/shard_map/all_to_all | solution.py:436
  19.2 7.7 %all-to-all-start.1 = ((bf16[8,224,128]{2,1,0:T(8,128)(2,1)}), bf16[8,224,128]{2,1,0:T(8,128)(2,1)S(1)}, u32[]{:S(2)}, u32[]{:S(2)}) async-start(bf16[8,224,128]{2,1,0:T(8,128)(2,1)} %shard_map.159), calls=%async_computation.1 | async-start | bytes 917504 | tf_op jit(solution)/shard_map/all_to_all | solution.py:436
  27.0 2.7 %collective-permute-start.10 = (bf16[144,256]{1,0:T(8,128)(2,1)S(1)}, bf16[144,256]{1,0:T(8,128)(2,1)S(1)}, u32[]{:S(2)}, u32[]{:S(2)}) collective-permute-start(bf16[144,256]{1,0:T(8,128)(2,1)S(1)} %shard_map.161.refs_0_), channel_id=1, source_target_pairs={{0,56},{8,0},{16,8},{24,16},{32,24},{40,32},{48,40},{56,48},{1,57}... | collective-permute-start | bytes 221192 | tf_op jit(solution)/shard_map/ppermute | solution.py:409
  29.8 2.1 %collective-permute-start.11 = (bf16[144,256]{1,0:T(8,128)(2,1)S(1)}, bf16[144,256]{1,0:T(8,128)(2,1)S(1)}, u32[]{:S(2)}, u32[]{:S(2)}) collective-permute-start(bf16[144,256]{1,0:T(8,128)(2,1)S(1)} %shard_map.161.refs_0_), channel_id=1, source_target_pairs={{0,48},{8,56},{16,0},{24,8},{32,16},{40,24},{48,32},{56,40},{1,49}... | collective-permute-start | bytes 221192 | tf_op jit(solution)/shard_map/ppermute | solution.py:409
  33.0 3.3 %collective-permute-start.13 = (bf16[144,256]{1,0:T(8,128)(2,1)S(1)}, bf16[144,256]{1,0:T(8,128)(2,1)S(1)}, u32[]{:S(2)}, u32[]{:S(2)}) collective-permute-start(bf16[144,256]{1,0:T(8,128)(2,1)S(1)} %shard_map.161.refs_0_), channel_id=1, source_target_pairs={{0,32},{8,40},{16,48},{24,56},{32,0},{40,8},{48,16},{56,24},{1,33}... | collective-permute-start | bytes 221192 | tf_op jit(solution)/shard_map/ppermute | solution.py:409
  36.3 2.0 %collective-permute-done.10.refs_1_ = bf16[144,256]{1,0:T(8,128)(2,1)S(1)} collective-permute-done((bf16[144,256]{1,0:T(8,128)(2,1)S(1)}, bf16[144,256]{1,0:T(8,128)(2,1)S(1)}, u32[]{:S(2)}, u32[]{:S(2)}) %collective-permute-start.10) | collective-permute-done | bytes 73760 | tf_op jit(solution)/shard_map/ppermute | solution.py:409
  39.6 1.8 %collective-permute-done.11.refs_2_ = bf16[144,256]{1,0:T(8,128)(2,1)S(1)} collective-permute-done((bf16[144,256]{1,0:T(8,128)(2,1)S(1)}, bf16[144,256]{1,0:T(8,128)(2,1)S(1)}, u32[]{:S(2)}, u32[]{:S(2)}) %collective-permute-start.11) | collective-permute-done | bytes 73760 | tf_op jit(solution)/shard_map/ppermute | solution.py:409
  42.2 2.6 %collective-permute-done.12.refs_3_ = bf16[144,256]{1,0:T(8,128)(2,1)S(1)} collective-permute-done((bf16[144,256]{1,0:T(8,128)(2,1)S(1)}, bf16[144,256]{1,0:T(8,128)(2,1)S(1)}, u32[]{:S(2)}, u32[]{:S(2)}) %collective-permute-start.12) | collective-permute-done | bytes 73760 | tf_op jit(solution)/shard_map/ppermute | solution.py:409
  44.8 2.0 %collective-permute-done.13.refs_4_ = bf16[144,256]{1,0:T(8,128)(2,1)S(1)} collective-permute-done((bf16[144,256]{1,0:T(8,128)(2,1)S(1)}, bf16[144,256]{1,0:T(8,128)(2,1)S(1)}, u32[]{:S(2)}, u32[]{:S(2)}) %collective-permute-start.13) | collective-permute-done | bytes 73760 | tf_op jit(solution)/shard_map/ppermute | solution.py:409
  46.8 4.9 %collective-permute-done.14.refs_5_ = bf16[144,256]{1,0:T(8,128)(2,1)S(1)} collective-permute-done((bf16[144,256]{1,0:T(8,128)(2,1)S(1)}, bf16[144,256]{1,0:T(8,128)(2,1)S(1)}, u32[]{:S(2)}, u32[]{:S(2)}) %collective-permute-start.14) | collective-permute-done | bytes 73760 | tf_op jit(solution)/shard_map/ppermute | solution.py:409
  54.2 2.2 %collective-permute-start = (bf16[8,160,128]{2,1,0:T(8,128)(2,1)S(1)}, bf16[8,160,128]{2,1,0:T(8,128)(2,1)S(1)}, u32[]{:S(2)}, u32[]{:S(2)}) collective-permute-start(bf16[8,160,128]{2,1,0:T(8,128)(2,1)S(1)} %slice.17.refs_0_), channel_id=1, source_target_pairs={{0,6},{2,0},{4,2},{6,4},{1,7},{3,1},{5,3},{7,5},{8,14},{10,8},{12,... | collective-permute-start | bytes 983048 | tf_op jit(solution)/shard_map/ppermute | solution.py:409
  56.4 8.8 %collective-permute-done.17.refs_6_ = bf16[8,144,256]{2,1,0:T(8,128)(2,1)S(1)} collective-permute-done((bf16[8,144,256]{2,1,0:T(8,128)(2,1)S(1)}, bf16[8,144,256]{2,1,0:T(8,128)(2,1)S(1)}, u32[]{:S(2)}, u32[]{:S(2)}) %collective-permute-start.17) | collective-permute-done | bytes 589856 | tf_op jit(solution)/shard_map/ppermute | solution.py:409
  65.2 2.2 %collective-permute-start.19 = (bf16[4,144,256]{2,1,0:T(8,128)(2,1)S(1)}, bf16[4,144,256]{2,1,0:T(8,128)(2,1)S(1)}, u32[]{:S(2)}, u32[]{:S(2)}) collective-permute-start(bf16[4,144,256]{2,1,0:T(8,128)(2,1)S(1)} %slice.18), channel_id=1, source_target_pairs={{0,6},{2,0},{4,2},{6,4},{1,7},{3,1},{5,3},{7,5},{8,14},{10,8},{12,... | collective-permute-start | bytes 884744 | tf_op jit(solution)/shard_map/ppermute | solution.py:409
  68.1 6.8 %collective-permute-start.3 = (bf16[8,160,128]{2,1,0:T(8,128)(2,1)S(1)}, bf16[8,160,128]{2,1,0:T(8,128)(2,1)S(1)}, u32[]{:S(2)}, u32[]{:S(2)}) collective-permute-start(bf16[8,160,128]{2,1,0:T(8,128)(2,1)S(1)} %slice.17.refs_0_), channel_id=1, source_target_pairs={{0,1},{1,0},{2,3},{3,2},{4,5},{5,4},{6,7},{7,6},{8,9},{9,8},{10,11... | collective-permute-start | bytes 983048 | tf_op jit(solution)/shard_map/ppermute | solution.py:409
  74.8 3.6 %collective-permute-start.4 = (bf16[8,160,128]{2,1,0:T(8,128)(2,1)S(1)}, bf16[8,160,128]{2,1,0:T(8,128)(2,1)S(1)}, u32[]{:S(2)}, u32[]{:S(2)}) collective-permute-start(bf16[8,160,128]{2,1,0:T(8,128)(2,1)S(1)} %collective-permute-done.refs_1_), channel_id=1, source_target_pairs={{0,1},{1,0},{2,3},{3,2},{4,5},{5,4},{6,7},{7,6},{8,9},{9,8},{10,11... | collective-permute-start | bytes 983048 | tf_op jit(solution)/shard_map/ppermute | solution.py:409
  79.3 10.1 %collective-permute-start.5 = (bf16[8,160,128]{2,1,0:T(8,128)(2,1)}, bf16[8,160,128]{2,1,0:T(8,128)(2,1)}, u32[]{:S(2)}, u32[]{:S(2)}) collective-permute-start(bf16[8,160,128]{2,1,0:T(8,128)(2,1)} %collective-permute-done.1.refs_2_), channel_id=1, source_target_pairs={{0,1},{1,0},{2,3},{3,2},{4,5},{5,4},{6,7},{7,6},{8,9},{9,8},{10,11... | collective-permute-start | bytes 983048 | tf_op jit(solution)/shard_map/ppermute | solution.py:409
  89.5 4.1 %collective-permute-start.21 = (bf16[8,144,256]{2,1,0:T(8,128)(2,1)S(1)}, bf16[8,144,256]{2,1,0:T(8,128)(2,1)S(1)}, u32[]{:S(2)}, u32[]{:S(2)}) collective-permute-start(bf16[8,144,256]{2,1,0:T(8,128)(2,1)S(1)} %shard_map.162.refs_5_), channel_id=1, source_target_pairs={{0,1},{1,0},{2,3},{3,2},{4,5},{5,4},{6,7},{7,6},{8,9},{9,8},{10,11... | collective-permute-start | bytes 1769480 | tf_op jit(solution)/shard_map/ppermute | solution.py:409
  100.1 7.8 %shard_map.160 = (bf16[8,256,512]{2,1,0:T(8,128)(2,1)}, f32[128,512]{1,0:T(8,128)S(1)}, bf16[8,256,512]{2,1,0:T(8,128)(2,1)}, bf16[8,128,256]{2,1,0:T(8,128)(2,1)}, bf16[4,128,256]{2,1,0:T(8,128)(2,1)}) custom-call(bf16[8,64,128]{2,1,0:T(8,128)(2,1)S(1)} %slice.16.lookups, bf16[8,160,128]{2,1,0:T(8,128)(2,1)S(1)} %slice.17.refs_0_, ...), custom_call_target="tpu_custom_call" | custom-call | flops 4294967296 | tf_op jit(solution)/shard_map/pallas_call | solution.py:284
  107.9 2.5 %collective-permute-start.7 = (f32[128,512]{1,0:T(8,128)S(1)}, f32[128,512]{1,0:T(8,128)S(1)}, u32[]{:S(2)}, u32[]{:S(2)}) collective-permute-start(f32[128,512]{1,0:T(8,128)S(1)} %get-tuple-element.27.refs_0_), channel_id=1, source_target_pairs={{0,192},{64,0},{128,64},{192,128},{1,193},{65,1},{129,65},{193,129... | collective-permute-start | bytes 786440 | tf_op jit(solution)/shard_map/ppermute | solution.py:409
  111.6 7.2 %shard_map.163 = (bf16[8,256,512]{2,1,0:T(8,128)(2,1)}, f32[128,512]{1,0:T(8,128)S(1)}) custom-call(bf16[8,64,128]{2,1,0:T(8,128)(2,1)S(1)} %slice.16.lookups, bf16[8,256,512]{2,1,0:T(8,128)(2,1)} %get-tuple-element.31.table_in, bf16[8,128,256]{2,1,0:T(8,128)(2,1)} %get-tuple-element.32.factor_in), custom_call_target="tpu_custom_call" | custom-call | flops 4294967296 | tf_op jit(solution)/shard_map/pallas_call | solution.py:330
  118.8 2.1 %collective-permute-start.29 = (f32[128,512]{1,0:T(8,128)S(1)}, f32[128,512]{1,0:T(8,128)S(1)}, u32[]{:S(2)}, u32[]{:S(2)}) collective-permute-start(f32[128,512]{1,0:T(8,128)S(1)} %get-tuple-element.33.refs_0_), channel_id=1, source_target_pairs={{0,192},{64,0},{128,64},{192,128},{1,193},{65,1},{129,65},{193,129... | collective-permute-start | bytes 786440 | tf_op jit(solution)/shard_map/ppermute | solution.py:409
  122.2 4.1 %collective-permute-done.9.refs_3_ = f32[128,512]{1,0:T(8,128)S(1)} collective-permute-done((f32[128,512]{1,0:T(8,128)S(1)}, f32[128,512]{1,0:T(8,128)S(1)}, u32[]{:S(2)}, u32[]{:S(2)}) %collective-permute-start.9) | collective-permute-done | bytes 262176 | tf_op jit(solution)/shard_map/ppermute | solution.py:409
  126.3 6.7 %shard_map.164 = (bf16[1024,128]{1,0:T(8,128)(2,1)S(1)}, bf16[1024,128]{1,0:T(8,128)(2,1)S(1)}, bf16[1024,128]{1,0:T(8,128)(2,1)S(1)}, bf16[1024,128]{1,0:T(8,128)(2,1)S(1)}) custom-call(f32[128,512]{1,0:T(8,128)S(1)} %get-tuple-element.27.refs_0_, f32[128,512]{1,0:T(8,128)S(1)} %collective-permute-done.7.refs_1_, ...), custom_call_target="tpu_custom_call" | custom-call | flops 4294967296 | tf_op jit(solution)/shard_map/pallas_call | solution.py:373
  133.2 3.8 %collective-permute-done.31.refs_3_ = f32[128,512]{1,0:T(8,128)S(1)} collective-permute-done((f32[128,512]{1,0:T(8,128)S(1)}, f32[128,512]{1,0:T(8,128)S(1)}, u32[]{:S(2)}, u32[]{:S(2)}) %collective-permute-start.31) | collective-permute-done | bytes 262176 | tf_op jit(solution)/shard_map/ppermute | solution.py:409
  137.0 6.7 %shard_map.165 = (bf16[1024,128]{1,0:T(8,128)(2,1)S(1)}, bf16[1024,128]{1,0:T(8,128)(2,1)S(1)}, bf16[1024,128]{1,0:T(8,128)(2,1)S(1)}, bf16[1024,128]{1,0:T(8,128)(2,1)S(1)}) custom-call(f32[128,512]{1,0:T(8,128)S(1)} %get-tuple-element.33.refs_0_, f32[128,512]{1,0:T(8,128)S(1)} %collective-permute-done.29.refs_1_, ...), custom_call_target="tpu_custom_call" | custom-call | flops 4294967296 | tf_op jit(solution)/shard_map/pallas_call | solution.py:373
  144.5 2.0 %collective-permute-start.34 = (bf16[1024,128]{1,0:T(8,128)(2,1)S(1)}, bf16[1024,128]{1,0:T(8,128)(2,1)S(1)}, u32[]{:S(2)}, u32[]{:S(2)}) collective-permute-start(bf16[1024,128]{1,0:T(8,128)(2,1)S(1)} %get-tuple-element.44), channel_id=1, source_target_pairs={{0,192},{64,0},{128,64},{192,128},{1,193},{65,1},{129,65},{193,129... | collective-permute-start | bytes 786440 | tf_op jit(solution)/shard_map/ppermute | solution.py:409
  147.0 1.8 %collective-permute-start.27 = (bf16[1024,128]{1,0:T(8,128)(2,1)S(1)}, bf16[1024,128]{1,0:T(8,128)(2,1)S(1)}, u32[]{:S(2)}, u32[]{:S(2)}) collective-permute-start(bf16[1024,128]{1,0:T(8,128)(2,1)S(1)} %get-tuple-element.37), channel_id=1, source_target_pairs={{0,128},{64,192},{128,0},{192,64},{1,129},{65,193},{129,1},{193,65... | collective-permute-start | bytes 786440 | tf_op jit(solution)/shard_map/ppermute | solution.py:409
  148.8 8.2 %collective-permute-done.32.refs_5_ = bf16[1024,128]{1,0:T(8,128)(2,1)S(1)} collective-permute-done((bf16[1024,128]{1,0:T(8,128)(2,1)S(1)}, bf16[1024,128]{1,0:T(8,128)(2,1)S(1)}, u32[]{:S(2)}, u32[]{:S(2)}) %collective-permute-start.32) | collective-permute-done | bytes 262176 | tf_op jit(solution)/shard_map/ppermute | solution.py:409
  159.1 10.1 %collective-permute-done.26.refs_1_ = bf16[1024,128]{1,0:T(8,128)(2,1)S(1)} collective-permute-done((bf16[1024,128]{1,0:T(8,128)(2,1)S(1)}, bf16[1024,128]{1,0:T(8,128)(2,1)S(1)}, u32[]{:S(2)}, u32[]{:S(2)}) %collective-permute-start.26) | collective-permute-done | bytes 262176 | tf_op jit(solution)/shard_map/ppermute | solution.py:409
  (98 shorter events, 23.8 us)
Async XLA Ops:
  3.1 13.0 %all-to-all-start = ((bf16[8,128,128]{2,1,0:T(8,128)(2,1)}), bf16[8,128,128]{2,1,0:T(8,128)(2,1)S(1)}, u32[]{:S(2)}, u32[]{:S(2)}) async-start(bf16[8,128,128]{2,1,0:T(8,128)(2,1)} %shard_map.157), calls=%async_computation | async-start | bytes 524288 | tf_op jit(solution)/shard_map/all_to_all | solution.py:436
  19.2 35.0 %all-to-all-start.1 = ((bf16[8,224,128]{2,1,0:T(8,128)(2,1)}), bf16[8,224,128]{2,1,0:T(8,128)(2,1)S(1)}, u32[]{:S(2)}, u32[]{:S(2)}) async-start(bf16[8,224,128]{2,1,0:T(8,128)(2,1)} %shard_map.159), calls=%async_computation.1 | async-start | bytes 917504 | tf_op jit(solution)/shard_map/all_to_all | solution.py:436
  31.8 13.0 %collective-permute-start.12 = (bf16[144,256]{1,0:T(8,128)(2,1)S(1)}, bf16[144,256]{1,0:T(8,128)(2,1)S(1)}, u32[]{:S(2)}, u32[]{:S(2)}) collective-permute-start(bf16[144,256]{1,0:T(8,128)(2,1)S(1)} %shard_map.161.refs_0_), channel_id=1, source_target_pairs={{0,40},{8,48},{16,56},{24,0},{32,8},{40,16},{48,24},{56,32},{1,41}... | collective-permute-start | bytes 221192 | tf_op jit(solution)/shard_map/ppermute | solution.py:409
  33.0 13.8 %collective-permute-start.13 = (bf16[144,256]{1,0:T(8,128)(2,1)S(1)}, bf16[144,256]{1,0:T(8,128)(2,1)S(1)}, u32[]{:S(2)}, u32[]{:S(2)}) collective-permute-start(bf16[144,256]{1,0:T(8,128)(2,1)S(1)} %shard_map.161.refs_0_), channel_id=1, source_target_pairs={{0,32},{8,40},{16,48},{24,56},{32,0},{40,8},{48,16},{56,24},{1,33}... | collective-permute-start | bytes 221192 | tf_op jit(solution)/shard_map/ppermute | solution.py:409
  36.3 15.4 %collective-permute-start.14 = (bf16[144,256]{1,0:T(8,128)(2,1)S(1)}, bf16[144,256]{1,0:T(8,128)(2,1)S(1)}, u32[]{:S(2)}, u32[]{:S(2)}) collective-permute-start(bf16[144,256]{1,0:T(8,128)(2,1)S(1)} %shard_map.161.refs_0_), channel_id=1, source_target_pairs={{0,24},{8,32},{16,40},{24,48},{32,56},{40,0},{48,8},{56,16},{1,25}... | collective-permute-start | bytes 221192 | tf_op jit(solution)/shard_map/ppermute | solution.py:409
  38.3 13.4 %collective-permute-start.15 = (bf16[144,256]{1,0:T(8,128)(2,1)S(1)}, bf16[144,256]{1,0:T(8,128)(2,1)S(1)}, u32[]{:S(2)}, u32[]{:S(2)}) collective-permute-start(bf16[144,256]{1,0:T(8,128)(2,1)S(1)} %shard_map.161.refs_0_), channel_id=1, source_target_pairs={{0,16},{8,24},{16,32},{24,40},{32,48},{40,56},{48,0},{56,8},{1,17}... | collective-permute-start | bytes 221192 | tf_op jit(solution)/shard_map/ppermute | solution.py:409
  52.7 12.5 %collective-permute-start.17 = (bf16[8,144,256]{2,1,0:T(8,128)(2,1)S(1)}, bf16[8,144,256]{2,1,0:T(8,128)(2,1)S(1)}, u32[]{:S(2)}, u32[]{:S(2)}) collective-permute-start(bf16[8,144,256]{2,1,0:T(8,128)(2,1)S(1)} %shard_map.162.refs_5_), channel_id=1, source_target_pairs={{0,6},{2,0},{4,2},{6,4},{1,7},{3,1},{5,3},{7,5},{8,14},{10,8},{12,... | collective-permute-start | bytes 1769480 | tf_op jit(solution)/shard_map/ppermute | solution.py:409
  53.6 14.4 %collective-permute-start.18 = (bf16[8,144,256]{2,1,0:T(8,128)(2,1)S(1)}, bf16[8,144,256]{2,1,0:T(8,128)(2,1)S(1)}, u32[]{:S(2)}, u32[]{:S(2)}) collective-permute-start(bf16[8,144,256]{2,1,0:T(8,128)(2,1)S(1)} %shard_map.162.refs_5_), channel_id=1, source_target_pairs={{0,2},{2,4},{4,6},{6,0},{1,3},{3,5},{5,7},{7,1},{8,10},{10,12},{12... | collective-permute-start | bytes 1769480 | tf_op jit(solution)/shard_map/ppermute | solution.py:409
  54.2 20.6 %collective-permute-start = (bf16[8,160,128]{2,1,0:T(8,128)(2,1)S(1)}, bf16[8,160,128]{2,1,0:T(8,128)(2,1)S(1)}, u32[]{:S(2)}, u32[]{:S(2)}) collective-permute-start(bf16[8,160,128]{2,1,0:T(8,128)(2,1)S(1)} %slice.17.refs_0_), channel_id=1, source_target_pairs={{0,6},{2,0},{4,2},{6,4},{1,7},{3,1},{5,3},{7,5},{8,14},{10,8},{12,... | collective-permute-start | bytes 983048 | tf_op jit(solution)/shard_map/ppermute | solution.py:409
  65.2 13.4 %collective-permute-start.19 = (bf16[4,144,256]{2,1,0:T(8,128)(2,1)S(1)}, bf16[4,144,256]{2,1,0:T(8,128)(2,1)S(1)}, u32[]{:S(2)}, u32[]{:S(2)}) collective-permute-start(bf16[4,144,256]{2,1,0:T(8,128)(2,1)S(1)} %slice.18), channel_id=1, source_target_pairs={{0,6},{2,0},{4,2},{6,4},{1,7},{3,1},{5,3},{7,5},{8,14},{10,8},{12,... | collective-permute-start | bytes 884744 | tf_op jit(solution)/shard_map/ppermute | solution.py:409
  67.4 11.9 %collective-permute-start.1 = (bf16[8,160,128]{2,1,0:T(8,128)(2,1)S(1)}, bf16[8,160,128]{2,1,0:T(8,128)(2,1)}, u32[]{:S(2)}, u32[]{:S(2)}) collective-permute-start(bf16[8,160,128]{2,1,0:T(8,128)(2,1)S(1)} %slice.17.refs_0_), channel_id=1, source_target_pairs={{0,4},{2,6},{4,0},{6,2},{1,5},{3,7},{5,1},{7,3},{8,12},{10,14},{12... | collective-permute-start | bytes 983048 | tf_op jit(solution)/shard_map/ppermute | solution.py:409
  67.4 22.0 %collective-permute-start.2 = (bf16[8,160,128]{2,1,0:T(8,128)(2,1)S(1)}, bf16[8,160,128]{2,1,0:T(8,128)(2,1)}, u32[]{:S(2)}, u32[]{:S(2)}) collective-permute-start(bf16[8,160,128]{2,1,0:T(8,128)(2,1)S(1)} %slice.17.refs_0_), channel_id=1, source_target_pairs={{0,2},{2,4},{4,6},{6,0},{1,3},{3,5},{5,7},{7,1},{8,10},{10,12},{12... | collective-permute-start | bytes 983048 | tf_op jit(solution)/shard_map/ppermute | solution.py:409
  68.1 25.6 %collective-permute-start.3 = (bf16[8,160,128]{2,1,0:T(8,128)(2,1)S(1)}, bf16[8,160,128]{2,1,0:T(8,128)(2,1)S(1)}, u32[]{:S(2)}, u32[]{:S(2)}) collective-permute-start(bf16[8,160,128]{2,1,0:T(8,128)(2,1)S(1)} %slice.17.refs_0_), channel_id=1, source_target_pairs={{0,1},{1,0},{2,3},{3,2},{4,5},{5,4},{6,7},{7,6},{8,9},{9,8},{10,11... | collective-permute-start | bytes 983048 | tf_op jit(solution)/shard_map/ppermute | solution.py:409
  74.8 19.6 %collective-permute-start.4 = (bf16[8,160,128]{2,1,0:T(8,128)(2,1)S(1)}, bf16[8,160,128]{2,1,0:T(8,128)(2,1)S(1)}, u32[]{:S(2)}, u32[]{:S(2)}) collective-permute-start(bf16[8,160,128]{2,1,0:T(8,128)(2,1)S(1)} %collective-permute-done.refs_1_), channel_id=1, source_target_pairs={{0,1},{1,0},{2,3},{3,2},{4,5},{5,4},{6,7},{7,6},{8,9},{9,8},{10,11... | collective-permute-start | bytes 983048 | tf_op jit(solution)/shard_map/ppermute | solution.py:409
  79.3 17.3 %collective-permute-start.5 = (bf16[8,160,128]{2,1,0:T(8,128)(2,1)}, bf16[8,160,128]{2,1,0:T(8,128)(2,1)}, u32[]{:S(2)}, u32[]{:S(2)}) collective-permute-start(bf16[8,160,128]{2,1,0:T(8,128)(2,1)} %collective-permute-done.1.refs_2_), channel_id=1, source_target_pairs={{0,1},{1,0},{2,3},{3,2},{4,5},{5,4},{6,7},{7,6},{8,9},{9,8},{10,11... | collective-permute-start | bytes 983048 | tf_op jit(solution)/shard_map/ppermute | solution.py:409
  89.5 18.4 %collective-permute-start.21 = (bf16[8,144,256]{2,1,0:T(8,128)(2,1)S(1)}, bf16[8,144,256]{2,1,0:T(8,128)(2,1)S(1)}, u32[]{:S(2)}, u32[]{:S(2)}) collective-permute-start(bf16[8,144,256]{2,1,0:T(8,128)(2,1)S(1)} %shard_map.162.refs_5_), channel_id=1, source_target_pairs={{0,1},{1,0},{2,3},{3,2},{4,5},{5,4},{6,7},{7,6},{8,9},{9,8},{10,11... | collective-permute-start | bytes 1769480 | tf_op jit(solution)/shard_map/ppermute | solution.py:409
  94.4 16.0 %collective-permute-start.22 = (bf16[8,144,256]{2,1,0:T(8,128)(2,1)S(1)}, bf16[8,144,256]{2,1,0:T(8,128)(2,1)S(1)}, u32[]{:S(2)}, u32[]{:S(2)}) collective-permute-start(bf16[8,144,256]{2,1,0:T(8,128)(2,1)S(1)} %collective-permute-done.17.refs_6_), channel_id=1, source_target_pairs={{0,1},{1,0},{2,3},{3,2},{4,5},{5,4},{6,7},{7,6},{8,9},{9,8},{10,11... | collective-permute-start | bytes 1769480 | tf_op jit(solution)/shard_map/ppermute | solution.py:409
  95.1 15.8 %collective-permute-start.23 = (bf16[8,144,256]{2,1,0:T(8,128)(2,1)S(1)}, bf16[8,144,256]{2,1,0:T(8,128)(2,1)}, u32[]{:S(2)}, u32[]{:S(2)}) collective-permute-start(bf16[8,144,256]{2,1,0:T(8,128)(2,1)S(1)} %collective-permute-done.18.refs_7_), channel_id=1, source_target_pairs={{0,1},{1,0},{2,3},{3,2},{4,5},{5,4},{6,7},{7,6},{8,9},{9,8},{10,11... | collective-permute-start | bytes 1769480 | tf_op jit(solution)/shard_map/ppermute | solution.py:409
  96.6 22.2 %collective-permute-start.24 = (bf16[4,144,256]{2,1,0:T(8,128)(2,1)}, bf16[4,144,256]{2,1,0:T(8,128)(2,1)S(1)}, u32[]{:S(2)}, u32[]{:S(2)}) collective-permute-start(bf16[4,144,256]{2,1,0:T(8,128)(2,1)} %copy-done.16), channel_id=1, source_target_pairs={{0,1},{1,0},{2,3},{3,2},{4,5},{5,4},{6,7},{7,6},{8,9},{9,8},{10,11... | collective-permute-start | bytes 884744 | tf_op jit(solution)/shard_map/ppermute | solution.py:409
  96.7 24.3 %collective-permute-start.25 = (bf16[4,144,256]{2,1,0:T(8,128)(2,1)}, bf16[4,144,256]{2,1,0:T(8,128)(2,1)S(1)}, u32[]{:S(2)}, u32[]{:S(2)}) collective-permute-start(bf16[4,144,256]{2,1,0:T(8,128)(2,1)} %collective-permute-done.20.refs_9_), channel_id=1, source_target_pairs={{0,1},{1,0},{2,3},{3,2},{4,5},{5,4},{6,7},{7,6},{8,9},{9,8},{10,11... | collective-permute-start | bytes 884744 | tf_op jit(solution)/shard_map/ppermute | solution.py:409
  107.9 14.3 %collective-permute-start.7 = (f32[128,512]{1,0:T(8,128)S(1)}, f32[128,512]{1,0:T(8,128)S(1)}, u32[]{:S(2)}, u32[]{:S(2)}) collective-permute-start(f32[128,512]{1,0:T(8,128)S(1)} %get-tuple-element.27.refs_0_), channel_id=1, source_target_pairs={{0,192},{64,0},{128,64},{192,128},{1,193},{65,1},{129,65},{193,129... | collective-permute-start | bytes 786440 | tf_op jit(solution)/shard_map/ppermute | solution.py:409
  110.4 11.8 %collective-permute-start.8 = (f32[128,512]{1,0:T(8,128)S(1)}, f32[128,512]{1,0:T(8,128)S(1)}, u32[]{:S(2)}, u32[]{:S(2)}) collective-permute-start(f32[128,512]{1,0:T(8,128)S(1)} %get-tuple-element.27.refs_0_), channel_id=1, source_target_pairs={{0,128},{64,192},{128,0},{192,64},{1,129},{65,193},{129,1},{193,65... | collective-permute-start | bytes 786440 | tf_op jit(solution)/shard_map/ppermute | solution.py:409
  111.0 15.4 %collective-permute-start.9 = (f32[128,512]{1,0:T(8,128)S(1)}, f32[128,512]{1,0:T(8,128)S(1)}, u32[]{:S(2)}, u32[]{:S(2)}) collective-permute-start(f32[128,512]{1,0:T(8,128)S(1)} %get-tuple-element.27.refs_0_), channel_id=1, source_target_pairs={{0,64},{64,128},{128,192},{192,0},{1,65},{65,129},{129,193},{193,1... | collective-permute-start | bytes 786440 | tf_op jit(solution)/shard_map/ppermute | solution.py:409
  118.8 14.3 %collective-permute-start.29 = (f32[128,512]{1,0:T(8,128)S(1)}, f32[128,512]{1,0:T(8,128)S(1)}, u32[]{:S(2)}, u32[]{:S(2)}) collective-permute-start(f32[128,512]{1,0:T(8,128)S(1)} %get-tuple-element.33.refs_0_), channel_id=1, source_target_pairs={{0,192},{64,0},{128,64},{192,128},{1,193},{65,1},{129,65},{193,129... | collective-permute-start | bytes 786440 | tf_op jit(solution)/shard_map/ppermute | solution.py:409
  121.0 12.2 %collective-permute-start.30 = (f32[128,512]{1,0:T(8,128)S(1)}, f32[128,512]{1,0:T(8,128)S(1)}, u32[]{:S(2)}, u32[]{:S(2)}) collective-permute-start(f32[128,512]{1,0:T(8,128)S(1)} %get-tuple-element.33.refs_0_), channel_id=1, source_target_pairs={{0,128},{64,192},{128,0},{192,64},{1,129},{65,193},{129,1},{193,65... | collective-permute-start | bytes 786440 | tf_op jit(solution)/shard_map/ppermute | solution.py:409
  122.2 14.8 %collective-permute-start.31 = (f32[128,512]{1,0:T(8,128)S(1)}, f32[128,512]{1,0:T(8,128)S(1)}, u32[]{:S(2)}, u32[]{:S(2)}) collective-permute-start(f32[128,512]{1,0:T(8,128)S(1)} %get-tuple-element.33.refs_0_), channel_id=1, source_target_pairs={{0,64},{64,128},{128,192},{192,0},{1,65},{65,129},{129,193},{193,1... | collective-permute-start | bytes 786440 | tf_op jit(solution)/shard_map/ppermute | solution.py:409
  143.7 13.3 %collective-permute-start.32 = (bf16[1024,128]{1,0:T(8,128)(2,1)S(1)}, bf16[1024,128]{1,0:T(8,128)(2,1)S(1)}, u32[]{:S(2)}, u32[]{:S(2)}) collective-permute-start(bf16[1024,128]{1,0:T(8,128)(2,1)S(1)} %get-tuple-element.42), channel_id=1, source_target_pairs={{0,64},{64,128},{128,192},{192,0},{1,65},{65,129},{129,193},{193,1... | collective-permute-start | bytes 786440 | tf_op jit(solution)/shard_map/ppermute | solution.py:409
  143.8 15.3 %collective-permute-start.33 = (bf16[1024,128]{1,0:T(8,128)(2,1)S(1)}, bf16[1024,128]{1,0:T(8,128)(2,1)S(1)}, u32[]{:S(2)}, u32[]{:S(2)}) collective-permute-start(bf16[1024,128]{1,0:T(8,128)(2,1)S(1)} %get-tuple-element.43), channel_id=1, source_target_pairs={{0,128},{64,192},{128,0},{192,64},{1,129},{65,193},{129,1},{193,65... | collective-permute-start | bytes 786440 | tf_op jit(solution)/shard_map/ppermute | solution.py:409
  144.5 14.6 %collective-permute-start.34 = (bf16[1024,128]{1,0:T(8,128)(2,1)S(1)}, bf16[1024,128]{1,0:T(8,128)(2,1)S(1)}, u32[]{:S(2)}, u32[]{:S(2)}) collective-permute-start(bf16[1024,128]{1,0:T(8,128)(2,1)S(1)} %get-tuple-element.44), channel_id=1, source_target_pairs={{0,192},{64,0},{128,64},{192,128},{1,193},{65,1},{129,65},{193,129... | collective-permute-start | bytes 786440 | tf_op jit(solution)/shard_map/ppermute | solution.py:409
  146.5 22.7 %collective-permute-start.26 = (bf16[1024,128]{1,0:T(8,128)(2,1)S(1)}, bf16[1024,128]{1,0:T(8,128)(2,1)S(1)}, u32[]{:S(2)}, u32[]{:S(2)}) collective-permute-start(bf16[1024,128]{1,0:T(8,128)(2,1)S(1)} %get-tuple-element.36), channel_id=1, source_target_pairs={{0,64},{64,128},{128,192},{192,0},{1,65},{65,129},{129,193},{193,1... | collective-permute-start | bytes 786440 | tf_op jit(solution)/shard_map/ppermute | solution.py:409
  147.0 22.1 %collective-permute-start.27 = (bf16[1024,128]{1,0:T(8,128)(2,1)S(1)}, bf16[1024,128]{1,0:T(8,128)(2,1)S(1)}, u32[]{:S(2)}, u32[]{:S(2)}) collective-permute-start(bf16[1024,128]{1,0:T(8,128)(2,1)S(1)} %get-tuple-element.37), channel_id=1, source_target_pairs={{0,128},{64,192},{128,0},{192,64},{1,129},{65,193},{129,1},{193,65... | collective-permute-start | bytes 786440 | tf_op jit(solution)/shard_map/ppermute | solution.py:409
  157.0 12.6 %collective-permute-start.28 = (bf16[1024,128]{1,0:T(8,128)(2,1)S(1)}, bf16[1024,128]{1,0:T(8,128)(2,1)S(1)}, u32[]{:S(2)}, u32[]{:S(2)}) collective-permute-start(bf16[1024,128]{1,0:T(8,128)(2,1)S(1)} %get-tuple-element.38), channel_id=1, source_target_pairs={{0,192},{64,0},{128,64},{192,128},{1,193},{65,1},{129,65},{193,129... | collective-permute-start | bytes 786440 | tf_op jit(solution)/shard_map/ppermute | solution.py:409
  (25 other events, 443.2 us)

commit v4 on v3

--- a/solution.py
+++ b/solution.py
@@ -80,13 +80,21 @@
     )(*far(promote, victim, backing))
 
 
-def piece_body(victim, arrived, cache, factors, sent, out):
+def piece_body(victim_in, cache_in, arrived, factors, sent, out, victim, cache, sems):
     s = lax.axis_index("y")
     c = lax.axis_index("c")
+    copies = [
+        pltpu.make_async_copy(victim_in, victim, sems.at[0]),
+        pltpu.make_async_copy(cache_in.at[s], cache, sems.at[1]),
+    ]
+    for copy in copies:
+        copy.start()
     total = arrived[0]
     for i in range(1, NY * NC):
         total = total + arrived[i]
-    block = cache[s]
+    for copy in copies:
+        copy.wait()
+    block = cache[...]
     kept = jnp.where(c == 0, block[:, :LANE], block[:, LANE:])
     evicted = (victim[0, 0] == s) | (victim[0, 1] == s)
     piece = jnp.where(evicted, total, kept).T
@@ -98,8 +106,9 @@
 
 def make_piece(victim, arrived, cache, factors, sent):
     return kernel(
-        piece_body, bf(NZ, 224, BLOCK), [SMEM] + [VMEM] * 4, VMEM
-    )(victim, *near(arrived, cache, factors, sent))
+        piece_body, bf(NZ, 224, BLOCK), [ANY] * 2 + [VMEM] * 3, VMEM,
+        [pltpu.SMEM((1, 2), jnp.int32), pltpu.VMEM((BLOCK, E), BF), pltpu.SemaphoreType.DMA((2,))],
+    )(*far(victim, cache), *near(arrived, factors, sent))
 
 
 def back_body(resident, victim, cache, backing, out):

time: 173 us -> 171 us (0.988)
    unnamed x40 -> x36, local copies, waits for them, and re-layouts: 6.04 us -> 4.45 us
where the time goes in v4:
time: 171 us; the launch traced here: 169 us
  starting transfers between devices  70.7 us (41%)
  waiting for transfers between devices  52.3 us (31%)
  Pallas kernels  39.3 us (23%)
  local copies, waits for them, and re-layouts  5.44 us (3%)
    ppermute x35, starting transfers between devices, shift(): return lax.ppermute(v, axis, [(i, (i + k) % size) for i in range(size)])  56.6 us
    ppermute x35, waiting for transfers between devices, shift(): return lax.ppermute(v, axis, [(i, (i + k) % size) for i in range(size)])  49.8 us
    all_to_all x2, starting transfers between devices, exchange(): return lax.all_to_all(v, axis, 0, 0, tiled=True)  14.1 us
    pallas_call x2, Pallas kernels, cross(): kernel(cross_body, [bf(HID, LANE)] * NX, [VMEM] * 15 + [ANY], [VMEM] * NX...  13.5 us
    pallas_call x1, Pallas kernels, pool0(): kernel(pool0_body, [pltpu.HBM((NZ, E, MANY), BF), jax.ShapeDtypeStruct((R...  7.72 us
    pallas_call x1, Pallas kernels, pool1(): kernel(pool1_body, [pltpu.HBM((NZ, E, MANY), BF), jax.ShapeDtypeStruct((R...  7.23 us
    unnamed x36, local copies, waits for them, and re-layouts  4.45 us
    pallas_call x1, Pallas kernels, route_lookups(): kernel(route_body, [bf(NZ, 64, LANE), bf(32, LANE)], [ANY] * 3, [VMEM] *...  3.96 us
  transfers between devices with their start and end apart: 37, of which 14 were waited for; matrix products, arithmetic and copies ran while one was open for 1% of the time, Pallas kernels for 16%

profile of v4, /device:TPU:1, one launch (start us, length us, event | category | flops | bytes accessed | tf_op | source)
XLA Modules:
  0.0 169.5 jit_solution(3483738763782257962)
XLA Ops:
  0.7 2.5 %shard_map.157 = bf16[8,128,128]{2,1,0:T(8,128)(2,1)} custom-call(s32[1,2]{1,0:T(1,128)} %promote_in.1, s32[1,2]{1,0:T(1,128)} %victim.1, bf16[8,128,256]{2,1,0:T(8,128)(2,1)} %bitcast.13), custom_call_target="tpu_custom_call" | custom-call | tf_op jit(solution)/shard_map/pallas_call | solution.py:76
  3.1 6.5 %all-to-all-start = ((bf16[8,128,128]{2,1,0:T(8,128)(2,1)}), bf16[8,128,128]{2,1,0:T(8,128)(2,1)S(1)}, u32[]{:S(2)}, u32[]{:S(2)}) async-start(bf16[8,128,128]{2,1,0:T(8,128)(2,1)} %shard_map.157), calls=%async_computation | async-start | bytes 524288 | tf_op jit(solution)/shard_map/all_to_all | solution.py:445
  9.6 4.0 %shard_map.158 = (bf16[8,64,128]{2,1,0:T(8,128)(2,1)S(1)}, bf16[32,128]{1,0:T(8,128)(2,1)S(1)}) custom-call(s32[2,8,4096]{2,1,0:T(8,128)} %bitcast.20, s32[2,32,128]{2,1,0:T(8,128)} %bitcast.21, bf16[256,128]{1,0:T(8,128)(2,1)} %down_in.1), custom_call_target="tpu_custom_call" | custom-call | flops 4194304 | tf_op jit(solution)/shard_map/pallas_call | solution.py:173
  13.6 2.5 %all-to-all-done.arrived = bf16[8,128,128]{2,1,0:T(8,128)(2,1)S(1)} async-done(((bf16[8,128,128]{2,1,0:T(8,128)(2,1)}), bf16[8,128,128]{2,1,0:T(8,128)(2,1)S(1)}, u32[]{:S(2)}, u32[]{:S(2)}) %all-to-all-start) | async-done | bytes 262176 | tf_op jit(solution)/shard_map/all_to_all | solution.py:445
  17.9 7.6 %all-to-all-start.1 = ((bf16[8,224,128]{2,1,0:T(8,128)(2,1)}), bf16[8,224,128]{2,1,0:T(8,128)(2,1)S(1)}, u32[]{:S(2)}, u32[]{:S(2)}) async-start(bf16[8,224,128]{2,1,0:T(8,128)(2,1)} %shard_map.159), calls=%async_computation.1 | async-start | bytes 917504 | tf_op jit(solution)/shard_map/all_to_all | solution.py:445
  25.6 2.7 %collective-permute-start.10 = (bf16[144,256]{1,0:T(8,128)(2,1)S(1)}, bf16[144,256]{1,0:T(8,128)(2,1)S(1)}, u32[]{:S(2)}, u32[]{:S(2)}) collective-permute-start(bf16[144,256]{1,0:T(8,128)(2,1)S(1)} %shard_map.161.refs_0_), channel_id=1, source_target_pairs={{0,56},{8,0},{16,8},{24,16},{32,24},{40,32},{48,40},{56,48},{1,57}... | collective-permute-start | bytes 221192 | tf_op jit(solution)/shard_map/ppermute | solution.py:418
  28.4 2.1 %collective-permute-start.11 = (bf16[144,256]{1,0:T(8,128)(2,1)S(1)}, bf16[144,256]{1,0:T(8,128)(2,1)S(1)}, u32[]{:S(2)}, u32[]{:S(2)}) collective-permute-start(bf16[144,256]{1,0:T(8,128)(2,1)S(1)} %shard_map.161.refs_0_), channel_id=1, source_target_pairs={{0,48},{8,56},{16,0},{24,8},{32,16},{40,24},{48,32},{56,40},{1,49}... | collective-permute-start | bytes 221192 | tf_op jit(solution)/shard_map/ppermute | solution.py:418
  31.6 3.3 %collective-permute-start.13 = (bf16[144,256]{1,0:T(8,128)(2,1)S(1)}, bf16[144,256]{1,0:T(8,128)(2,1)S(1)}, u32[]{:S(2)}, u32[]{:S(2)}) collective-permute-start(bf16[144,256]{1,0:T(8,128)(2,1)S(1)} %shard_map.161.refs_0_), channel_id=1, source_target_pairs={{0,32},{8,40},{16,48},{24,56},{32,0},{40,8},{48,16},{56,24},{1,33}... | collective-permute-start | bytes 221192 | tf_op jit(solution)/shard_map/ppermute | solution.py:418
  34.9 2.0 %collective-permute-done.10.refs_1_ = bf16[144,256]{1,0:T(8,128)(2,1)S(1)} collective-permute-done((bf16[144,256]{1,0:T(8,128)(2,1)S(1)}, bf16[144,256]{1,0:T(8,128)(2,1)S(1)}, u32[]{:S(2)}, u32[]{:S(2)}) %collective-permute-start.10) | collective-permute-done | bytes 73760 | tf_op jit(solution)/shard_map/ppermute | solution.py:418
  38.2 1.8 %collective-permute-done.11.refs_2_ = bf16[144,256]{1,0:T(8,128)(2,1)S(1)} collective-permute-done((bf16[144,256]{1,0:T(8,128)(2,1)S(1)}, bf16[144,256]{1,0:T(8,128)(2,1)S(1)}, u32[]{:S(2)}, u32[]{:S(2)}) %collective-permute-start.11) | collective-permute-done | bytes 73760 | tf_op jit(solution)/shard_map/ppermute | solution.py:418
  40.8 2.6 %collective-permute-done.12.refs_3_ = bf16[144,256]{1,0:T(8,128)(2,1)S(1)} collective-permute-done((bf16[144,256]{1,0:T(8,128)(2,1)S(1)}, bf16[144,256]{1,0:T(8,128)(2,1)S(1)}, u32[]{:S(2)}, u32[]{:S(2)}) %collective-permute-start.12) | collective-permute-done | bytes 73760 | tf_op jit(solution)/shard_map/ppermute | solution.py:418
  43.4 2.0 %collective-permute-done.13.refs_4_ = bf16[144,256]{1,0:T(8,128)(2,1)S(1)} collective-permute-done((bf16[144,256]{1,0:T(8,128)(2,1)S(1)}, bf16[144,256]{1,0:T(8,128)(2,1)S(1)}, u32[]{:S(2)}, u32[]{:S(2)}) %collective-permute-start.13) | collective-permute-done | bytes 73760 | tf_op jit(solution)/shard_map/ppermute | solution.py:418
  45.4 4.9 %collective-permute-done.14.refs_5_ = bf16[144,256]{1,0:T(8,128)(2,1)S(1)} collective-permute-done((bf16[144,256]{1,0:T(8,128)(2,1)S(1)}, bf16[144,256]{1,0:T(8,128)(2,1)S(1)}, u32[]{:S(2)}, u32[]{:S(2)}) %collective-permute-start.14) | collective-permute-done | bytes 73760 | tf_op jit(solution)/shard_map/ppermute | solution.py:418
  52.8 2.2 %collective-permute-start = (bf16[8,160,128]{2,1,0:T(8,128)(2,1)S(1)}, bf16[8,160,128]{2,1,0:T(8,128)(2,1)S(1)}, u32[]{:S(2)}, u32[]{:S(2)}) collective-permute-start(bf16[8,160,128]{2,1,0:T(8,128)(2,1)S(1)} %slice.17.refs_0_), channel_id=1, source_target_pairs={{0,6},{2,0},{4,2},{6,4},{1,7},{3,1},{5,3},{7,5},{8,14},{10,8},{12,... | collective-permute-start | bytes 983048 | tf_op jit(solution)/shard_map/ppermute | solution.py:418
  55.0 8.8 %collective-permute-done.17.refs_6_ = bf16[8,144,256]{2,1,0:T(8,128)(2,1)S(1)} collective-permute-done((bf16[8,144,256]{2,1,0:T(8,128)(2,1)S(1)}, bf16[8,144,256]{2,1,0:T(8,128)(2,1)S(1)}, u32[]{:S(2)}, u32[]{:S(2)}) %collective-permute-start.17) | collective-permute-done | bytes 589856 | tf_op jit(solution)/shard_map/ppermute | solution.py:418
  63.8 2.2 %collective-permute-start.19 = (bf16[4,144,256]{2,1,0:T(8,128)(2,1)S(1)}, bf16[4,144,256]{2,1,0:T(8,128)(2,1)S(1)}, u32[]{:S(2)}, u32[]{:S(2)}) collective-permute-start(bf16[4,144,256]{2,1,0:T(8,128)(2,1)S(1)} %slice.18), channel_id=1, source_target_pairs={{0,6},{2,0},{4,2},{6,4},{1,7},{3,1},{5,3},{7,5},{8,14},{10,8},{12,... | collective-permute-start | bytes 884744 | tf_op jit(solution)/shard_map/ppermute | solution.py:418
  66.7 6.8 %collective-permute-start.3 = (bf16[8,160,128]{2,1,0:T(8,128)(2,1)S(1)}, bf16[8,160,128]{2,1,0:T(8,128)(2,1)S(1)}, u32[]{:S(2)}, u32[]{:S(2)}) collective-permute-start(bf16[8,160,128]{2,1,0:T(8,128)(2,1)S(1)} %slice.17.refs_0_), channel_id=1, source_target_pairs={{0,1},{1,0},{2,3},{3,2},{4,5},{5,4},{6,7},{7,6},{8,9},{9,8},{10,11... | collective-permute-start | bytes 983048 | tf_op jit(solution)/shard_map/ppermute | solution.py:418
  73.4 3.6 %collective-permute-start.4 = (bf16[8,160,128]{2,1,0:T(8,128)(2,1)S(1)}, bf16[8,160,128]{2,1,0:T(8,128)(2,1)S(1)}, u32[]{:S(2)}, u32[]{:S(2)}) collective-permute-start(bf16[8,160,128]{2,1,0:T(8,128)(2,1)S(1)} %collective-permute-done.refs_1_), channel_id=1, source_target_pairs={{0,1},{1,0},{2,3},{3,2},{4,5},{5,4},{6,7},{7,6},{8,9},{9,8},{10,11... | collective-permute-start | bytes 983048 | tf_op jit(solution)/shard_map/ppermute | solution.py:418
  77.9 10.1 %collective-permute-start.5 = (bf16[8,160,128]{2,1,0:T(8,128)(2,1)}, bf16[8,160,128]{2,1,0:T(8,128)(2,1)}, u32[]{:S(2)}, u32[]{:S(2)}) collective-permute-start(bf16[8,160,128]{2,1,0:T(8,128)(2,1)} %collective-permute-done.1.refs_2_), channel_id=1, source_target_pairs={{0,1},{1,0},{2,3},{3,2},{4,5},{5,4},{6,7},{7,6},{8,9},{9,8},{10,11... | collective-permute-start | bytes 983048 | tf_op jit(solution)/shard_map/ppermute | solution.py:418
  88.1 4.1 %collective-permute-start.21 = (bf16[8,144,256]{2,1,0:T(8,128)(2,1)S(1)}, bf16[8,144,256]{2,1,0:T(8,128)(2,1)S(1)}, u32[]{:S(2)}, u32[]{:S(2)}) collective-permute-start(bf16[8,144,256]{2,1,0:T(8,128)(2,1)S(1)} %shard_map.162.refs_5_), channel_id=1, source_target_pairs={{0,1},{1,0},{2,3},{3,2},{4,5},{5,4},{6,7},{7,6},{8,9},{9,8},{10,11... | collective-permute-start | bytes 1769480 | tf_op jit(solution)/shard_map/ppermute | solution.py:418
  98.7 7.7 %shard_map.160 = (bf16[8,256,512]{2,1,0:T(8,128)(2,1)}, f32[128,512]{1,0:T(8,128)S(1)}, bf16[8,256,512]{2,1,0:T(8,128)(2,1)}, bf16[8,128,256]{2,1,0:T(8,128)(2,1)}, bf16[4,128,256]{2,1,0:T(8,128)(2,1)}) custom-call(bf16[8,64,128]{2,1,0:T(8,128)(2,1)S(1)} %slice.16.lookups, bf16[8,160,128]{2,1,0:T(8,128)(2,1)S(1)} %slice.17.refs_0_, ...), custom_call_target="tpu_custom_call" | custom-call | flops 4294967296 | tf_op jit(solution)/shard_map/pallas_call | solution.py:293
  106.5 2.6 %collective-permute-start.7 = (f32[128,512]{1,0:T(8,128)S(1)}, f32[128,512]{1,0:T(8,128)S(1)}, u32[]{:S(2)}, u32[]{:S(2)}) collective-permute-start(f32[128,512]{1,0:T(8,128)S(1)} %get-tuple-element.27.refs_0_), channel_id=1, source_target_pairs={{0,192},{64,0},{128,64},{192,128},{1,193},{65,1},{129,65},{193,129... | collective-permute-start | bytes 786440 | tf_op jit(solution)/shard_map/ppermute | solution.py:418
  110.2 7.2 %shard_map.163 = (bf16[8,256,512]{2,1,0:T(8,128)(2,1)}, f32[128,512]{1,0:T(8,128)S(1)}) custom-call(bf16[8,64,128]{2,1,0:T(8,128)(2,1)S(1)} %slice.16.lookups, bf16[8,256,512]{2,1,0:T(8,128)(2,1)} %get-tuple-element.31.table_in, bf16[8,128,256]{2,1,0:T(8,128)(2,1)} %get-tuple-element.32.factor_in), custom_call_target="tpu_custom_call" | custom-call | flops 4294967296 | tf_op jit(solution)/shard_map/pallas_call | solution.py:339
  117.4 2.1 %collective-permute-start.29 = (f32[128,512]{1,0:T(8,128)S(1)}, f32[128,512]{1,0:T(8,128)S(1)}, u32[]{:S(2)}, u32[]{:S(2)}) collective-permute-start(f32[128,512]{1,0:T(8,128)S(1)} %get-tuple-element.33.refs_0_), channel_id=1, source_target_pairs={{0,192},{64,0},{128,64},{192,128},{1,193},{65,1},{129,65},{193,129... | collective-permute-start | bytes 786440 | tf_op jit(solution)/shard_map/ppermute | solution.py:418
  120.8 4.2 %collective-permute-done.9.refs_3_ = f32[128,512]{1,0:T(8,128)S(1)} collective-permute-done((f32[128,512]{1,0:T(8,128)S(1)}, f32[128,512]{1,0:T(8,128)S(1)}, u32[]{:S(2)}, u32[]{:S(2)}) %collective-permute-start.9) | collective-permute-done | bytes 262176 | tf_op jit(solution)/shard_map/ppermute | solution.py:418
  125.0 6.7 %shard_map.164 = (bf16[1024,128]{1,0:T(8,128)(2,1)S(1)}, bf16[1024,128]{1,0:T(8,128)(2,1)S(1)}, bf16[1024,128]{1,0:T(8,128)(2,1)S(1)}, bf16[1024,128]{1,0:T(8,128)(2,1)S(1)}) custom-call(f32[128,512]{1,0:T(8,128)S(1)} %get-tuple-element.27.refs_0_, f32[128,512]{1,0:T(8,128)S(1)} %collective-permute-done.7.refs_1_, ...), custom_call_target="tpu_custom_call" | custom-call | flops 4294967296 | tf_op jit(solution)/shard_map/pallas_call | solution.py:382
  131.8 3.7 %collective-permute-done.31.refs_3_ = f32[128,512]{1,0:T(8,128)S(1)} collective-permute-done((f32[128,512]{1,0:T(8,128)S(1)}, f32[128,512]{1,0:T(8,128)S(1)}, u32[]{:S(2)}, u32[]{:S(2)}) %collective-permute-start.31) | collective-permute-done | bytes 262176 | tf_op jit(solution)/shard_map/ppermute | solution.py:418
  135.6 6.7 %shard_map.165 = (bf16[1024,128]{1,0:T(8,128)(2,1)S(1)}, bf16[1024,128]{1,0:T(8,128)(2,1)S(1)}, bf16[1024,128]{1,0:T(8,128)(2,1)S(1)}, bf16[1024,128]{1,0:T(8,128)(2,1)S(1)}) custom-call(f32[128,512]{1,0:T(8,128)S(1)} %get-tuple-element.33.refs_0_, f32[128,512]{1,0:T(8,128)S(1)} %collective-permute-done.29.refs_1_, ...), custom_call_target="tpu_custom_call" | custom-call | flops 4294967296 | tf_op jit(solution)/shard_map/pallas_call | solution.py:382
  143.2 1.9 %collective-permute-start.34 = (bf16[1024,128]{1,0:T(8,128)(2,1)S(1)}, bf16[1024,128]{1,0:T(8,128)(2,1)S(1)}, u32[]{:S(2)}, u32[]{:S(2)}) collective-permute-start(bf16[1024,128]{1,0:T(8,128)(2,1)S(1)} %get-tuple-element.44), channel_id=1, source_target_pairs={{0,192},{64,0},{128,64},{192,128},{1,193},{65,1},{129,65},{193,129... | collective-permute-start | bytes 786440 | tf_op jit(solution)/shard_map/ppermute | solution.py:418
  145.7 1.8 %collective-permute-start.27 = (bf16[1024,128]{1,0:T(8,128)(2,1)S(1)}, bf16[1024,128]{1,0:T(8,128)(2,1)S(1)}, u32[]{:S(2)}, u32[]{:S(2)}) collective-permute-start(bf16[1024,128]{1,0:T(8,128)(2,1)S(1)} %get-tuple-element.37), channel_id=1, source_target_pairs={{0,128},{64,192},{128,0},{192,64},{1,129},{65,193},{129,1},{193,65... | collective-permute-start | bytes 786440 | tf_op jit(solution)/shard_map/ppermute | solution.py:418
  147.4 8.2 %collective-permute-done.32.refs_5_ = bf16[1024,128]{1,0:T(8,128)(2,1)S(1)} collective-permute-done((bf16[1024,128]{1,0:T(8,128)(2,1)S(1)}, bf16[1024,128]{1,0:T(8,128)(2,1)S(1)}, u32[]{:S(2)}, u32[]{:S(2)}) %collective-permute-start.32) | collective-permute-done | bytes 262176 | tf_op jit(solution)/shard_map/ppermute | solution.py:418
  157.7 10.1 %collective-permute-done.26.refs_1_ = bf16[1024,128]{1,0:T(8,128)(2,1)S(1)} collective-permute-done((bf16[1024,128]{1,0:T(8,128)(2,1)S(1)}, bf16[1024,128]{1,0:T(8,128)(2,1)S(1)}, u32[]{:S(2)}, u32[]{:S(2)}) %collective-permute-start.26) | collective-permute-done | bytes 262176 | tf_op jit(solution)/shard_map/ppermute | solution.py:418
  (94 shorter events, 22.6 us)
Async XLA Ops:
  3.1 13.0 %all-to-all-start = ((bf16[8,128,128]{2,1,0:T(8,128)(2,1)}), bf16[8,128,128]{2,1,0:T(8,128)(2,1)S(1)}, u32[]{:S(2)}, u32[]{:S(2)}) async-start(bf16[8,128,128]{2,1,0:T(8,128)(2,1)} %shard_map.157), calls=%async_computation | async-start | bytes 524288 | tf_op jit(solution)/shard_map/all_to_all | solution.py:445
  17.9 34.9 %all-to-all-start.1 = ((bf16[8,224,128]{2,1,0:T(8,128)(2,1)}), bf16[8,224,128]{2,1,0:T(8,128)(2,1)S(1)}, u32[]{:S(2)}, u32[]{:S(2)}) async-start(bf16[8,224,128]{2,1,0:T(8,128)(2,1)} %shard_map.159), calls=%async_computation.1 | async-start | bytes 917504 | tf_op jit(solution)/shard_map/all_to_all | solution.py:445
  30.4 13.0 %collective-permute-start.12 = (bf16[144,256]{1,0:T(8,128)(2,1)S(1)}, bf16[144,256]{1,0:T(8,128)(2,1)S(1)}, u32[]{:S(2)}, u32[]{:S(2)}) collective-permute-start(bf16[144,256]{1,0:T(8,128)(2,1)S(1)} %shard_map.161.refs_0_), channel_id=1, source_target_pairs={{0,40},{8,48},{16,56},{24,0},{32,8},{40,16},{48,24},{56,32},{1,41}... | collective-permute-start | bytes 221192 | tf_op jit(solution)/shard_map/ppermute | solution.py:418
  31.6 13.8 %collective-permute-start.13 = (bf16[144,256]{1,0:T(8,128)(2,1)S(1)}, bf16[144,256]{1,0:T(8,128)(2,1)S(1)}, u32[]{:S(2)}, u32[]{:S(2)}) collective-permute-start(bf16[144,256]{1,0:T(8,128)(2,1)S(1)} %shard_map.161.refs_0_), channel_id=1, source_target_pairs={{0,32},{8,40},{16,48},{24,56},{32,0},{40,8},{48,16},{56,24},{1,33}... | collective-permute-start | bytes 221192 | tf_op jit(solution)/shard_map/ppermute | solution.py:418
  34.9 15.4 %collective-permute-start.14 = (bf16[144,256]{1,0:T(8,128)(2,1)S(1)}, bf16[144,256]{1,0:T(8,128)(2,1)S(1)}, u32[]{:S(2)}, u32[]{:S(2)}) collective-permute-start(bf16[144,256]{1,0:T(8,128)(2,1)S(1)} %shard_map.161.refs_0_), channel_id=1, source_target_pairs={{0,24},{8,32},{16,40},{24,48},{32,56},{40,0},{48,8},{56,16},{1,25}... | collective-permute-start | bytes 221192 | tf_op jit(solution)/shard_map/ppermute | solution.py:418
  36.9 13.4 %collective-permute-start.15 = (bf16[144,256]{1,0:T(8,128)(2,1)S(1)}, bf16[144,256]{1,0:T(8,128)(2,1)S(1)}, u32[]{:S(2)}, u32[]{:S(2)}) collective-permute-start(bf16[144,256]{1,0:T(8,128)(2,1)S(1)} %shard_map.161.refs_0_), channel_id=1, source_target_pairs={{0,16},{8,24},{16,32},{24,40},{32,48},{40,56},{48,0},{56,8},{1,17}... | collective-permute-start | bytes 221192 | tf_op jit(solution)/shard_map/ppermute | solution.py:418
  51.3 12.5 %collective-permute-start.17 = (bf16[8,144,256]{2,1,0:T(8,128)(2,1)S(1)}, bf16[8,144,256]{2,1,0:T(8,128)(2,1)S(1)}, u32[]{:S(2)}, u32[]{:S(2)}) collective-permute-start(bf16[8,144,256]{2,1,0:T(8,128)(2,1)S(1)} %shard_map.162.refs_5_), channel_id=1, source_target_pairs={{0,6},{2,0},{4,2},{6,4},{1,7},{3,1},{5,3},{7,5},{8,14},{10,8},{12,... | collective-permute-start | bytes 1769480 | tf_op jit(solution)/shard_map/ppermute | solution.py:418
  52.2 14.4 %collective-permute-start.18 = (bf16[8,144,256]{2,1,0:T(8,128)(2,1)S(1)}, bf16[8,144,256]{2,1,0:T(8,128)(2,1)S(1)}, u32[]{:S(2)}, u32[]{:S(2)}) collective-permute-start(bf16[8,144,256]{2,1,0:T(8,128)(2,1)S(1)} %shard_map.162.refs_5_), channel_id=1, source_target_pairs={{0,2},{2,4},{4,6},{6,0},{1,3},{3,5},{5,7},{7,1},{8,10},{10,12},{12... | collective-permute-start | bytes 1769480 | tf_op jit(solution)/shard_map/ppermute | solution.py:418
  52.8 20.6 %collective-permute-start = (bf16[8,160,128]{2,1,0:T(8,128)(2,1)S(1)}, bf16[8,160,128]{2,1,0:T(8,128)(2,1)S(1)}, u32[]{:S(2)}, u32[]{:S(2)}) collective-permute-start(bf16[8,160,128]{2,1,0:T(8,128)(2,1)S(1)} %slice.17.refs_0_), channel_id=1, source_target_pairs={{0,6},{2,0},{4,2},{6,4},{1,7},{3,1},{5,3},{7,5},{8,14},{10,8},{12,... | collective-permute-start | bytes 983048 | tf_op jit(solution)/shard_map/ppermute | solution.py:418
  63.8 13.4 %collective-permute-start.19 = (bf16[4,144,256]{2,1,0:T(8,128)(2,1)S(1)}, bf16[4,144,256]{2,1,0:T(8,128)(2,1)S(1)}, u32[]{:S(2)}, u32[]{:S(2)}) collective-permute-start(bf16[4,144,256]{2,1,0:T(8,128)(2,1)S(1)} %slice.18), channel_id=1, source_target_pairs={{0,6},{2,0},{4,2},{6,4},{1,7},{3,1},{5,3},{7,5},{8,14},{10,8},{12,... | collective-permute-start | bytes 884744 | tf_op jit(solution)/shard_map/ppermute | solution.py:418
  66.0 11.9 %collective-permute-start.1 = (bf16[8,160,128]{2,1,0:T(8,128)(2,1)S(1)}, bf16[8,160,128]{2,1,0:T(8,128)(2,1)}, u32[]{:S(2)}, u32[]{:S(2)}) collective-permute-start(bf16[8,160,128]{2,1,0:T(8,128)(2,1)S(1)} %slice.17.refs_0_), channel_id=1, source_target_pairs={{0,4},{2,6},{4,0},{6,2},{1,5},{3,7},{5,1},{7,3},{8,12},{10,14},{12... | collective-permute-start | bytes 983048 | tf_op jit(solution)/shard_map/ppermute | solution.py:418
  66.0 22.0 %collective-permute-start.2 = (bf16[8,160,128]{2,1,0:T(8,128)(2,1)S(1)}, bf16[8,160,128]{2,1,0:T(8,128)(2,1)}, u32[]{:S(2)}, u32[]{:S(2)}) collective-permute-start(bf16[8,160,128]{2,1,0:T(8,128)(2,1)S(1)} %slice.17.refs_0_), channel_id=1, source_target_pairs={{0,2},{2,4},{4,6},{6,0},{1,3},{3,5},{5,7},{7,1},{8,10},{10,12},{12... | collective-permute-start | bytes 983048 | tf_op jit(solution)/shard_map/ppermute | solution.py:418
  66.7 25.6 %collective-permute-start.3 = (bf16[8,160,128]{2,1,0:T(8,128)(2,1)S(1)}, bf16[8,160,128]{2,1,0:T(8,128)(2,1)S(1)}, u32[]{:S(2)}, u32[]{:S(2)}) collective-permute-start(bf16[8,160,128]{2,1,0:T(8,128)(2,1)S(1)} %slice.17.refs_0_), channel_id=1, source_target_pairs={{0,1},{1,0},{2,3},{3,2},{4,5},{5,4},{6,7},{7,6},{8,9},{9,8},{10,11... | collective-permute-start | bytes 983048 | tf_op jit(solution)/shard_map/ppermute | solution.py:418
  73.4 19.6 %collective-permute-start.4 = (bf16[8,160,128]{2,1,0:T(8,128)(2,1)S(1)}, bf16[8,160,128]{2,1,0:T(8,128)(2,1)S(1)}, u32[]{:S(2)}, u32[]{:S(2)}) collective-permute-start(bf16[8,160,128]{2,1,0:T(8,128)(2,1)S(1)} %collective-permute-done.refs_1_), channel_id=1, source_target_pairs={{0,1},{1,0},{2,3},{3,2},{4,5},{5,4},{6,7},{7,6},{8,9},{9,8},{10,11... | collective-permute-start | bytes 983048 | tf_op jit(solution)/shard_map/ppermute | solution.py:418
  77.9 17.3 %collective-permute-start.5 = (bf16[8,160,128]{2,1,0:T(8,128)(2,1)}, bf16[8,160,128]{2,1,0:T(8,128)(2,1)}, u32[]{:S(2)}, u32[]{:S(2)}) collective-permute-start(bf16[8,160,128]{2,1,0:T(8,128)(2,1)} %collective-permute-done.1.refs_2_), channel_id=1, source_target_pairs={{0,1},{1,0},{2,3},{3,2},{4,5},{5,4},{6,7},{7,6},{8,9},{9,8},{10,11... | collective-permute-start | bytes 983048 | tf_op jit(solution)/shard_map/ppermute | solution.py:418
  88.1 18.3 %collective-permute-start.21 = (bf16[8,144,256]{2,1,0:T(8,128)(2,1)S(1)}, bf16[8,144,256]{2,1,0:T(8,128)(2,1)S(1)}, u32[]{:S(2)}, u32[]{:S(2)}) collective-permute-start(bf16[8,144,256]{2,1,0:T(8,128)(2,1)S(1)} %shard_map.162.refs_5_), channel_id=1, source_target_pairs={{0,1},{1,0},{2,3},{3,2},{4,5},{5,4},{6,7},{7,6},{8,9},{9,8},{10,11... | collective-permute-start | bytes 1769480 | tf_op jit(solution)/shard_map/ppermute | solution.py:418
  93.0 16.1 %collective-permute-start.22 = (bf16[8,144,256]{2,1,0:T(8,128)(2,1)S(1)}, bf16[8,144,256]{2,1,0:T(8,128)(2,1)S(1)}, u32[]{:S(2)}, u32[]{:S(2)}) collective-permute-start(bf16[8,144,256]{2,1,0:T(8,128)(2,1)S(1)} %collective-permute-done.17.refs_6_), channel_id=1, source_target_pairs={{0,1},{1,0},{2,3},{3,2},{4,5},{5,4},{6,7},{7,6},{8,9},{9,8},{10,11... | collective-permute-start | bytes 1769480 | tf_op jit(solution)/shard_map/ppermute | solution.py:418
  93.8 15.8 %collective-permute-start.23 = (bf16[8,144,256]{2,1,0:T(8,128)(2,1)S(1)}, bf16[8,144,256]{2,1,0:T(8,128)(2,1)}, u32[]{:S(2)}, u32[]{:S(2)}) collective-permute-start(bf16[8,144,256]{2,1,0:T(8,128)(2,1)S(1)} %collective-permute-done.18.refs_7_), channel_id=1, source_target_pairs={{0,1},{1,0},{2,3},{3,2},{4,5},{5,4},{6,7},{7,6},{8,9},{9,8},{10,11... | collective-permute-start | bytes 1769480 | tf_op jit(solution)/shard_map/ppermute | solution.py:418
  95.2 22.2 %collective-permute-start.24 = (bf16[4,144,256]{2,1,0:T(8,128)(2,1)}, bf16[4,144,256]{2,1,0:T(8,128)(2,1)S(1)}, u32[]{:S(2)}, u32[]{:S(2)}) collective-permute-start(bf16[4,144,256]{2,1,0:T(8,128)(2,1)} %copy-done.14), channel_id=1, source_target_pairs={{0,1},{1,0},{2,3},{3,2},{4,5},{5,4},{6,7},{7,6},{8,9},{9,8},{10,11... | collective-permute-start | bytes 884744 | tf_op jit(solution)/shard_map/ppermute | solution.py:418
  95.3 24.3 %collective-permute-start.25 = (bf16[4,144,256]{2,1,0:T(8,128)(2,1)}, bf16[4,144,256]{2,1,0:T(8,128)(2,1)S(1)}, u32[]{:S(2)}, u32[]{:S(2)}) collective-permute-start(bf16[4,144,256]{2,1,0:T(8,128)(2,1)} %collective-permute-done.20.refs_9_), channel_id=1, source_target_pairs={{0,1},{1,0},{2,3},{3,2},{4,5},{5,4},{6,7},{7,6},{8,9},{9,8},{10,11... | collective-permute-start | bytes 884744 | tf_op jit(solution)/shard_map/ppermute | solution.py:418
  106.5 14.4 %collective-permute-start.7 = (f32[128,512]{1,0:T(8,128)S(1)}, f32[128,512]{1,0:T(8,128)S(1)}, u32[]{:S(2)}, u32[]{:S(2)}) collective-permute-start(f32[128,512]{1,0:T(8,128)S(1)} %get-tuple-element.27.refs_0_), channel_id=1, source_target_pairs={{0,192},{64,0},{128,64},{192,128},{1,193},{65,1},{129,65},{193,129... | collective-permute-start | bytes 786440 | tf_op jit(solution)/shard_map/ppermute | solution.py:418
  109.1 11.8 %collective-permute-start.8 = (f32[128,512]{1,0:T(8,128)S(1)}, f32[128,512]{1,0:T(8,128)S(1)}, u32[]{:S(2)}, u32[]{:S(2)}) collective-permute-start(f32[128,512]{1,0:T(8,128)S(1)} %get-tuple-element.27.refs_0_), channel_id=1, source_target_pairs={{0,128},{64,192},{128,0},{192,64},{1,129},{65,193},{129,1},{193,65... | collective-permute-start | bytes 786440 | tf_op jit(solution)/shard_map/ppermute | solution.py:418
  109.6 15.5 %collective-permute-start.9 = (f32[128,512]{1,0:T(8,128)S(1)}, f32[128,512]{1,0:T(8,128)S(1)}, u32[]{:S(2)}, u32[]{:S(2)}) collective-permute-start(f32[128,512]{1,0:T(8,128)S(1)} %get-tuple-element.27.refs_0_), channel_id=1, source_target_pairs={{0,64},{64,128},{128,192},{192,0},{1,65},{65,129},{129,193},{193,1... | collective-permute-start | bytes 786440 | tf_op jit(solution)/shard_map/ppermute | solution.py:418
  117.4 14.4 %collective-permute-start.29 = (f32[128,512]{1,0:T(8,128)S(1)}, f32[128,512]{1,0:T(8,128)S(1)}, u32[]{:S(2)}, u32[]{:S(2)}) collective-permute-start(f32[128,512]{1,0:T(8,128)S(1)} %get-tuple-element.33.refs_0_), channel_id=1, source_target_pairs={{0,192},{64,0},{128,64},{192,128},{1,193},{65,1},{129,65},{193,129... | collective-permute-start | bytes 786440 | tf_op jit(solution)/shard_map/ppermute | solution.py:418
  119.6 12.3 %collective-permute-start.30 = (f32[128,512]{1,0:T(8,128)S(1)}, f32[128,512]{1,0:T(8,128)S(1)}, u32[]{:S(2)}, u32[]{:S(2)}) collective-permute-start(f32[128,512]{1,0:T(8,128)S(1)} %get-tuple-element.33.refs_0_), channel_id=1, source_target_pairs={{0,128},{64,192},{128,0},{192,64},{1,129},{65,193},{129,1},{193,65... | collective-permute-start | bytes 786440 | tf_op jit(solution)/shard_map/ppermute | solution.py:418
  120.8 14.8 %collective-permute-start.31 = (f32[128,512]{1,0:T(8,128)S(1)}, f32[128,512]{1,0:T(8,128)S(1)}, u32[]{:S(2)}, u32[]{:S(2)}) collective-permute-start(f32[128,512]{1,0:T(8,128)S(1)} %get-tuple-element.33.refs_0_), channel_id=1, source_target_pairs={{0,64},{64,128},{128,192},{192,0},{1,65},{65,129},{129,193},{193,1... | collective-permute-start | bytes 786440 | tf_op jit(solution)/shard_map/ppermute | solution.py:418
  142.3 13.3 %collective-permute-start.32 = (bf16[1024,128]{1,0:T(8,128)(2,1)S(1)}, bf16[1024,128]{1,0:T(8,128)(2,1)S(1)}, u32[]{:S(2)}, u32[]{:S(2)}) collective-permute-start(bf16[1024,128]{1,0:T(8,128)(2,1)S(1)} %get-tuple-element.42), channel_id=1, source_target_pairs={{0,64},{64,128},{128,192},{192,0},{1,65},{65,129},{129,193},{193,1... | collective-permute-start | bytes 786440 | tf_op jit(solution)/shard_map/ppermute | solution.py:418
  142.4 15.3 %collective-permute-start.33 = (bf16[1024,128]{1,0:T(8,128)(2,1)S(1)}, bf16[1024,128]{1,0:T(8,128)(2,1)S(1)}, u32[]{:S(2)}, u32[]{:S(2)}) collective-permute-start(bf16[1024,128]{1,0:T(8,128)(2,1)S(1)} %get-tuple-element.43), channel_id=1, source_target_pairs={{0,128},{64,192},{128,0},{192,64},{1,129},{65,193},{129,1},{193,65... | collective-permute-start | bytes 786440 | tf_op jit(solution)/shard_map/ppermute | solution.py:418
  143.2 14.5 %collective-permute-start.34 = (bf16[1024,128]{1,0:T(8,128)(2,1)S(1)}, bf16[1024,128]{1,0:T(8,128)(2,1)S(1)}, u32[]{:S(2)}, u32[]{:S(2)}) collective-permute-start(bf16[1024,128]{1,0:T(8,128)(2,1)S(1)} %get-tuple-element.44), channel_id=1, source_target_pairs={{0,192},{64,0},{128,64},{192,128},{1,193},{65,1},{129,65},{193,129... | collective-permute-start | bytes 786440 | tf_op jit(solution)/shard_map/ppermute | solution.py:418
  145.1 22.7 %collective-permute-start.26 = (bf16[1024,128]{1,0:T(8,128)(2,1)S(1)}, bf16[1024,128]{1,0:T(8,128)(2,1)S(1)}, u32[]{:S(2)}, u32[]{:S(2)}) collective-permute-start(bf16[1024,128]{1,0:T(8,128)(2,1)S(1)} %get-tuple-element.36), channel_id=1, source_target_pairs={{0,64},{64,128},{128,192},{192,0},{1,65},{65,129},{129,193},{193,1... | collective-permute-start | bytes 786440 | tf_op jit(solution)/shard_map/ppermute | solution.py:418
  145.7 22.1 %collective-permute-start.27 = (bf16[1024,128]{1,0:T(8,128)(2,1)S(1)}, bf16[1024,128]{1,0:T(8,128)(2,1)S(1)}, u32[]{:S(2)}, u32[]{:S(2)}) collective-permute-start(bf16[1024,128]{1,0:T(8,128)(2,1)S(1)} %get-tuple-element.37), channel_id=1, source_target_pairs={{0,128},{64,192},{128,0},{192,64},{1,129},{65,193},{129,1},{193,65... | collective-permute-start | bytes 786440 | tf_op jit(solution)/shard_map/ppermute | solution.py:418
  155.6 12.6 %collective-permute-start.28 = (bf16[1024,128]{1,0:T(8,128)(2,1)S(1)}, bf16[1024,128]{1,0:T(8,128)(2,1)S(1)}, u32[]{:S(2)}, u32[]{:S(2)}) collective-permute-start(bf16[1024,128]{1,0:T(8,128)(2,1)S(1)} %get-tuple-element.38), channel_id=1, source_target_pairs={{0,192},{64,0},{128,64},{192,128},{1,193},{65,1},{129,65},{193,129... | collective-permute-start | bytes 786440 | tf_op jit(solution)/shard_map/ppermute | solution.py:418
  (23 other events, 438.5 us)
